TPU v7x, 32 devices: a whole 2x2x4 slice. The times are simulated.
32 devices in a mesh: dp: 16 (over z, y, core), seq: 2 (over x).
Axes of the slice: x: 2, y: 2, z: 4, core: 2. Of those that a mesh axis runs over, the one named last changes fastest.
Arguments:
- tokens: bfloat16 [4096, 2304], P(('dp', 'seq')), may hold values from -6 to 6
- doc_lengths: int32 [16, 3], P('dp'), may hold values from 1 to 170, 256 in all within a row
- attn_weight: bfloat16 [2304, 6144], P(('dp', 'seq')), may hold values from -0.125 to 0.125
- ffn_weight: bfloat16 [9216, 6912], P(('dp', 'seq')), may hold values from -0.125 to 0.125
- gains: bfloat16 [2304, 4], P(('dp', 'seq')), may hold values from 0.099609375 to 1.8984375
- out_grad: bfloat16 [4096, 2304], P(('dp', 'seq')), may hold values from -6 to 6
Outputs:
- block_out: bfloat16 [4096, 2304], P(('dp', 'seq'))
- tokens_grad: float32 [4096, 2304], P(('dp', 'seq'))
- attn_weight_grad: float32 [2304, 6144], P(('dp', 'seq'))
- ffn_weight_grad: float32 [9216, 6912], P(('dp', 'seq'))
- gains_grad: float32 [2304, 4], P(('dp', 'seq'))
Inputs may be any that keep to these rules, and one draw needn't show every extreme that they name: `doc_lengths`: row b lists in order the lengths of the 3 documents of pack b; they add up to 256, and one of them is 170.
All inputs are finite; a program needn't handle non-finite values.
Results may differ from a plain program's by a relative error of at most 0.014.
Values may be sent and summed in bfloat16 or wider, within the bound.
A program may use at most 448 MiB of HBM per device.

v0:
```python
import math

import jax
import jax.numpy as jnp
from jax import lax
from jax.sharding import PartitionSpec as P

D = 2304
HEADS = 8
KV_HEADS = 4
HEAD_DIM = 256
WINDOW = 128


soft_cap = 50.0
eps_norm = 1e-06
rope_base = 10000.0
gelu_coef = math.sqrt(2.0 / math.pi)


def passed_along(x, axis, by):
    devices = lax.axis_size(axis)
    pairs = [(i, i + by) for i in range(devices) if 0 <= i + by < devices]
    return lax.ppermute(x, axis, pairs)


def gelu_tanh(value):
    return 0.5 * value * (1.0 + jnp.tanh(gelu_coef * (value + 0.044715 * value * value * value)))


def gated_gelu(gate_pre, up_pre):
    return gelu_tanh(gate_pre) * up_pre


def gate_grads(gate_rows, d_hidden):
    d_gate, d_up = jax.vjp(gated_gelu, gate_rows[:, 0], gate_rows[:, 1])[1](d_hidden)
    return jnp.stack([d_gate, d_up], axis=1).astype(jnp.bfloat16)


def rms_norm(value, gain_vec):
    return value * lax.rsqrt(jnp.mean(value * value, axis=-1, keepdims=True) + eps_norm) * gain_vec


def norm_back(value, gain_vec, incoming):
    return jax.vjp(rms_norm, value, gain_vec)[1](incoming)


def doc_layout(lengths, places):
    doc_ends = jnp.cumsum(lengths, dtype=jnp.int32)
    starts = doc_ends - lengths
    doc_ids = jnp.sum(
        (places[:, None] >= doc_ends[None, :]).astype(jnp.int32), axis=1, dtype=jnp.int32
    )
    onehot = doc_ids[:, None] == jnp.arange(lengths.shape[0], dtype=jnp.int32)[None, :]
    doc_first = jnp.sum(jnp.where(onehot, starts[None, :], 0), axis=1, dtype=jnp.int32)
    return (doc_ids, places - doc_first)


def rotate(value, doc_pos):
    half_dim = value.shape[-1] // 2
    frequency = rope_base ** (-2.0 * jnp.arange(half_dim, dtype=jnp.float32) / value.shape[-1])
    angles = doc_pos.astype(jnp.float32)[:, None] * frequency[None, :]
    cosine = jnp.cos(angles)[:, None, :]
    sine_part = jnp.sin(angles)[:, None, :]
    first_half = value[..., :half_dim]
    second_half = value[..., half_dim:]
    return jnp.concatenate(
        [
            first_half * cosine - second_half * sine_part,
            second_half * cosine + first_half * sine_part,
        ],
        axis=-1,
    )


def contract_rows(left_side, right_side):
    return lax.dot_general(
        left_side, right_side, (((0,), (0,)), ((), ())), preferred_element_type=jnp.float32
    )


def contract_cols(left_side, right_side):
    return lax.dot_general(
        left_side, right_side, (((1,), (1,)), ((), ())), preferred_element_type=jnp.float32
    )


def key_mask(query_places, query_docs, key_places, key_docs):
    return (
        (key_places[None, :] >= 0)
        & (query_docs[:, None] == key_docs[None, :])
        & (key_places[None, :] <= query_places[:, None])
        & (query_places[:, None] - key_places[None, :] < WINDOW)
    )


def attn_scores(queries, all_keys, allowed):
    scores = jnp.einsum("qkgd,pkd->kgqp", queries, all_keys, preferred_element_type=jnp.float32)
    capped = jnp.where(allowed[None, None], soft_cap * jnp.tanh(scores / soft_cap), -1e30)
    return (scores, capped)


def on_device(tokens, doc_lengths, attn_weight, ffn_weight, gains, out_grad):
    tok_rows = tokens.shape[0]
    q_cols = HEADS * HEAD_DIM
    k_cols = KV_HEADS * HEAD_DIM
    proj_cols = q_cols + 2 * k_cols
    group_size = HEADS // KV_HEADS
    query_scale = HEAD_DIM ** (-0.5)
    seq_index = lax.axis_index("seq")
    own_places = seq_index * tok_rows + jnp.arange(tok_rows, dtype=jnp.int32)
    halo_places = own_places - tok_rows
    own_docs, own_pos = doc_layout(doc_lengths[0], own_places)
    halo_docs = doc_layout(doc_lengths[0], halo_places)[0]
    all_places = jnp.concatenate([halo_places, own_places])
    all_docs = jnp.concatenate([halo_docs, own_docs])
    allowed = key_mask(own_places, own_docs, all_places, all_docs)
    attn_full, gain_full = (
        lax.all_gather(attn_weight, ("dp", "seq"), axis=0, tiled=True),
        lax.all_gather(gains, ("dp", "seq"), axis=0, tiled=True),
    )
    gain_vals = gain_full.astype(jnp.float32)
    tokens_f = tokens.astype(jnp.float32)
    attn_in = rms_norm(tokens_f, gain_vals[:, 0]).astype(jnp.bfloat16)
    projected = jnp.dot(attn_in, attn_full[:, :proj_cols], preferred_element_type=jnp.float32)
    queries = (
        rotate(projected[:, :q_cols].reshape(tok_rows, HEADS, HEAD_DIM), own_pos) * query_scale
    ).astype(jnp.bfloat16)
    queries = queries.reshape(tok_rows, KV_HEADS, group_size, HEAD_DIM)
    own_keys = rotate(
        projected[:, q_cols : q_cols + k_cols].reshape(tok_rows, KV_HEADS, HEAD_DIM), own_pos
    ).astype(jnp.bfloat16)
    own_values = (
        projected[:, q_cols + k_cols :].reshape(tok_rows, KV_HEADS, HEAD_DIM).astype(jnp.bfloat16)
    )
    halo_keys, halo_values = passed_along((own_keys, own_values), "seq", 1)
    all_keys = jnp.concatenate([halo_keys, own_keys])
    all_values = jnp.concatenate([halo_values, own_values])
    scores, capped = attn_scores(queries, all_keys, allowed)
    row_max = jnp.max(capped, axis=-1, keepdims=True)
    exp_terms = jnp.exp(capped - row_max)
    row_total = jnp.sum(exp_terms, axis=-1, keepdims=True)
    log_total = row_max + jnp.log(row_total)
    attn_probs = (exp_terms / row_total).astype(jnp.bfloat16)
    mixed_heads = jnp.einsum(
        "kgqp,pkd->qkgd", attn_probs, all_values, preferred_element_type=jnp.float32
    )
    mixed_heads = mixed_heads.reshape(tok_rows, q_cols).astype(jnp.bfloat16)
    attn_out = contract_cols(mixed_heads, attn_full[:, proj_cols:])
    middle = tokens_f + rms_norm(attn_out, gain_vals[:, 1])
    ffn_input = rms_norm(middle, gain_vals[:, 2]).astype(jnp.bfloat16)
    unit_weights = lax.all_gather(ffn_weight, "seq", axis=0, tiled=True)
    unit_count = unit_weights.shape[0]
    in_weights = unit_weights[:, : 2 * D].reshape(unit_count, 2, D)
    ffn_all = lax.all_gather(ffn_input, "dp", axis=0, tiled=True)
    gate_up = jnp.einsum("td,cjd->tjc", ffn_all, in_weights, preferred_element_type=jnp.float32)
    hidden = gated_gelu(gate_up[:, 0], gate_up[:, 1]).astype(jnp.bfloat16)
    ffn_out = lax.psum_scatter(
        jnp.dot(hidden, unit_weights[:, 2 * D :], preferred_element_type=jnp.float32),
        "dp",
        scatter_dimension=0,
        tiled=True,
    )
    out_gain = gain_vals[:, 3]
    block_out = (middle + rms_norm(ffn_out, out_gain)).astype(jnp.bfloat16)
    cotangent = out_grad.astype(jnp.float32)
    d_ffn_f, d_gain_out = norm_back(ffn_out, out_gain, cotangent)
    d_ffn = d_ffn_f.astype(jnp.bfloat16)
    shard_piece = lax.all_gather(d_ffn, "dp", axis=0, tiled=True)
    d_hidden = contract_cols(shard_piece, unit_weights[:, 2 * D :])
    d_gate_up = gate_grads(gate_up, d_hidden)
    in_grad = jnp.einsum(
        "tjc,td->cjd", d_gate_up, ffn_all, preferred_element_type=jnp.float32
    ).reshape(unit_count, 2 * D)
    out_rows_grad = contract_rows(hidden, shard_piece)
    weight_sum = jnp.concatenate([in_grad, out_rows_grad], axis=1)
    d_ffn_input = lax.psum_scatter(
        jnp.einsum("tjc,cjd->td", d_gate_up, in_weights, preferred_element_type=jnp.float32),
        "dp",
        scatter_dimension=0,
        tiled=True,
    )
    ffn_weight_grad = lax.psum_scatter(
        weight_sum.astype(jnp.bfloat16), "seq", scatter_dimension=0, tiled=True
    ).astype(jnp.float32)
    d_middle_add, d_gain_ffn = norm_back(middle, gain_vals[:, 2], d_ffn_input)
    d_middle = cotangent + d_middle_add
    d_attn_f, d_gain_post = norm_back(attn_out, gain_vals[:, 1], d_middle)
    d_attn = d_attn_f.astype(jnp.bfloat16)
    attn_back = lax.all_gather(attn_weight, ("dp", "seq"), axis=0, tiled=True)
    out_cols_grad = contract_rows(d_attn, mixed_heads)
    d_mixed = jnp.dot(d_attn, attn_back[:, proj_cols:], preferred_element_type=jnp.float32).astype(
        jnp.bfloat16
    )
    d_mixed = d_mixed.reshape(tok_rows, KV_HEADS, group_size, HEAD_DIM)
    scores, capped = attn_scores(queries, all_keys, allowed)
    attn_p = jnp.exp(capped - log_total)
    d_probs = jnp.einsum("qkgd,pkd->kgqp", d_mixed, all_values, preferred_element_type=jnp.float32)
    d_values = jnp.einsum(
        "kgqp,qkgd->pkd", attn_p.astype(jnp.bfloat16), d_mixed, preferred_element_type=jnp.float32
    )
    d_capped = attn_p * (d_probs - jnp.sum(attn_p * d_probs, axis=-1, keepdims=True))
    tanh_part = jnp.tanh(scores / soft_cap)
    d_scores = (d_capped * (1.0 - tanh_part * tanh_part)).astype(jnp.bfloat16)
    d_queries = jnp.einsum("kgqp,pkd->qkgd", d_scores, all_keys, preferred_element_type=jnp.float32)
    d_keys = jnp.einsum("kgqp,qkgd->pkd", d_scores, queries, preferred_element_type=jnp.float32)
    back_keys, back_values = (
        passed_along(d_keys[:tok_rows].astype(jnp.bfloat16), "seq", -1).astype(jnp.float32),
        passed_along(d_values[:tok_rows].astype(jnp.bfloat16), "seq", -1).astype(jnp.float32),
    )
    d_own_keys = d_keys[tok_rows:] + back_keys
    d_own_values = d_values[tok_rows:] + back_values
    d_query_raw = rotate(d_queries.reshape(tok_rows, HEADS, HEAD_DIM) * query_scale, -own_pos)
    d_key_raw = rotate(d_own_keys, -own_pos)
    d_projected = jnp.concatenate(
        [
            d_query_raw.reshape(tok_rows, q_cols),
            d_key_raw.reshape(tok_rows, k_cols),
            d_own_values.reshape(tok_rows, k_cols),
        ],
        axis=1,
    ).astype(jnp.bfloat16)
    proj_grad = contract_rows(attn_in, d_projected)
    d_attn_in = contract_cols(d_projected, attn_back[:, :proj_cols])
    d_tokens_add, d_gain_in = norm_back(tokens_f, gain_vals[:, 0], d_attn_in)
    tokens_grad = d_middle + d_tokens_add
    attn_part = jnp.concatenate([proj_grad, out_cols_grad], axis=1)
    gain_part = jnp.stack([d_gain_in, d_gain_post, d_gain_ffn, d_gain_out], axis=1)
    attn_weight_grad, gains_grad = (
        lax.psum_scatter(attn_part, ("dp", "seq"), scatter_dimension=0, tiled=True),
        lax.psum_scatter(gain_part, ("dp", "seq"), scatter_dimension=0, tiled=True),
    )
    return (block_out, tokens_grad, attn_weight_grad, ffn_weight_grad, gains_grad)


def solution(mesh):
    return jax.shard_map(
        on_device,
        mesh=mesh,
        in_specs=(
            P(("dp", "seq"), None),
            P("dp", None),
            P(("dp", "seq"), None),
            P(("dp", "seq"), None),
            P(("dp", "seq"), None),
            P(("dp", "seq"), None),
        ),
        out_specs=(
            P(("dp", "seq"), None),
            P(("dp", "seq"), None),
            P(("dp", "seq"), None),
            P(("dp", "seq"), None),
            P(("dp", "seq"), None),
        ),
        check_vma=False,
    )
```

profile of v0, /device:TPU:0, one launch (start us, length us, event | category | flops | bytes accessed | tf_op | source)
XLA Modules:
  0.0 1508.4 jit_solution(18155339416416400928)
XLA Ops:
  8.7 72.1 %all-gather = bf16[32,72,4]{1,2,0:T(4,128)(2,1)S(1)} all-gather(bf16[1,72,4]{1,2,0:T(4,128)(2,1)S(1)} %bitcast.189), channel_id=1, replica_groups=mesh['dp'=16,'seq'=2] {'dp','seq'}, dimensions={0}, use_global_device_ids=true | all-gather | bytes 19008 | tf_op jit(solution)/shard_map/all_gather | solution.py:120
  84.7 98.3 %all-gather.6.cloned.1.call-done = bf16[2304,6144]{1,0:T(8,128)(2,1)} async-done(((bf16[72,6144]{1,0:T(8,128)(2,1)}), bf16[2304,6144]{1,0:T(8,128)(2,1)}) %all-gather.6.cloned.1.call-update) | async-done | bytes 28311568 | tf_op jit(solution)/shard_map/all_gather | solution.py:119
  183.1 8.3 fusion.3
  199.0 20.2 %collective-permute-done.1 = bf16[128,4,256]{2,0,1:T(8,128)(2,1)S(1)} collective-permute-done((bf16[128,4,256]{2,0,1:T(8,128)(2,1)S(1)}, bf16[128,4,256]{2,0,1:T(8,128)(2,1)S(1)}, u32[]{:S(2)}, u32[]{:S(2)}) %collective-permute-start.1) | collective-permute-done | bytes 262176 | tf_op jit(solution)/shard_map/ppermute | solution.py:24
  221.5 6.0 multiply_reduce_fusion.6
  229.8 61.2 %all-gather.10.cloned.1.call-done = bf16[576,6912]{1,0:T(8,128)(2,1)} async-done(((bf16[288,6912]{1,0:T(8,128)(2,1)}), bf16[576,6912]{1,0:T(8,128)(2,1)}) %all-gather.10.cloned.1.call-update) | async-done | bytes 7962640 | tf_op jit(solution)/shard_map/all_gather | solution.py:152
  296.2 79.6 %all-gather.8.cloned.1.call-done = bf16[2048,2304]{1,0:T(8,128)(2,1)} async-done(((bf16[128,2304]{1,0:T(8,128)(2,1)}), bf16[2048,2304]{1,0:T(8,128)(2,1)}) %all-gather.8.cloned.1.call-update) | async-done | bytes 9437200 | tf_op jit(solution)/shard_map/all_gather | solution.py:155
  375.7 15.4 %fusion.29 = f32[2048,2,576]{0,2,1:T(8,128)S(1)} fusion(bf16[72,2,8,2304]{3,2,1,0:T(8,128)(2,1)} %bitcast.165, bf16[2048,2304]{1,0:T(8,128)(2,1)} %all-gather.8.cloned.1.call-done), kind=kOutput, calls=%fused_computation.38 | convolution fusion | flops 10871635968 | bytes 24182784 | tf_op jit(solution)/shard_map/td,cjd->tjc/dot_general | solution.py:156
  396.2 13.2 fusion.41
  409.5 192.6 %reduce-scatter.8.cloned.1.call-done = f32[128,2304]{1,0:T(8,128)} async-done(((f32[2048,2304]{1,0:T(8,128)}), f32[128,2304]{1,0:T(8,128)}) %reduce-scatter.8.cloned.1.call-update) | async-done | bytes 1179664 | tf_op jit(solution)/shard_map/reduce_scatter | solution.py:158
  608.1 79.9 %all-gather.12.cloned.1.call-done = bf16[2048,2304]{1,0:T(8,128)(2,1)} async-done(((bf16[128,2304]{1,0:T(8,128)(2,1)}), bf16[2048,2304]{1,0:T(8,128)(2,1)}) %all-gather.12.cloned.1.call-update) | async-done | bytes 9437200 | tf_op jit(solution)/shard_map/all_gather | solution.py:169
  688.0 14.8 fusion.38
  704.9 17.4 %convolution_bitcast_fusion = f32[2048,2304]{1,0:T(8,128)} fusion(bf16[72,2,8,2304]{3,2,1,0:T(8,128)(2,1)} %bitcast.166, bf16[2048,1,576]{0,2,1:T(8,128)(2,1)S(1)} %get-tuple-element.23, bf16[2048,1,576]{0,2,1:T(8,128)(2,1)S(1)} %get-tuple-element.22), kind=kOutput, calls=%fused_computation.6 | convolution fusion | flops 10873995264 | bytes 28901376 | tf_op jit(solution)/shard_map/tjc,cjd->td/dot_general | solution.py:178
  722.6 14.9 fusion.18
  740.9 12.4 convolution_convert_fusion
  753.3 7.3 pad_maximum_fusion.1
  762.9 152.0 %reduce-scatter.10.cloned.1.call-done = f32[128,2304]{1,0:T(8,128)} async-done(((f32[2048,2304]{1,0:T(8,128)}), f32[128,2304]{1,0:T(8,128)}) %reduce-scatter.10.cloned.1.call-update) | async-done | bytes 1179664 | tf_op jit(solution)/shard_map/reduce_scatter | solution.py:177
  943.6 7.9 fusion.141
  955.3 9.7 collective-permute-done.3
  966.7 16.1 %fusion.99 = f32[2304,4096]{1,0:T(8,128)} fusion(bf16[128,1024]{0,1:T(8,128)(2,1)S(1)} %bitcast.175, bf16[128,1024]{0,1:T(8,128)(2,1)S(1)} %bitcast.173, bf16[128,2048]{0,1:T(8,128)(2,1)S(1)} %bitcast.171, bf16[128,2304]{1,0:T(8,128)(2,1)S(1)} %copy-done.2, f32[2304]{0:T(1024)S(1)} %copy-done.36, f32[128]{0:T(128)S(1)} %copy-done.43), kind=kOutput, calls=%fused_computation.136 | convolution fusion | flops 2420244480 | bytes 39396864 | tf_op jit(solution)/shard_map/dot_general | solution.py:77
  982.8 38.6 %pad_maximum_fusion = f32[2304,6144]{1,0:T(8,128)} fusion(f32[2304,2048]{1,0:T(8,128)} %fusion.141, f32[2304,4096]{1,0:T(8,128)} %fusion.99), kind=kLoop, calls=%fused_computation.1 | loop fusion | flops 14155776 | bytes 113246208 | tf_op jit(solution)/shard_map/concatenate | solution.py:227
  1028.9 14.7 fusion.53
  1043.6 39.6 %all-reduce.1 = f32[2304,4]{0,1:T(4,128)S(1)} all-reduce(f32[2304,4]{0,1:T(4,128)S(1)} %pad_maximum_fusion.11), channel_id=6, replica_groups=mesh['dp'=16,'seq'=2] {'dp','seq'}, use_global_device_ids=true, to_apply=%region_23.24.clone | all-reduce | flops 9216 | bytes 73728
  1086.9 414.2 %reduce-scatter.14.cloned.1.call-done = f32[72,6144]{1,0:T(8,128)} async-done(((f32[2304,6144]{1,0:T(8,128)}), f32[72,6144]{1,0:T(8,128)}) %reduce-scatter.14.cloned.1.call-update) | async-done | bytes 1769488
  (210 shorter events, 86.5 us)
Async XLA Ops:
  7.2 73.8 %copy-start.51 = (s32[1,3]{1,0:T(1,128)S(1)}, s32[1,3]{1,0:T(1,128)}, u32[]{:S(2)}) copy-start(s32[1,3]{1,0:T(1,128)} %param.7) | copy-start | bytes 40
  7.2 175.9 %all-gather.6.cloned.1.call-start = ((), (), s32[]{:S(2)}) async-start(), calls=%async_computation.4 | async-start | bytes 29196288 | tf_op jit(solution)/shard_map/all_gather | solution.py:119
  7.9 74.2 %copy-start.1 = (bf16[128,2304]{1,0:T(8,128)(2,1)S(1)}, bf16[128,2304]{1,0:T(8,128)(2,1)}, u32[]{:S(2)}) copy-start(bf16[128,2304]{1,0:T(8,128)(2,1)} %param.6) | copy-start | bytes 1769476
  7.9 283.0 %all-gather.10.cloned.1.call-start = ((), (), s32[]{:S(2)}) async-start(), calls=%async_computation.6 | async-start | bytes 11943936 | tf_op jit(solution)/shard_map/all_gather | solution.py:152
  8.7 367.1 %all-gather.8.cloned.1.call-start = ((), (), s32[]{:S(2)}) async-start(), calls=%async_computation.5 | async-start | bytes 10027008 | tf_op jit(solution)/shard_map/all_gather | solution.py:155
  82.1 109.3 %copy-start.35 = (f32[2304]{0:T(1024)}, f32[2304]{0:T(1024)S(1)}, u32[]{:S(2)}) copy-start(f32[2304]{0:T(1024)S(1)} %get-tuple-element.16) | copy-start | bytes 27652
  82.8 108.6 %copy-start.42 = (f32[128]{0:T(128)}, f32[128]{0:T(128)S(1)}, u32[]{:S(2)}) copy-start(f32[128]{0:T(128)S(1)} %fusion.108) | copy-start | bytes 1540
  192.4 27.5 %collective-permute-start = (bf16[128,4,256]{0,2,1:T(8,128)(2,1)}, bf16[128,4,256]{0,2,1:T(8,128)(2,1)}, u32[]{:S(2)}, u32[]{:S(2)}) collective-permute-start(bf16[128,4,256]{0,2,1:T(8,128)(2,1)} %bitcast.43), channel_id=1, source_target_pairs={{0,1},{2,3},{4,5},{6,7},{8,9},{10,11},{12,13},{14,15},{16,17},{18,... | collective-permute-start | bytes 786440 | tf_op jit(solution)/shard_map/ppermute | solution.py:24
  197.1 22.0 %copy-start.28 = (bf16[128,4,128]{2,0,1:T(8,128)(2,1)}, bf16[128,4,128]{2,0,1:T(8,128)(2,1)S(1)}, u32[]{:S(2)}) copy-start(bf16[128,4,128]{2,0,1:T(8,128)(2,1)S(1)} %get-tuple-element.32) | copy-start | bytes 393220
  197.1 22.0 %copy-start.30 = (bf16[128,4,128]{2,0,1:T(8,128)(2,1)}, bf16[128,4,128]{2,0,1:T(8,128)(2,1)S(1)}, u32[]{:S(2)}) copy-start(bf16[128,4,128]{2,0,1:T(8,128)(2,1)S(1)} %get-tuple-element.33) | copy-start | bytes 393220
  197.1 22.0 %copy-start.31 = (pred[128,256]{0,1:T(8,128)(4,1)S(1)}, pred[128,256]{0,1:T(8,128)(4,1)}, u32[]{:S(2)}) copy-start(pred[128,256]{0,1:T(8,128)(4,1)} %fusion.102) | copy-start | bytes 98308
  197.2 22.0 %collective-permute-start.1 = (bf16[128,4,256]{2,0,1:T(8,128)(2,1)S(1)}, bf16[128,4,256]{2,0,1:T(8,128)(2,1)S(1)}, u32[]{:S(2)}, u32[]{:S(2)}) collective-permute-start(bf16[128,4,256]{2,0,1:T(8,128)(2,1)S(1)} %pad_maximum_fusion.9), channel_id=1, source_target_pairs={{0,1},{2,3},{4,5},{6,7},{8,9},{10,11},{12,13},{14,15},{16,17},{18,... | collective-permute-start | bytes 786440 | tf_op jit(solution)/shard_map/ppermute | solution.py:24
  199.0 20.9 %copy-start.27 = (f32[128,8,128]{2,0,1:T(8,128)}, f32[128,8,128]{2,0,1:T(8,128)S(1)}, u32[]{:S(2)}) copy-start(f32[128,8,128]{2,0,1:T(8,128)S(1)} %copy.109) | copy-start | bytes 1572868
  228.0 687.0 %copy-start.44 = (f32[128]{0:T(128)}, f32[128]{0:T(128)S(1)}, u32[]{:S(2)}) copy-start(f32[128]{0:T(128)S(1)} %fusion.110) | copy-start | bytes 1540
  229.2 372.8 %reduce-scatter.8.cloned.1.call-start = ((), (), s32[]{:S(2)}) async-start(), calls=%async_computation.7 | async-start | bytes 20054016 | tf_op jit(solution)/shard_map/reduce_scatter | solution.py:158
  409.4 194.2 %copy-start.4 = (bf16[128,2304]{1,0:T(8,128)(2,1)S(1)}, bf16[128,2304]{1,0:T(8,128)(2,1)}, u32[]{:S(2)}) copy-start(bf16[128,2304]{1,0:T(8,128)(2,1)} %param.11) | copy-start | bytes 1769476
  409.4 194.2 %copy-start.38 = (f32[2304]{0:T(1024)S(1)}, f32[2304]{0:T(1024)}, u32[]{:S(2)}) copy-start(f32[2304]{0:T(1024)} %get-tuple-element.13) | copy-start | bytes 27652
  409.4 278.6 %all-gather.12.cloned.1.call-start = ((), (), s32[]{:S(2)}) async-start(), calls=%async_computation.8 | async-start | bytes 10027008 | tf_op jit(solution)/shard_map/all_gather | solution.py:169
  607.8 307.1 %reduce-scatter.10.cloned.1.call-start = ((), (), s32[]{:S(2)}) async-start(), calls=%async_computation.9 | async-start | bytes 20054016 | tf_op jit(solution)/shard_map/reduce_scatter | solution.py:177
  722.3 300.6 %reduce-scatter.12.cloned.1.call-start = ((), (), s32[]{:S(2)}) async-start(), calls=%async_computation.10 | async-start | bytes 11943936 | tf_op jit(solution)/shard_map/reduce_scatter | solution.py:183
  760.6 740.5 %reduce-scatter.14.cloned.1.call-start = ((), (), s32[]{:S(2)}) async-start(), calls=%async_computation.11 | async-start | bytes 58392576
  937.0 17.1 %collective-permute-start.2 = (bf16[128,4,256]{0,2,1:T(8,128)(2,1)}, bf16[128,4,256]{0,2,1:T(8,128)(2,1)}, u32[]{:S(2)}, u32[]{:S(2)}) collective-permute-start(bf16[128,4,256]{0,2,1:T(8,128)(2,1)} %slice.198), channel_id=1, source_target_pairs={{1,0},{3,2},{5,4},{7,6},{9,8},{11,10},{13,12},{15,14},{17,16},{19,... | collective-permute-start | bytes 786440 | tf_op jit(solution)/shard_map/ppermute | solution.py:24
  938.4 26.5 %collective-permute-start.3 = (bf16[128,4,256]{0,2,1:T(8,128)(2,1)}, bf16[128,4,256]{0,2,1:T(8,128)(2,1)}, u32[]{:S(2)}, u32[]{:S(2)}) collective-permute-start(bf16[128,4,256]{0,2,1:T(8,128)(2,1)} %slice.197), channel_id=1, source_target_pairs={{1,0},{3,2},{5,4},{7,6},{9,8},{11,10},{13,12},{15,14},{17,16},{19,... | collective-permute-start | bytes 786440 | tf_op jit(solution)/shard_map/ppermute | solution.py:24
  1028.9 55.1 %copy-start.49 = (f32[128]{0:T(128)S(1)}, f32[128]{0:T(128)}, u32[]{:S(2)}) copy-start(f32[128]{0:T(128)} %copy-done.48) | copy-start | bytes 1540
  (44 other events, 229.3 us)
Sparse Core Ops, SparseCore 0:
  10.9 172.0 all-gather.5
  184.6 106.3 all-gather.9
  293.8 81.8 all-gather.7
  409.6 192.4 reduce-scatter.7
  608.0 79.9 all-gather.11
  722.4 192.4 reduce-scatter.9
  917.8 105.0 reduce-scatter.11
  1029.9 471.1 reduce-scatter.13
where the time goes:
time: 1510 us
  waiting for transfers between devices  1110 us (74%)
  matrix products  159 us (11%)
  blocking collectives  112 us (7%)
  other arithmetic  73.9 us (5%)
  local copies, waits for them, and re-layouts  26.5 us (2%)
  between operations  15.4 us (1%)
    unnamed x9, waiting for transfers between devices  416 us
    reduce_scatter x1, waiting for transfers between devices, on_device(): lax.psum_scatter(jnp.dot(hidden, unit_weights[:, 2 * D:], preferred_eleme...  193 us
    reduce_scatter x1, waiting for transfers between devices, on_device(): lax.psum_scatter(jnp.einsum('tjc,cjd->td', d_gate_up, in_weights, preferr...  152 us
    all_gather x1, waiting for transfers between devices, on_device(): lax.all_gather(attn_weight, ('dp', 'seq'), axis=0, tiled=True)  98.3 us
    all_gather x1, waiting for transfers between devices, on_device(): shard_piece = lax.all_gather(d_ffn, 'dp', axis=0, tiled=True)  79.9 us
    all_gather x1, waiting for transfers between devices, on_device(): ffn_all = lax.all_gather(ffn_input, 'dp', axis=0, tiled=True)  79.6 us
    all_gather x1, blocking collectives, on_device(): lax.all_gather(gains, ('dp', 'seq'), axis=0, tiled=True)  72.1 us
    all_gather x1, waiting for transfers between devices, on_device(): unit_weights = lax.all_gather(ffn_weight, 'seq', axis=0, tiled=True)  61.2 us
  transfers between devices with their start and end apart: 12, of which 11 were waited for; matrix products, arithmetic and copies ran while one was open for 12% of the time, Pallas kernels for 0%

commit v1 on v0

v1 whole, which is shorter than its diff:
```python
import functools
import math

import jax
import jax.numpy as jnp
from jax import lax
from jax.experimental import pallas as pl
from jax.experimental.pallas import tpu as pltpu
from jax.sharding import PartitionSpec as P

D = 2304
HEADS = 8
KV_HEADS = 4
HEAD_DIM = 256
WINDOW = 128


soft_cap = 50.0
eps_norm = 1e-06
rope_base = 10000.0
gelu_coef = math.sqrt(2.0 / math.pi)


MESH = pl.DeviceIdType.MESH


def gelu_tanh(value):
    return 0.5 * value * (1.0 + jnp.tanh(gelu_coef * (value + 0.044715 * value * value * value)))


def gated_gelu(gate_pre, up_pre):
    return gelu_tanh(gate_pre) * up_pre


def gate_grads(gate_rows, d_hidden):
    d_gate, d_up = jax.vjp(gated_gelu, gate_rows[:, 0], gate_rows[:, 1])[1](d_hidden)
    return jnp.stack([d_gate, d_up], axis=1).astype(jnp.bfloat16)


def rms_norm(value, gain_vec):
    return value * lax.rsqrt(jnp.mean(value * value, axis=-1, keepdims=True) + eps_norm) * gain_vec


def norm_back(value, gain_vec, incoming):
    return jax.vjp(rms_norm, value, gain_vec)[1](incoming)


def doc_layout(lengths, places):
    doc_ends = jnp.cumsum(lengths, dtype=jnp.int32)
    starts = doc_ends - lengths
    doc_ids = jnp.sum(
        (places[:, None] >= doc_ends[None, :]).astype(jnp.int32), axis=1, dtype=jnp.int32
    )
    onehot = doc_ids[:, None] == jnp.arange(lengths.shape[0], dtype=jnp.int32)[None, :]
    doc_first = jnp.sum(jnp.where(onehot, starts[None, :], 0), axis=1, dtype=jnp.int32)
    return (doc_ids, places - doc_first)


def rotate(value, doc_pos):
    half_dim = value.shape[-1] // 2
    frequency = rope_base ** (-2.0 * jnp.arange(half_dim, dtype=jnp.float32) / value.shape[-1])
    angles = doc_pos.astype(jnp.float32)[:, None] * frequency[None, :]
    cosine = jnp.cos(angles)[:, None, :]
    sine_part = jnp.sin(angles)[:, None, :]
    first_half = value[..., :half_dim]
    second_half = value[..., half_dim:]
    return jnp.concatenate(
        [
            first_half * cosine - second_half * sine_part,
            second_half * cosine + first_half * sine_part,
        ],
        axis=-1,
    )


def contract_rows(left_side, right_side):
    return lax.dot_general(
        left_side, right_side, (((0,), (0,)), ((), ())), preferred_element_type=jnp.float32
    )


def contract_cols(left_side, right_side):
    return lax.dot_general(
        left_side, right_side, (((1,), (1,)), ((), ())), preferred_element_type=jnp.float32
    )


def key_mask(query_places, query_docs, key_places, key_docs):
    return (
        (key_places[None, :] >= 0)
        & (query_docs[:, None] == key_docs[None, :])
        & (key_places[None, :] <= query_places[:, None])
        & (query_places[:, None] - key_places[None, :] < WINDOW)
    )


def attn_scores(queries, all_keys, allowed):
    scores = jnp.einsum("qkgd,pkd->kgqp", queries, all_keys, preferred_element_type=jnp.float32)
    capped = jnp.where(allowed[None, None], soft_cap * jnp.tanh(scores / soft_cap), -1e30)
    return (scores, capped)


def swapped(x):
    return lax.ppermute(x, "seq", [(0, 1), (1, 0)])


def place_of(n_dp):
    dp = lax.axis_index("dp")
    seq = lax.axis_index("seq")
    a, b, c = dp // 4, lax.rem(dp // 2, 2), lax.rem(dp, 2)
    return a, b, c, seq


def number(a, b, c):
    return (a * 2 + b) * 2 + c


def enter(line, a, b, c, seq):
    barrier = pltpu.get_barrier_semaphore()

    def tell(a2, b2, c2):
        pl.semaphore_signal(
            barrier, inc=1, device_id=(number(a2, b2, c2), seq), device_id_type=MESH
        )

    tell(a, b, 1 - c)
    tell(a, 1 - b, c)

    @pl.when(a > 0)
    def _():
        tell(a - 1, b, c)

    @pl.when(a < line - 1)
    def _():
        tell(a + 1, b, c)

    peers = 2 + jnp.minimum(a, 1) + jnp.minimum(line - 1 - a, 1)
    pl.semaphore_wait(barrier, peers)


def gather_kernel(n_dp, x_ref, out_ref, own_sem, send_sem, recv_sem):
    line = n_dp // 4
    a, b, c, seq = place_of(n_dp)
    me = number(a, b, c)
    own = pltpu.make_async_copy(x_ref, out_ref.at[me], own_sem)
    own.start()
    enter(line, a, b, c, seq)

    def copy(way, src, block, a2, b2, c2):
        return pltpu.make_async_remote_copy(
            src_ref=src,
            dst_ref=out_ref.at[block],
            send_sem=send_sem.at[way, block],
            recv_sem=recv_sem.at[block],
            device_id=(number(a2, b2, c2), seq),
            device_id_type=MESH,
        )

    def up(src, block):
        return copy(0, src, block, a + 1, b, c)

    def down(src, block):
        return copy(1, src, block, a - 1, b, c)

    def across(src, block):
        return copy(2, src, block, a, 1 - b, c)

    def over(src, block):
        return copy(3, src, block, a, b, 1 - c)

    has_up, has_down = a < line - 1, a > 0

    @pl.when(has_up)
    def _():
        up(x_ref, me).start()

    @pl.when(has_down)
    def _():
        down(x_ref, me).start()

    across(x_ref, me).start()
    over(x_ref, me).start()

    def arrived(block):
        over(out_ref.at[block], block).wait_recv()

    for k in range(1, line + 1):
        if k < line:

            @pl.when(a - k >= 0)
            def _(k=k):
                block = number(a - k, b, c)
                arrived(block)
                view = out_ref.at[block]

                @pl.when(has_up)
                def _():
                    up(view, block).start()

                across(view, block).start()
                over(view, block).start()

            @pl.when(a + k < line)
            def _(k=k):
                block = number(a + k, b, c)
                arrived(block)
                view = out_ref.at[block]

                @pl.when(has_down)
                def _():
                    down(view, block).start()

                across(view, block).start()
                over(view, block).start()

        j = k - 1
        for sign in (-1, 1) if j else (1,):

            @pl.when((a + sign * j >= 0) & (a + sign * j < line))
            def _(j=j, sign=sign):
                block = number(a + sign * j, 1 - b, c)
                arrived(block)
                over(out_ref.at[block], block).start()

    for other in range(n_dp // 2):
        block = other * 2 + 1 - c
        arrived(block)

    own.wait()
    for i in range(line):
        block = number(i, b, c)
        across(out_ref.at[block], block).wait_send()
        over(out_ref.at[block], block).wait_send()
        second = number(i, 1 - b, c)
        over(out_ref.at[second], second).wait_send()

        @pl.when(has_up & (i <= a))
        def _(block=block):
            up(out_ref.at[block], block).wait_send()

        @pl.when(has_down & (i >= a))
        def _(block=block):
            down(out_ref.at[block], block).wait_send()


def gathered(x, n_dp, collective_id):
    return pl.pallas_call(
        functools.partial(gather_kernel, n_dp),
        out_shape=jax.ShapeDtypeStruct((n_dp, *x.shape), x.dtype),
        in_specs=[pl.BlockSpec(memory_space=pltpu.VMEM)],
        out_specs=pl.BlockSpec(memory_space=pl.ANY),
        scratch_shapes=[
            pltpu.SemaphoreType.DMA,
            pltpu.SemaphoreType.DMA((4, n_dp)),
            pltpu.SemaphoreType.DMA((n_dp,)),
        ],
        compiler_params=pltpu.CompilerParams(
            collective_id=collective_id, has_side_effects=True
        ),
    )(x)


def scatter_kernel(n_dp, p_ref, out_ref, from_core, from_pair, up_in, down_in, pair_out, up_out,
                   down_out, core_send, core_recv, pair_send, pair_recv, up_send, up_recv,
                   down_send, down_recv):
    line = n_dp // 4
    a, b, c, seq = place_of(n_dp)
    f32 = jnp.float32
    enter(line, a, b, c, seq)

    def core_copy(block):
        half = block // 2
        return pltpu.make_async_remote_copy(
            src_ref=p_ref.at[block],
            dst_ref=from_core.at[half],
            send_sem=core_send.at[half],
            recv_sem=core_recv.at[half],
            device_id=(number(a, b, 1 - c), seq),
            device_id_type=MESH,
        )

    def pair_copy(to):
        return pltpu.make_async_remote_copy(
            src_ref=pair_out.at[to],
            dst_ref=from_pair.at[to],
            send_sem=pair_send.at[to],
            recv_sem=pair_recv.at[to],
            device_id=(number(a, 1 - b, c), seq),
            device_id_type=MESH,
        )

    def up_copy(to):
        return pltpu.make_async_remote_copy(
            src_ref=up_out.at[to],
            dst_ref=up_in.at[to],
            send_sem=up_send.at[to],
            recv_sem=up_recv.at[to],
            device_id=(number(a + 1, b, c), seq),
            device_id_type=MESH,
        )

    def down_copy(to):
        return pltpu.make_async_remote_copy(
            src_ref=down_out.at[to],
            dst_ref=down_in.at[to],
            send_sem=down_send.at[to],
            recv_sem=down_recv.at[to],
            device_id=(number(a - 1, b, c), seq),
            device_id_type=MESH,
        )

    def each_target(act):
        for k in range(line - 1, 0, -1):

            @pl.when(a + k < line)
            def _(k=k):
                act(a + k, 1)

            @pl.when(a - k >= 0)
            def _(k=k):
                act(a - k, -1)

        act(a, 0)

    each_target(lambda to, way: core_copy(number(to, 1 - b, 1 - c)).start())
    each_target(lambda to, way: core_copy(number(to, b, 1 - c)).start())

    def send_pair(to, way):
        core_copy(number(to, 1 - b, c)).wait_recv()
        pair_out[to] = (
            p_ref[number(to, 1 - b, c)].astype(f32) + from_core[to * 2 + 1 - b].astype(f32)
        ).astype(pair_out.dtype)
        pair_copy(to).start()

    each_target(send_pair)

    def own_sum(to):
        core_copy(number(to, b, c)).wait_recv()
        pair_copy(to).wait_recv()
        return (
            p_ref[number(to, b, c)].astype(f32)
            + from_core[to * 2 + b].astype(f32)
            + from_pair[to].astype(f32)
        )

    def send_line(to, way):
        if way == 1:
            total = own_sum(to)

            @pl.when(a > 0)
            def _():
                up_copy(to).wait_recv()
                up_out[to] = (total + up_in[to].astype(f32)).astype(up_out.dtype)

            @pl.when(a == 0)
            def _():
                up_out[to] = total.astype(up_out.dtype)

            up_copy(to).start()
        elif way == -1:
            total = own_sum(to)

            @pl.when(a < line - 1)
            def _():
                down_copy(to).wait_recv()
                down_out[to] = (total + down_in[to].astype(f32)).astype(down_out.dtype)

            @pl.when(a == line - 1)
            def _():
                down_out[to] = total.astype(down_out.dtype)

            down_copy(to).start()
        else:
            out_ref[...] = own_sum(to)

            @pl.when(a > 0)
            def _():
                up_copy(to).wait_recv()
                out_ref[...] += up_in[to].astype(f32)

            @pl.when(a < line - 1)
            def _():
                down_copy(to).wait_recv()
                out_ref[...] += down_in[to].astype(f32)

    each_target(send_line)

    for i in range(n_dp // 2):
        core_copy(i * 2 + 1 - c).wait_send()
    for i in range(line):
        pair_copy(i).wait_send()

        @pl.when(i > a)
        def _(i=i):
            up_copy(i).wait_send()

        @pl.when(i < a)
        def _(i=i):
            down_copy(i).wait_send()


def scattered(parts, collective_id):
    n_dp, rows, cols = parts.shape
    held = 3 * n_dp * (rows + 16) * cols * 2
    pieces = 1
    while held > pieces * 50 * 2**20 or cols % (128 * pieces):
        pieces += 1
    width = cols // pieces
    return jnp.concatenate(
        [
            scattered_piece(parts[:, :, i * width : (i + 1) * width], collective_id)
            for i in range(pieces)
        ],
        axis=1,
    )


def scattered_piece(parts, collective_id):
    n_dp, rows, cols = parts.shape
    line = n_dp // 4
    block = (rows, cols)
    return pl.pallas_call(
        functools.partial(scatter_kernel, n_dp),
        out_shape=jax.ShapeDtypeStruct(block, jnp.float32),
        in_specs=[pl.BlockSpec(memory_space=pltpu.VMEM)],
        out_specs=pl.BlockSpec(memory_space=pltpu.VMEM),
        scratch_shapes=[pltpu.VMEM((n_dp // 2, *block), parts.dtype)]
        + [pltpu.VMEM((line, *block), parts.dtype)] * 6
        + [pltpu.SemaphoreType.DMA((n_dp // 2,))] * 2
        + [pltpu.SemaphoreType.DMA((line,))] * 6,
        compiler_params=pltpu.CompilerParams(
            collective_id=collective_id, has_side_effects=True
        ),
    )(parts)


def mine_and_other(halves, seq_index):
    first = seq_index == 0
    return (
        jnp.where(first, halves[0], halves[1]),
        jnp.where(first, halves[1], halves[0]),
    )


def in_order(own, other, seq_index):
    first = seq_index == 0
    return jnp.where(first, own, other), jnp.where(first, other, own)


def column_halves(weight):
    q_cols, k_cols = HEADS * HEAD_DIM, KV_HEADS * HEAD_DIM
    starts = (0, q_cols, q_cols + k_cols, q_cols + 2 * k_cols)
    sizes = (q_cols // 2, k_cols // 2, k_cols // 2, q_cols // 2)
    return [
        jnp.concatenate(
            [weight[:, s + h * n : s + (h + 1) * n] for s, n in zip(starts, sizes)], axis=1
        )
        for h in range(2)
    ]


def on_device(tokens, doc_lengths, attn_weight, ffn_weight, gains, out_grad):
    tok_rows = tokens.shape[0]
    n_dp = lax.axis_size("dp")
    heads, kv_heads = HEADS // 2, KV_HEADS // 2
    q_cols = heads * HEAD_DIM
    k_cols = kv_heads * HEAD_DIM
    proj_cols = q_cols + 2 * k_cols
    half_cols = proj_cols + q_cols
    group_size = HEADS // KV_HEADS
    query_scale = HEAD_DIM ** (-0.5)
    bf16 = jnp.bfloat16
    seq_index = lax.axis_index("seq")
    weight_rows = attn_weight.shape[0]

    run = jnp.arange(tok_rows, dtype=jnp.int32)
    places = jnp.concatenate([seq_index * tok_rows + run, (1 - seq_index) * tok_rows + run])
    docs, pos = doc_layout(doc_lengths[0], places)
    allowed = key_mask(places, docs, places, docs)

    gain_cols = jnp.pad(gains, ((0, 0), (0, 124)))
    my_cols, other_cols = mine_and_other(column_halves(attn_weight), seq_index)
    my_cols = jnp.concatenate([my_cols, gain_cols], axis=1)
    other_cols = jnp.concatenate([other_cols, gain_cols], axis=1)
    partner_cols = swapped(other_cols)
    other_tokens = swapped(tokens)
    ffn_own, partner_cols = lax.optimization_barrier((ffn_weight, partner_cols))
    ffn_other = swapped(ffn_own)
    block = jnp.concatenate(in_order(my_cols, partner_cols, seq_index), axis=0)
    attn_full = gathered(block, n_dp, 0).reshape(-1, half_cols + 128)
    gain_vals = attn_full[:, half_cols : half_cols + 4].astype(jnp.float32).T
    attn_weights = attn_full[:, :proj_cols]
    out_weights = attn_full[:, proj_cols:half_cols]

    pack_tokens = jnp.concatenate([tokens, other_tokens]).astype(jnp.float32)
    tokens_f = tokens.astype(jnp.float32)
    attn_in = rms_norm(pack_tokens, gain_vals[0]).astype(bf16)
    projected = jnp.dot(attn_in, attn_weights, preferred_element_type=jnp.float32)
    pack = 2 * tok_rows
    queries = (
        rotate(projected[:, :q_cols].reshape(pack, heads, HEAD_DIM), pos) * query_scale
    ).astype(bf16)
    queries = queries.reshape(pack, kv_heads, group_size, HEAD_DIM)
    keys = rotate(
        projected[:, q_cols : q_cols + k_cols].reshape(pack, kv_heads, HEAD_DIM), pos
    ).astype(bf16)
    values = projected[:, q_cols + k_cols :].reshape(pack, kv_heads, HEAD_DIM).astype(bf16)
    scores, capped = attn_scores(queries, keys, allowed)
    row_max = jnp.max(capped, axis=-1, keepdims=True)
    exp_terms = jnp.exp(capped - row_max)
    row_total = jnp.sum(exp_terms, axis=-1, keepdims=True)
    log_total = row_max + jnp.log(row_total)
    attn_probs = (exp_terms / row_total).astype(bf16)
    mixed_heads = jnp.einsum(
        "kgqp,pkd->qkgd", attn_probs, values, preferred_element_type=jnp.float32
    )
    mixed_heads = mixed_heads.reshape(pack, q_cols).astype(bf16)
    attn_part_out = contract_cols(mixed_heads, out_weights)
    attn_out = attn_part_out[:tok_rows] + swapped(attn_part_out[tok_rows:].astype(bf16)).astype(
        jnp.float32
    )
    middle = tokens_f + rms_norm(attn_out, gain_vals[1])
    ffn_input = rms_norm(middle, gain_vals[2]).astype(bf16)

    unit_weights = jnp.concatenate([ffn_own, ffn_other], axis=0)
    unit_count = unit_weights.shape[0]
    gate_weights = unit_weights[:, :D]
    up_weights = unit_weights[:, D : 2 * D]
    down_weights = unit_weights[:, 2 * D :]
    ffn_all = gathered(ffn_input, n_dp, 1).reshape(-1, D)
    gate = contract_cols(ffn_all, gate_weights)
    up = contract_cols(ffn_all, up_weights)
    hidden = gated_gelu(gate, up).astype(bf16)
    ffn_parts = jnp.dot(hidden, down_weights, preferred_element_type=jnp.float32).astype(bf16)
    ffn_out = scattered(ffn_parts.reshape(n_dp, tok_rows, D), 2)
    out_gain = gain_vals[3]
    block_out = (middle + rms_norm(ffn_out, out_gain)).astype(bf16)
    cotangent = out_grad.astype(jnp.float32)
    d_ffn_f, d_gain_out = norm_back(ffn_out, out_gain, cotangent)
    d_ffn_all = gathered(d_ffn_f.astype(bf16), n_dp, 1).reshape(-1, D)
    d_hidden = contract_cols(d_ffn_all, down_weights)
    d_gate, d_up = jax.vjp(gated_gelu, gate, up)[1](d_hidden)
    d_gate, d_up = d_gate.astype(bf16), d_up.astype(bf16)
    d_parts = (
        jnp.dot(d_gate, gate_weights, preferred_element_type=jnp.float32)
        + jnp.dot(d_up, up_weights, preferred_element_type=jnp.float32)
    ).astype(bf16)
    d_ffn_input = scattered(d_parts.reshape(n_dp, tok_rows, D), 2)

    own_units = unit_count // 2
    weight_sum = [
        contract_rows(d_gate, ffn_all),
        contract_rows(d_up, ffn_all),
        contract_rows(hidden, d_ffn_all),
    ]
    sent = jnp.concatenate([w[own_units:].astype(bf16) for w in weight_sum], axis=1)
    kept = jnp.concatenate([w[:own_units] for w in weight_sum], axis=1)
    ffn_weight_grad = kept + swapped(sent).astype(jnp.float32)

    d_middle_add, d_gain_ffn = norm_back(middle, gain_vals[2], d_ffn_input)
    d_middle = cotangent + d_middle_add
    d_attn_f, d_gain_post = norm_back(attn_out, gain_vals[1], d_middle)
    d_attn_own = d_attn_f.astype(bf16)
    d_attn = jnp.concatenate([d_attn_own, swapped(d_attn_own)])
    out_cols_grad = contract_rows(d_attn, mixed_heads)
    d_mixed = jnp.dot(d_attn, out_weights, preferred_element_type=jnp.float32).astype(bf16)
    d_mixed = d_mixed.reshape(pack, kv_heads, group_size, HEAD_DIM)
    attn_p = jnp.exp(capped - log_total)
    d_probs = jnp.einsum("qkgd,pkd->kgqp", d_mixed, values, preferred_element_type=jnp.float32)
    d_values = jnp.einsum(
        "kgqp,qkgd->pkd", attn_probs, d_mixed, preferred_element_type=jnp.float32
    )
    d_capped = attn_p * (d_probs - jnp.sum(attn_p * d_probs, axis=-1, keepdims=True))
    tanh_part = jnp.tanh(scores / soft_cap)
    d_scores = (d_capped * (1.0 - tanh_part * tanh_part)).astype(bf16)
    d_queries = jnp.einsum("kgqp,pkd->qkgd", d_scores, keys, preferred_element_type=jnp.float32)
    d_keys = jnp.einsum("kgqp,qkgd->pkd", d_scores, queries, preferred_element_type=jnp.float32)
    d_query_raw = rotate(d_queries.reshape(pack, heads, HEAD_DIM) * query_scale, -pos)
    d_key_raw = rotate(d_keys, -pos)
    d_projected = jnp.concatenate(
        [
            d_query_raw.reshape(pack, q_cols),
            d_key_raw.reshape(pack, k_cols),
            d_values.reshape(pack, k_cols),
        ],
        axis=1,
    ).astype(bf16)
    proj_grad = contract_rows(attn_in, d_projected)
    d_attn_in_part = contract_cols(d_projected, attn_weights)
    d_attn_in = d_attn_in_part[:tok_rows] + swapped(
        d_attn_in_part[tok_rows:].astype(bf16)
    ).astype(jnp.float32)
    d_tokens_add, d_gain_in = norm_back(tokens_f, gain_vals[0], d_attn_in)
    tokens_grad = d_middle + d_tokens_add

    gain_part = jnp.stack([d_gain_in, d_gain_post, d_gain_ffn, d_gain_out], axis=1)
    attn_parts = jnp.concatenate(
        [proj_grad.astype(bf16), out_cols_grad.astype(bf16),
         jnp.pad(gain_part.astype(bf16), ((0, 0), (0, 124)))],
        axis=1,
    )
    attn_sum = scattered(attn_parts.reshape(n_dp, 2 * weight_rows, half_cols + 128), 3)
    mine, others = mine_and_other(
        (attn_sum[:weight_rows], attn_sum[weight_rows:]), seq_index
    )
    partner = swapped(others.astype(bf16)).astype(jnp.float32)
    gains_grad = mine[:, half_cols : half_cols + 4] + partner[:, half_cols : half_cols + 4]
    first, second = in_order(mine, partner, seq_index)
    cuts = ((0, q_cols), (q_cols, q_cols + k_cols), (q_cols + k_cols, proj_cols),
            (proj_cols, half_cols))
    attn_weight_grad = jnp.concatenate(
        [half[:, lo:hi] for lo, hi in cuts for half in (first, second)], axis=1
    )
    return (block_out, tokens_grad, attn_weight_grad, ffn_weight_grad, gains_grad)


def solution(mesh):
    return jax.shard_map(
        on_device,
        mesh=mesh,
        in_specs=(
            P(("dp", "seq"), None),
            P("dp", None),
            P(("dp", "seq"), None),
            P(("dp", "seq"), None),
            P(("dp", "seq"), None),
            P(("dp", "seq"), None),
        ),
        out_specs=(
            P(("dp", "seq"), None),
            P(("dp", "seq"), None),
            P(("dp", "seq"), None),
            P(("dp", "seq"), None),
            P(("dp", "seq"), None),
        ),
        check_vma=False,
    )
```

time: 1510 us -> 806 us (0.53)
  waiting for transfers between devices: 1110 us -> 112 us
  Pallas kernels: 0 us -> 434 us
  blocking collectives: 112 us -> 0 us
  matrix products: 159 us -> 126 us
  local copies, waits for them, and re-layouts: 26.5 us -> 54.5 us
  other arithmetic: 73.9 us -> 58.3 us
    pallas_call x0 -> x6, Pallas kernels: none -> 434 us  [the longest x3 226 us: scattered_piece(): pl.pallas_call(functools.partial(scatter_kernel, n_dp), out_shape=jax.Sha...]
    unnamed x9 -> x0, waiting for transfers between devices: 416 us -> none
    reduce_scatter x3 -> x0, waiting for transfers between devices: 345 us -> none  [the longest x1 193 us: on_device(): lax.psum_scatter(jnp.dot(hidden, unit_weights[:, 2 * D:], preferred_eleme...]
    all_gather x4 -> x0, waiting for transfers between devices: 319 us -> none  [the longest x1 98.3 us: on_device(): lax.all_gather(attn_weight, ('dp', 'seq'), axis=0, tiled=True)]
    ppermute x4 -> x8, waiting for transfers between devices: 32.2 us -> 112 us  [swapped(): return lax.ppermute(x, 'seq', [(0, 1), (1, 0)])]
    all_gather x1 -> x0, blocking collectives: 72.1 us -> none  [on_device(): lax.all_gather(gains, ('dp', 'seq'), axis=0, tiled=True)]
    unnamed x1 -> x0, blocking collectives: 39.6 us -> none
    dot_general x10 -> x9, matrix products: 83 us -> 53.7 us  [the longest x1 14.4 us: on_device(): jnp.dot(d_gate, gate_weights, preferred_element_type=jnp.float32)]
  transfers between devices with their start and end apart: 12 -> 8, of which waited for: 11 -> 5; matrix products, arithmetic and copies ran while one was open for 12% -> 14% of each run, Pallas kernels for 0% -> 31%
where the time goes in v1:
time: 806 us; the launch traced here: 795 us
  Pallas kernels  434 us (54%)
  matrix products  126 us (16%)
  waiting for transfers between devices  112 us (14%)
  other arithmetic  58.3 us (7%)
  local copies, waits for them, and re-layouts  54.5 us (7%)
  starting transfers between devices  8.25 us (1%)
    pallas_call x3, Pallas kernels, scattered_piece(): pl.pallas_call(functools.partial(scatter_kernel, n_dp), out_shape=jax.Sha...  226 us
    pallas_call x3, Pallas kernels, gathered(): pl.pallas_call(functools.partial(gather_kernel, n_dp), out_shape=jax.Shap...  208 us
    ppermute x8, waiting for transfers between devices, swapped(): return lax.ppermute(x, 'seq', [(0, 1), (1, 0)])  112 us
    dot_general x5, matrix products, contract_cols(): lax.dot_general(left_side, right_side, (((1,), (1,)), ((), ())), preferre...  43.6 us
    dot_general x5, matrix products, contract_rows(): lax.dot_general(left_side, right_side, (((0,), (0,)), ((), ())), preferre...  24.2 us
    concatenate x1, other arithmetic, on_device(): jnp.concatenate([proj_grad.astype(bf16), out_cols_grad.astype(bf16), jnp....  22.5 us
    concatenate x1, local copies, waits for them, and re-layouts, on_device(): jnp.concatenate([proj_grad.astype(bf16), out_cols_grad.astype(bf16), jnp....  19.3 us
    unnamed x151, local copies, waits for them, and re-layouts  16.3 us
  transfers between devices with their start and end apart: 8, of which 5 were waited for; matrix products, arithmetic and copies ran while one was open for 14% of the time, Pallas kernels for 31%

profile of v1, /device:TPU:0, one launch (start us, length us, event | category | flops | bytes accessed | tf_op | source)
XLA Modules:
  0.0 795.2 jit_solution(6118533435369616564)
XLA Ops:
  10.1 8.3 %collective-permute-done.1 = bf16[72,3200]{1,0:T(8,128)(2,1)} collective-permute-done((bf16[72,3200]{1,0:T(8,128)(2,1)S(1)}, bf16[72,3200]{1,0:T(8,128)(2,1)}, u32[]{:S(2)}, u32[]{:S(2)}) %collective-permute-start.1) | collective-permute-done | bytes 460832 | tf_op jit(solution)/shard_map/ppermute | solution.py:104
  22.6 91.1 %shard_map.101 = bf16[16,144,3200]{2,1,0:T(8,128)(2,1)} custom-call(bf16[144,3200]{1,0:T(8,128)(2,1)} %pad_maximum_fusion.5.x_ref), custom_call_target="tpu_custom_call" | custom-call | tf_op jit(solution)/shard_map/pallas_call | solution.py:247
  116.3 6.3 fusion.3
  133.9 12.3 %collective-permute-done.2 = bf16[128,2304]{1,0:T(8,128)(2,1)S(1)} collective-permute-done((bf16[128,2304]{1,0:T(8,128)(2,1)S(1)}, bf16[128,2304]{1,0:T(8,128)(2,1)S(1)}, u32[]{:S(2)}, u32[]{:S(2)}) %collective-permute-start.2) | collective-permute-done | bytes 589856 | tf_op jit(solution)/shard_map/ppermute | solution.py:104
  150.1 57.8 %shard_map.102 = bf16[16,128,2304]{2,1,0:T(8,128)(2,1)} custom-call(bf16[128,2304]{1,0:T(8,128)(2,1)} %multiply_convert_fusion.2.x_ref), custom_call_target="tpu_custom_call" | custom-call | tf_op jit(solution)/shard_map/pallas_call | solution.py:247
  213.6 9.2 %fusion.26 = f32[2048,576]{0,1:T(8,128)S(1)} fusion(bf16[2048,2304]{1,0:T(8,128)(2,1)} %bitcast.108, bf16[576,6912]{1,0:T(8,128)(2,1)} %constant_dynamic-update-slice_fusion), kind=kOutput, calls=%fused_computation.50 | convolution fusion | flops 5435817984 | bytes 16809984 | tf_op jit(solution)/shard_map/dot_general | solution.py:83
  222.8 7.9 multiply_convert_fusion.1
  230.8 11.4 %convolution_convert_fusion.1 = bf16[2048,2304]{1,0:T(8,128)(2,1)} fusion(bf16[2048,576]{0,1:T(8,128)(2,1)} %get-tuple-element.78, bf16[576,6912]{1,0:T(8,128)(2,1)S(1)} %copy-done.28), kind=kOutput, calls=%fused_computation.4 | convolution fusion | flops 5440536576 | bytes 14450688 | tf_op jit(solution)/shard_map/dot_general | solution.py:534
  242.2 66.7 %shard_map.103 = f32[128,2304]{1,0:T(8,128)} custom-call(bf16[16,128,2304]{2,1,0:T(8,128)(2,1)} %bitcast.119), custom_call_target="tpu_custom_call" | custom-call | tf_op jit(solution)/shard_map/pallas_call | solution.py:422
  314.9 59.6 %shard_map.104 = bf16[16,128,2304]{2,1,0:T(8,128)(2,1)} custom-call(bf16[128,2304]{1,0:T(8,128)(2,1)} %get-tuple-element.47.x_ref), custom_call_target="tpu_custom_call" | custom-call | tf_op jit(solution)/shard_map/pallas_call | solution.py:247
  374.5 8.7 %fusion.123 = f32[576,2304]{1,0:T(8,128)S(1)} fusion(bf16[2048,576]{0,1:T(8,128)(2,1)} %get-tuple-element.78, bf16[2048,2304]{1,0:T(8,128)(2,1)} %bitcast.116), kind=kOutput, calls=%fused_computation.227 | convolution fusion | flops 5435817984 | bytes 17104896 | tf_op jit(solution)/shard_map/dot_general | solution.py:77
  386.0 16.8 %fusion.8 = (bf16[2048,576]{0,1:T(8,128)(2,1)}, bf16[2048,576]{0,1:T(8,128)(2,1)S(1)}) fusion(f32[2048,576]{0,1:T(8,128)} %copy-done.61, f32[2048,576]{0,1:T(8,128)} %get-tuple-element.79, bf16[2048,2304]{1,0:T(8,128)(2,1)} %bitcast.117, bf16[576,6912]{1,0:T(8,128)(2,1)} %constant_dynamic-update-slice_fusion), kind=kOutput, calls=%fused_computation.18 | convolution fusion | flops 5468848128 | bytes 26247168 | tf_op jit(solution)/shard_map/dot_general | solution.py:83
  402.9 5.7 fusion.122
  412.5 5.7 fusion.121
  421.1 13.5 %fusion.21 = f32[2048,2304]{1,0:T(8,128)} fusion(bf16[2048,576]{0,1:T(8,128)(2,1)S(1)} %get-tuple-element.42, bf16[576,6912]{1,0:T(8,128)(2,1)} %constant_dynamic-update-slice_fusion), kind=kOutput, calls=%fused_computation.45 | convolution fusion | flops 5435817984 | bytes 23887872 | tf_op jit(solution)/shard_map/dot_general | solution.py:546
  435.2 14.4 %add_convert_fusion = bf16[2048,2304]{1,0:T(8,128)(2,1)} fusion(f32[2048,2304]{1,0:T(8,128)} %fusion.21, bf16[2048,576]{0,1:T(8,128)(2,1)S(1)} %copy-done.63, bf16[576,6912]{1,0:T(8,128)(2,1)} %constant_dynamic-update-slice_fusion), kind=kOutput, calls=%fused_computation.1 | convolution fusion | flops 5445255168 | bytes 33325056 | tf_op jit(solution)/shard_map/dot_general | solution.py:545
  449.6 64.4 %shard_map.105 = f32[128,2304]{1,0:T(8,128)} custom-call(bf16[16,128,2304]{2,1,0:T(8,128)(2,1)} %bitcast.118), custom_call_target="tpu_custom_call" | custom-call | tf_op jit(solution)/shard_map/pallas_call | solution.py:422
  523.2 10.9 %collective-permute-done.4 = bf16[128,2304]{1,0:T(8,128)(2,1)S(1)} collective-permute-done((bf16[128,2304]{1,0:T(8,128)(2,1)S(1)}, bf16[128,2304]{1,0:T(8,128)(2,1)S(1)}, u32[]{:S(2)}, u32[]{:S(2)}) %collective-permute-start.4) | collective-permute-done | bytes 589856 | tf_op jit(solution)/shard_map/ppermute | solution.py:104
  557.8 71.1 %collective-permute-done.5 = bf16[128,2304]{1,0:T(8,128)(2,1)S(1)} collective-permute-done((bf16[128,2304]{1,0:T(8,128)(2,1)S(1)}, bf16[128,2304]{1,0:T(8,128)(2,1)S(1)}, u32[]{:S(2)}, u32[]{:S(2)}) %collective-permute-start.5) | collective-permute-done | bytes 589856 | tf_op jit(solution)/shard_map/ppermute | solution.py:104
  629.6 22.5 %pad_maximum_fusion = bf16[2304,3200]{0,1:T(8,128)(2,1)} fusion(bf16[2304,128]{0,1:T(8,128)(2,1)S(1)} %fusion.63, bf16[2304,1024]{0,1:T(8,128)(2,1)S(1)} %convolution_convert_fusion.2, bf16[2304,2048]{0,1:T(8,128)(2,1)S(1)} %convolution_convert_fusion), kind=kLoop, calls=%fused_computation.2 | loop fusion | flops 44236800 | bytes 29491200 | tf_op jit(solution)/shard_map/concatenate | solution.py:597
  652.1 19.3 %copy.74 = bf16[2304,3200]{1,0:T(8,128)(2,1)} copy(bf16[2304,3200]{0,1:T(8,128)(2,1)} %pad_maximum_fusion) | data formatting | bytes 29491200 | tf_op jit(solution)/shard_map/concatenate | solution.py:597
  671.4 94.6 %shard_map.106 = f32[144,3200]{1,0:T(8,128)} custom-call(bf16[16,144,3200]{2,1,0:T(8,128)(2,1)} %bitcast.102), custom_call_target="tpu_custom_call" | custom-call | tf_op jit(solution)/shard_map/pallas_call | solution.py:422
  770.9 9.7 %collective-permute-done.6 = bf16[72,3200]{1,0:T(8,128)(2,1)S(1)} collective-permute-done((bf16[72,3200]{1,0:T(8,128)(2,1)S(1)}, bf16[72,3200]{1,0:T(8,128)(2,1)S(1)}, u32[]{:S(2)}, u32[]{:S(2)}) %collective-permute-start.6) | collective-permute-done | bytes 460832 | tf_op jit(solution)/shard_map/ppermute | solution.py:104
  789.2 5.8 maximum_add_fusion
  (259 shorter events, 99.5 us)
Async XLA Ops:
  3.9 14.6 %collective-permute-start.1 = (bf16[72,3200]{1,0:T(8,128)(2,1)S(1)}, bf16[72,3200]{1,0:T(8,128)(2,1)}, u32[]{:S(2)}, u32[]{:S(2)}) collective-permute-start(bf16[72,3200]{1,0:T(8,128)(2,1)S(1)} %fusion.83), channel_id=1, source_target_pairs={{0,1},{1,0},{2,3},{3,2},{4,5},{5,4},{6,7},{7,6},{8,9},{9,8},{10,11... | collective-permute-start | bytes 1382408 | tf_op jit(solution)/shard_map/ppermute | solution.py:104
  6.9 109.0 %collective-permute-start = (bf16[128,2304]{1,0:T(8,128)(2,1)S(1)}, bf16[128,2304]{1,0:T(8,128)(2,1)S(1)}, u32[]{:S(2)}, u32[]{:S(2)}) collective-permute-start(bf16[128,2304]{1,0:T(8,128)(2,1)S(1)} %copy-done.8), channel_id=1, source_target_pairs={{0,1},{1,0},{2,3},{3,2},{4,5},{5,4},{6,7},{7,6},{8,9},{9,8},{10,11... | collective-permute-start | bytes 1769480 | tf_op jit(solution)/shard_map/ppermute | solution.py:104
  10.1 115.2 %copy-start.31 = (pred[256,256]{0,1:T(8,128)(4,1)}, pred[256,256]{0,1:T(8,128)(4,1)S(1)}, u32[]{:S(2)}) copy-start(pred[256,256]{0,1:T(8,128)(4,1)S(1)} %fusion.84) | copy-start | bytes 196612
  18.5 190.6 %collective-permute-start.3 = (bf16[288,6912]{1,0:T(8,128)(2,1)}, bf16[288,6912]{1,0:T(8,128)(2,1)}, u32[]{:S(2)}, u32[]{:S(2)}) collective-permute-start(bf16[288,6912]{1,0:T(8,128)(2,1)} %param.9), channel_id=1, source_target_pairs={{0,1},{1,0},{2,3},{3,2},{4,5},{5,4},{6,7},{7,6},{8,9},{9,8},{10,11... | collective-permute-start | bytes 11943944 | tf_op jit(solution)/shard_map/ppermute | solution.py:104
  130.5 16.5 %copy-start.9 = (bf16[128,2304]{1,0:T(8,128)(2,1)S(1)}, bf16[128,2304]{1,0:T(8,128)(2,1)}, u32[]{:S(2)}) copy-start(bf16[128,2304]{1,0:T(8,128)(2,1)} %param.6) | copy-start | bytes 1769476
  130.5 15.7 %collective-permute-start.2 = (bf16[128,2304]{1,0:T(8,128)(2,1)S(1)}, bf16[128,2304]{1,0:T(8,128)(2,1)S(1)}, u32[]{:S(2)}, u32[]{:S(2)}) collective-permute-start(bf16[128,2304]{1,0:T(8,128)(2,1)S(1)} %slice.335), channel_id=1, source_target_pairs={{0,1},{1,0},{2,3},{3,2},{4,5},{5,4},{6,7},{7,6},{8,9},{9,8},{10,11... | collective-permute-start | bytes 1769480 | tf_op jit(solution)/shard_map/ppermute | solution.py:104
  133.9 15.2 %copy-start.37 = (f32[2304]{0:T(1024)S(1)}, f32[2304]{0:T(1024)}, u32[]{:S(2)}) copy-start(f32[2304]{0:T(1024)} %get-tuple-element.33) | copy-start | bytes 27652
  209.1 13.7 %slice-start.2 = ((s8[9437184]{0:T(1024)(128)(4,1)}), s8[4194304]{0:T(1024)(128)(4,1)S(1)}, s32[]{:S(2)}) async-start(s8[9437184]{0:T(1024)(128)(4,1)} %bitcast.109), calls=%async_computation.2 | async-start | bytes 8388608
  384.5 18.4 %slice-start.5 = ((s8[9437184]{0:T(1024)(128)(4,1)}), s8[4194304]{0:T(1024)(128)(4,1)S(1)}, s32[]{:S(2)}) async-start(s8[9437184]{0:T(1024)(128)(4,1)} %bitcast.112), calls=%async_computation.5 | async-start | bytes 8388608
  386.0 16.9 %slice-start.6 = ((s8[9437184]{0:T(1024)(128)(4,1)}), s8[4194304]{0:T(1024)(128)(4,1)S(1)}, s32[]{:S(2)}) async-start(s8[9437184]{0:T(1024)(128)(4,1)} %bitcast.112), calls=%async_computation.6 | async-start | bytes 8388608
  386.0 16.9 %slice-start.7 = ((s8[9437184]{0:T(1024)(128)(4,1)}), s8[1048576]{0:T(1024)(128)(4,1)S(1)}, s32[]{:S(2)}) async-start(s8[9437184]{0:T(1024)(128)(4,1)} %bitcast.112), calls=%async_computation.7 | async-start | bytes 2097152
  421.1 14.1 %copy-start.63 = (bf16[2048,576]{0,1:T(8,128)(2,1)S(1)}, bf16[2048,576]{0,1:T(8,128)(2,1)}, u32[]{:S(2)}) copy-start(bf16[2048,576]{0,1:T(8,128)(2,1)} %get-tuple-element.41) | copy-start | bytes 7077892
  517.9 16.2 %collective-permute-start.4 = (bf16[128,2304]{1,0:T(8,128)(2,1)S(1)}, bf16[128,2304]{1,0:T(8,128)(2,1)S(1)}, u32[]{:S(2)}, u32[]{:S(2)}) collective-permute-start(bf16[128,2304]{1,0:T(8,128)(2,1)S(1)} %fusion.42), channel_id=1, source_target_pairs={{0,1},{1,0},{2,3},{3,2},{4,5},{5,4},{6,7},{7,6},{8,9},{9,8},{10,11... | collective-permute-start | bytes 1769480 | tf_op jit(solution)/shard_map/ppermute | solution.py:104
  521.2 268.0 %collective-permute-start.7 = (bf16[288,6912]{1,0:T(8,128)(2,1)}, bf16[288,6912]{1,0:T(8,128)(2,1)}, u32[]{:S(2)}, u32[]{:S(2)}) collective-permute-start(bf16[288,6912]{1,0:T(8,128)(2,1)} %pad_maximum_fusion.1), channel_id=1, source_target_pairs={{0,1},{1,0},{2,3},{3,2},{4,5},{5,4},{6,7},{7,6},{8,9},{9,8},{10,11... | collective-permute-start | bytes 11943944 | tf_op jit(solution)/shard_map/ppermute | solution.py:104
  523.2 14.8 %copy-start.19 = (bf16[2,2,256,256]{2,3,1,0:T(8,128)(2,1)S(1)}, bf16[2,2,256,256]{2,3,1,0:T(8,128)(2,1)}, u32[]{:S(2)}) copy-start(bf16[2,2,256,256]{2,3,1,0:T(8,128)(2,1)} %copy-done.18) | copy-start | bytes 1572868
  552.9 76.0 %copy-start.23 = (f32[256,2304]{1,0:T(8,128)}, f32[256,2304]{1,0:T(8,128)S(1)}, u32[]{:S(2)}) copy-start(f32[256,2304]{1,0:T(8,128)S(1)} %fusion.1) | copy-start | bytes 7077892
  553.0 75.9 %collective-permute-start.5 = (bf16[128,2304]{1,0:T(8,128)(2,1)S(1)}, bf16[128,2304]{1,0:T(8,128)(2,1)S(1)}, u32[]{:S(2)}, u32[]{:S(2)}) collective-permute-start(bf16[128,2304]{1,0:T(8,128)(2,1)S(1)} %slice.334), channel_id=1, source_target_pairs={{0,1},{1,0},{2,3},{3,2},{4,5},{5,4},{6,7},{7,6},{8,9},{9,8},{10,11... | collective-permute-start | bytes 1769480 | tf_op jit(solution)/shard_map/ppermute | solution.py:104
  555.0 73.9 %copy-start.52 = (f32[128]{0:T(128)S(1)}, f32[128]{0:T(128)}, u32[]{:S(2)}) copy-start(f32[128]{0:T(128)} %fusion.95) | copy-start | bytes 1540
  557.8 71.7 %copy-start.55 = (f32[128]{0:T(128)S(1)}, f32[128]{0:T(128)}, u32[]{:S(2)}) copy-start(f32[128]{0:T(128)} %get-tuple-element.65) | copy-start | bytes 1540
  557.8 71.7 %copy-start.45 = (bf16[2304,1]{0,1:T(2,128)(2,1)S(1)}, bf16[2304,1]{0,1:T(2,128)(2,1)}, u32[]{:S(2)}) copy-start(bf16[2304,1]{0,1:T(2,128)(2,1)} %stack.23) | copy-start | bytes 13828
  557.8 71.7 %copy-start.46 = (bf16[2304,1]{0,1:T(2,128)(2,1)S(1)}, bf16[2304,1]{0,1:T(2,128)(2,1)}, u32[]{:S(2)}) copy-start(bf16[2304,1]{0,1:T(2,128)(2,1)} %stack.21) | copy-start | bytes 13828
  557.8 71.7 %copy-start.47 = (bf16[2304,1]{0,1:T(2,128)(2,1)S(1)}, bf16[2304,1]{0,1:T(2,128)(2,1)}, u32[]{:S(2)}) copy-start(bf16[2304,1]{0,1:T(2,128)(2,1)} %stack.22) | copy-start | bytes 13828
  671.4 96.8 %copy-start.3 = (f32[128,2304]{1,0:T(8,128)S(1)}, f32[128,2304]{1,0:T(8,128)}, u32[]{:S(2)}) copy-start(f32[128,2304]{1,0:T(8,128)} %copy-done.2) | copy-start | bytes 3538948
  767.6 13.0 %collective-permute-start.6 = (bf16[72,3200]{1,0:T(8,128)(2,1)S(1)}, bf16[72,3200]{1,0:T(8,128)(2,1)S(1)}, u32[]{:S(2)}, u32[]{:S(2)}) collective-permute-start(bf16[72,3200]{1,0:T(8,128)(2,1)S(1)} %select_convert_fusion), channel_id=1, source_target_pairs={{0,1},{1,0},{2,3},{3,2},{4,5},{5,4},{6,7},{7,6},{8,9},{9,8},{10,11... | collective-permute-start | bytes 1382408 | tf_op jit(solution)/shard_map/ppermute | solution.py:104
  (56 other events, 206.5 us)

commit v2 on v1

--- a/solution.py
+++ b/solution.py
@@ -257,21 +257,23 @@
         compiler_params=pltpu.CompilerParams(
             collective_id=collective_id, has_side_effects=True
         ),
+        cost_estimate=pl.CostEstimate(
+            flops=0, bytes_accessed=150_000_000, transcendentals=0
+        ),
     )(x)
 
 
-def scatter_kernel(n_dp, p_ref, out_ref, from_core, from_pair, up_in, down_in, pair_out, up_out,
-                   down_out, core_send, core_recv, pair_send, pair_recv, up_send, up_recv,
-                   down_send, down_recv):
+def scatter_steps(n_dp, place, produce, core_source, out_ref, from_core, from_pair, up_buf,
+                  down_buf, pair_out, core_send, core_recv, pair_send, pair_recv, up_send,
+                  up_recv, down_send, down_recv):
     line = n_dp // 4
-    a, b, c, seq = place_of(n_dp)
-    f32 = jnp.float32
+    a, b, c, seq = place
     enter(line, a, b, c, seq)
 
     def core_copy(block):
         half = block // 2
         return pltpu.make_async_remote_copy(
-            src_ref=p_ref.at[block],
+            src_ref=core_source(block),
             dst_ref=from_core.at[half],
             send_sem=core_send.at[half],
             recv_sem=core_recv.at[half],
@@ -291,8 +293,8 @@
 
     def up_copy(to):
         return pltpu.make_async_remote_copy(
-            src_ref=up_out.at[to],
-            dst_ref=up_in.at[to],
+            src_ref=up_buf.at[to],
+            dst_ref=up_buf.at[to],
             send_sem=up_send.at[to],
             recv_sem=up_recv.at[to],
             device_id=(number(a + 1, b, c), seq),
@@ -301,8 +303,8 @@
 
     def down_copy(to):
         return pltpu.make_async_remote_copy(
-            src_ref=down_out.at[to],
-            dst_ref=down_in.at[to],
+            src_ref=down_buf.at[to],
+            dst_ref=down_buf.at[to],
             send_sem=down_send.at[to],
             recv_sem=down_recv.at[to],
             device_id=(number(a - 1, b, c), seq),
@@ -322,66 +324,53 @@
 
         act(a, 0)
 
-    each_target(lambda to, way: core_copy(number(to, 1 - b, 1 - c)).start())
-    each_target(lambda to, way: core_copy(number(to, b, 1 - c)).start())
+    def send_core(block):
+        produce(block, None, core_source(block))
+        core_copy(block).start()
+
+    each_target(lambda to, way: send_core(number(to, 1 - b, 1 - c)))
+    each_target(lambda to, way: send_core(number(to, b, 1 - c)))
 
     def send_pair(to, way):
-        core_copy(number(to, 1 - b, c)).wait_recv()
-        pair_out[to] = (
-            p_ref[number(to, 1 - b, c)].astype(f32) + from_core[to * 2 + 1 - b].astype(f32)
-        ).astype(pair_out.dtype)
+        block = number(to, 1 - b, c)
+        core_copy(block).wait_recv()
+        produce(block, [from_core.at[block // 2]], pair_out.at[to])
         pair_copy(to).start()
 
     each_target(send_pair)
 
-    def own_sum(to):
+    def line_sum(to, more, dst):
+        block = number(to, b, c)
+        produce(block, [from_core.at[block // 2], from_pair.at[to], *more], dst)
+
+    def send_line(to, way):
         core_copy(number(to, b, c)).wait_recv()
         pair_copy(to).wait_recv()
-        return (
-            p_ref[number(to, b, c)].astype(f32)
-            + from_core[to * 2 + b].astype(f32)
-            + from_pair[to].astype(f32)
-        )
-
-    def send_line(to, way):
-        if way == 1:
-            total = own_sum(to)
-
-            @pl.when(a > 0)
+        if way:
+            buf, copy = (up_buf, up_copy) if way == 1 else (down_buf, down_copy)
+            at_end = (a == 0) if way == 1 else (a == line - 1)
+
+            @pl.when(at_end)
             def _():
-                up_copy(to).wait_recv()
-                up_out[to] = (total + up_in[to].astype(f32)).astype(up_out.dtype)
-
-            @pl.when(a == 0)
+                line_sum(to, [], buf.at[to])
+
+            @pl.when(jnp.logical_not(at_end))
             def _():
-                up_out[to] = total.astype(up_out.dtype)
-
-            up_copy(to).start()
-        elif way == -1:
-            total = own_sum(to)
-
-            @pl.when(a < line - 1)
-            def _():
-                down_copy(to).wait_recv()
-                down_out[to] = (total + down_in[to].astype(f32)).astype(down_out.dtype)
-
-            @pl.when(a == line - 1)
-            def _():
-                down_out[to] = total.astype(down_out.dtype)
-
-            down_copy(to).start()
+                copy(to).wait_recv()
+                line_sum(to, [buf.at[to]], buf.at[to])
+
+            copy(to).start()
         else:
-            out_ref[...] = own_sum(to)
-
-            @pl.when(a > 0)
-            def _():
-                up_copy(to).wait_recv()
-                out_ref[...] += up_in[to].astype(f32)
-
-            @pl.when(a < line - 1)
-            def _():
-                down_copy(to).wait_recv()
-                out_ref[...] += down_in[to].astype(f32)
+            line_sum(to, [], out_ref)
+            for copy, buf, there in (
+                (up_copy, up_buf, a > 0),
+                (down_copy, down_buf, a < line - 1),
+            ):
+
+                @pl.when(there)
+                def _(copy=copy, buf=buf):
+                    copy(to).wait_recv()
+                    add_rows(out_ref, buf.at[to])
 
     each_target(send_line)
 
@@ -399,9 +388,105 @@
             down_copy(i).wait_send()
 
 
+def row_tiles(rows):
+    return 16 if rows % 16 == 0 else rows
+
+
+def add_rows(out_ref, term):
+    tile = row_tiles(out_ref.shape[0])
+
+    def step(i, _):
+        at = pl.ds(pl.multiple_of(i * tile, tile), tile)
+        out_ref[at, :] += term[at, :].astype(jnp.float32)
+        return 0
+
+    lax.fori_loop(0, out_ref.shape[0] // tile, step, 0)
+
+
+def scatter_kernel(n_dp, p_ref, out_ref, *scratch):
+    def produce(block, terms, dst):
+        if terms is None:
+            return
+        tile = row_tiles(p_ref.shape[1])
+
+        def step(i, _):
+            at = pl.ds(pl.multiple_of(i * tile, tile), tile)
+            total = p_ref[block, at, :].astype(jnp.float32)
+            for term in terms:
+                total += term[at, :].astype(jnp.float32)
+            dst[at, :] = total.astype(dst.dtype)
+            return 0
+
+        lax.fori_loop(0, p_ref.shape[1] // tile, step, 0)
+
+    scatter_steps(
+        n_dp, place_of(n_dp), produce, lambda block: p_ref.at[block], out_ref, *scratch
+    )
+
+
+def product_kernel(n_dp, left_a, right_a, left_b, right_b, extra, out_ref, core_out, *scratch):
+    cols_a, cols_b = right_a.shape[1], right_b.shape[1]
+
+    def produce(block, terms, dst):
+        def part(left, right, first, wide):
+            def step(i, _):
+                inner = pl.ds(pl.multiple_of(i * wide, wide), wide)
+                outer = pl.ds(pl.multiple_of(first + i * wide, 128), wide)
+                total = jnp.dot(
+                    left[block], right[:, inner], preferred_element_type=jnp.float32
+                )
+                for term in terms or []:
+                    total += term[:, outer].astype(jnp.float32)
+                dst[:, outer] = total.astype(dst.dtype)
+                return 0
+
+            lax.fori_loop(0, right.shape[1] // wide, step, 0)
+
+        part(left_a, right_a, 0, 256)
+        part(left_b, right_b, cols_a, 256)
+        last = pl.ds(cols_a + cols_b, extra.shape[2])
+        total = extra[block].astype(jnp.float32)
+        for term in terms or []:
+            total += term[:, last].astype(jnp.float32)
+        dst[:, last] = total.astype(dst.dtype)
+
+    scatter_steps(
+        n_dp, place_of(n_dp), produce, lambda block: core_out.at[block // 2], out_ref, *scratch
+    )
+
+
+def scatter_scratch(n_dp, rows, cols, dtype):
+    line = n_dp // 4
+    return (
+        [pltpu.VMEM((n_dp // 2, rows, cols), dtype)]
+        + [pltpu.VMEM((line, rows, cols), dtype)] * 4
+        + [pltpu.SemaphoreType.DMA((n_dp // 2,))] * 2
+        + [pltpu.SemaphoreType.DMA((line,))] * 6
+    )
+
+
+def scattered_products(left_a, right_a, left_b, right_b, extra, collective_id):
+    n_dp, rows, _ = left_a.shape
+    cols = right_a.shape[1] + right_b.shape[1] + extra.shape[2]
+    return pl.pallas_call(
+        functools.partial(product_kernel, n_dp),
+        out_shape=jax.ShapeDtypeStruct((rows, cols), jnp.float32),
+        in_specs=[pl.BlockSpec(memory_space=pltpu.VMEM)] * 5,
+        out_specs=pl.BlockSpec(memory_space=pltpu.VMEM),
+        scratch_shapes=[pltpu.VMEM((n_dp // 2, rows, cols), jnp.bfloat16)]
+        + scatter_scratch(n_dp, rows, cols, jnp.bfloat16),
+        compiler_params=pltpu.CompilerParams(
+            collective_id=collective_id, has_side_effects=True
+        ),
+        cost_estimate=pl.CostEstimate(
+            flops=0, bytes_accessed=200_000_000, transcendentals=0
+        ),
+    )(left_a, right_a, left_b, right_b, extra)
+
+
 def scattered(parts, collective_id):
     n_dp, rows, cols = parts.shape
-    held = 3 * n_dp * (rows + 16) * cols * 2
+    held = n_dp * (1 + 1 / 2 + 1) * rows * cols * 2
     pieces = 1
     while held > pieces * 50 * 2**20 or cols % (128 * pieces):
         pieces += 1
@@ -417,19 +502,17 @@
 
 def scattered_piece(parts, collective_id):
     n_dp, rows, cols = parts.shape
-    line = n_dp // 4
-    block = (rows, cols)
     return pl.pallas_call(
         functools.partial(scatter_kernel, n_dp),
-        out_shape=jax.ShapeDtypeStruct(block, jnp.float32),
+        out_shape=jax.ShapeDtypeStruct((rows, cols), jnp.float32),
         in_specs=[pl.BlockSpec(memory_space=pltpu.VMEM)],
         out_specs=pl.BlockSpec(memory_space=pltpu.VMEM),
-        scratch_shapes=[pltpu.VMEM((n_dp // 2, *block), parts.dtype)]
-        + [pltpu.VMEM((line, *block), parts.dtype)] * 6
-        + [pltpu.SemaphoreType.DMA((n_dp // 2,))] * 2
-        + [pltpu.SemaphoreType.DMA((line,))] * 6,
+        scratch_shapes=scatter_scratch(n_dp, rows, cols, parts.dtype),
         compiler_params=pltpu.CompilerParams(
             collective_id=collective_id, has_side_effects=True
+        ),
+        cost_estimate=pl.CostEstimate(
+            flops=0, bytes_accessed=150_000_000, transcendentals=0
         ),
     )(parts)
 
@@ -562,7 +645,6 @@
     d_attn_f, d_gain_post = norm_back(attn_out, gain_vals[1], d_middle)
     d_attn_own = d_attn_f.astype(bf16)
     d_attn = jnp.concatenate([d_attn_own, swapped(d_attn_own)])
-    out_cols_grad = contract_rows(d_attn, mixed_heads)
     d_mixed = jnp.dot(d_attn, out_weights, preferred_element_type=jnp.float32).astype(bf16)
     d_mixed = d_mixed.reshape(pack, kv_heads, group_size, HEAD_DIM)
     attn_p = jnp.exp(capped - log_total)
@@ -585,21 +667,27 @@
         ],
         axis=1,
     ).astype(bf16)
-    proj_grad = contract_rows(attn_in, d_projected)
     d_attn_in_part = contract_cols(d_projected, attn_weights)
     d_attn_in = d_attn_in_part[:tok_rows] + swapped(
         d_attn_in_part[tok_rows:].astype(bf16)
     ).astype(jnp.float32)
-    d_tokens_add, d_gain_in = norm_back(tokens_f, gain_vals[0], d_attn_in)
+    normed = pack_tokens * lax.rsqrt(
+        jnp.mean(pack_tokens * pack_tokens, axis=-1, keepdims=True) + eps_norm
+    )
+    d_gain_in = jnp.sum(d_attn_in_part * normed, axis=0)
+
+    gain_part = jnp.stack([d_gain_in, d_gain_post, d_gain_ffn, d_gain_out], axis=1)
+    block_rows = (n_dp, 2 * weight_rows)
+    attn_sum = scattered_products(
+        attn_in.T.reshape(*block_rows, pack),
+        d_projected,
+        d_attn.T.reshape(*block_rows, pack),
+        mixed_heads,
+        jnp.pad(gain_part.astype(bf16), ((0, 0), (0, 124))).reshape(*block_rows, 128),
+        3,
+    )
+    d_tokens_add = norm_back(tokens_f, gain_vals[0], d_attn_in)[0]
     tokens_grad = d_middle + d_tokens_add
-
-    gain_part = jnp.stack([d_gain_in, d_gain_post, d_gain_ffn, d_gain_out], axis=1)
-    attn_parts = jnp.concatenate(
-        [proj_grad.astype(bf16), out_cols_grad.astype(bf16),
-         jnp.pad(gain_part.astype(bf16), ((0, 0), (0, 124)))],
-        axis=1,
-    )
-    attn_sum = scattered(attn_parts.reshape(n_dp, 2 * weight_rows, half_cols + 128), 3)
     mine, others = mine_and_other(
         (attn_sum[:weight_rows], attn_sum[weight_rows:]), seq_index
     )

time: 806 us -> 798 us (0.990)
  other arithmetic: 58.3 us -> 38.4 us
  Pallas kernels: 434 us -> 450 us
    pallas_call x0 -> x1, Pallas kernels: none -> 109 us  [scattered_products(): pl.pallas_call(functools.partial(product_kernel, n_dp), out_shape=jax.Sha...]
    pallas_call x3 -> x2, Pallas kernels: 226 us -> 132 us  [scattered_piece(): pl.pallas_call(functools.partial(scatter_kernel, n_dp), out_shape=jax.Sha...]
    concatenate x1, other arithmetic: 22.5 us -> 1.1 us  [on_device(): jnp.concatenate([d_query_raw.reshape(pack, q_cols), d_key_raw.reshape(pac...]
    concatenate x1 -> x0, local copies, waits for them, and re-layouts: 19.3 us -> none  [on_device(): jnp.concatenate([proj_grad.astype(bf16), out_cols_grad.astype(bf16), jnp....]
    unnamed x151 -> x157, local copies, waits for them, and re-layouts: 16.3 us -> 20.5 us
    dot_general x5 -> x3, matrix products: 24.2 us -> 27.7 us  [contract_rows(): lax.dot_general(left_side, right_side, (((0,), (0,)), ((), ())), preferre...]
  transfers between devices with their start and end apart: 8 -> 8, of which waited for: 5 -> 4; matrix products, arithmetic and copies ran while one was open for 14% -> 8% of each run, Pallas kernels for 31% -> 19%
where the time goes in v2:
time: 798 us; the launch traced here: 787 us
  Pallas kernels  450 us (56%)
  matrix products  126 us (16%)
  waiting for transfers between devices  109 us (14%)
  local copies, waits for them, and re-layouts  52.6 us (7%)
  other arithmetic  38.4 us (5%)
  starting transfers between devices  8.67 us (1%)
    pallas_call x3, Pallas kernels, gathered(): pl.pallas_call(functools.partial(gather_kernel, n_dp), out_shape=jax.Shap...  209 us
    pallas_call x2, Pallas kernels, scattered_piece(): pl.pallas_call(functools.partial(scatter_kernel, n_dp), out_shape=jax.Sha...  132 us
    pallas_call x1, Pallas kernels, scattered_products(): pl.pallas_call(functools.partial(product_kernel, n_dp), out_shape=jax.Sha...  109 us
    ppermute x8, waiting for transfers between devices, swapped(): return lax.ppermute(x, 'seq', [(0, 1), (1, 0)])  109 us
    dot_general x5, matrix products, contract_cols(): lax.dot_general(left_side, right_side, (((1,), (1,)), ((), ())), preferre...  41.5 us
    dot_general x3, matrix products, contract_rows(): lax.dot_general(left_side, right_side, (((0,), (0,)), ((), ())), preferre...  27.7 us
    unnamed x157, local copies, waits for them, and re-layouts  20.5 us
  transfers between devices with their start and end apart: 8, of which 4 were waited for; matrix products, arithmetic and copies ran while one was open for 8% of the time, Pallas kernels for 19%

profile of v2, /device:TPU:0, one launch (start us, length us, event | category | flops | bytes accessed | tf_op | source)
XLA Modules:
  0.0 787.2 jit_solution(11926975632253196305)
XLA Ops:
  10.1 8.3 %collective-permute-done.1 = bf16[72,3200]{1,0:T(8,128)(2,1)} collective-permute-done((bf16[72,3200]{1,0:T(8,128)(2,1)S(1)}, bf16[72,3200]{1,0:T(8,128)(2,1)}, u32[]{:S(2)}, u32[]{:S(2)}) %collective-permute-start.1) | collective-permute-done | bytes 460832 | tf_op jit(solution)/shard_map/ppermute | solution.py:104
  22.7 91.1 %shard_map.101 = bf16[16,144,3200]{2,1,0:T(8,128)(2,1)} custom-call(bf16[144,3200]{1,0:T(8,128)(2,1)} %pad_maximum_fusion.4.x_ref), custom_call_target="tpu_custom_call" | custom-call | bytes 150000000 | tf_op jit(solution)/shard_map/pallas_call | solution.py:247
  116.3 6.3 fusion.3
  129.6 4.0 fusion.13
  140.6 9.8 %collective-permute-done.2 = bf16[128,2304]{1,0:T(8,128)(2,1)S(1)} collective-permute-done((bf16[128,2304]{1,0:T(8,128)(2,1)}, bf16[128,2304]{1,0:T(8,128)(2,1)S(1)}, u32[]{:S(2)}, u32[]{:S(2)}) %collective-permute-start.2) | collective-permute-done | bytes 589856 | tf_op jit(solution)/shard_map/ppermute | solution.py:104
  153.9 57.7 %shard_map.102 = bf16[16,128,2304]{2,1,0:T(8,128)(2,1)} custom-call(bf16[128,2304]{1,0:T(8,128)(2,1)} %multiply_convert_fusion.2.x_ref), custom_call_target="tpu_custom_call" | custom-call | bytes 150000000 | tf_op jit(solution)/shard_map/pallas_call | solution.py:247
  211.6 4.5 constant_dynamic-update-slice_fusion
  216.0 9.2 %fusion.28 = f32[2048,576]{0,1:T(8,128)S(1)} fusion(bf16[2048,2304]{1,0:T(8,128)(2,1)} %bitcast.115, bf16[576,6912]{1,0:T(8,128)(2,1)} %constant_dynamic-update-slice_fusion), kind=kOutput, calls=%fused_computation.44 | convolution fusion | flops 5435817984 | bytes 16809984 | tf_op jit(solution)/shard_map/dot_general | solution.py:83
  225.3 8.0 %multiply_convert_fusion.1 = (bf16[2048,576]{0,1:T(8,128)(2,1)}, f32[2048,576]{0,1:T(8,128)}) fusion(f32[2048,576]{0,1:T(8,128)S(1)} %fusion.28, bf16[2048,2304]{1,0:T(8,128)(2,1)S(1)} %bitcast.119, bf16[576,6912]{1,0:T(8,128)(2,1)S(1)} %copy-done.23), kind=kOutput, calls=%fused_computation.19 | convolution fusion | flops 5447614464 | bytes 23887872 | tf_op jit(solution)/shard_map/dot_general | solution.py:83
  233.3 11.5 %convolution_convert_fusion = bf16[2048,2304]{1,0:T(8,128)(2,1)} fusion(bf16[2048,576]{0,1:T(8,128)(2,1)} %get-tuple-element.83, bf16[576,6912]{1,0:T(8,128)(2,1)S(1)} %copy-done.23), kind=kOutput, calls=%fused_computation.2 | convolution fusion | flops 5440536576 | bytes 14450688 | tf_op jit(solution)/shard_map/dot_general | solution.py:617
  244.8 67.2 %shard_map.103 = f32[128,2304]{1,0:T(8,128)} custom-call(bf16[16,128,2304]{2,1,0:T(8,128)(2,1)} %bitcast.126), custom_call_target="tpu_custom_call" | custom-call | bytes 150000000 | tf_op jit(solution)/shard_map/pallas_call | solution.py:505
  317.1 59.9 %shard_map.104 = bf16[16,128,2304]{2,1,0:T(8,128)(2,1)} custom-call(bf16[128,2304]{1,0:T(8,128)(2,1)} %get-tuple-element.47.x_ref), custom_call_target="tpu_custom_call" | custom-call | bytes 150000000 | tf_op jit(solution)/shard_map/pallas_call | solution.py:247
  377.1 11.7 %fusion.116 = f32[576,2304]{1,0:T(8,128)} fusion(bf16[2048,576]{0,1:T(8,128)(2,1)} %get-tuple-element.83, bf16[2048,2304]{1,0:T(8,128)(2,1)} %bitcast.123), kind=kOutput, calls=%fused_computation.217 | convolution fusion | flops 5435817984 | bytes 17104896 | tf_op jit(solution)/shard_map/dot_general | solution.py:77
  388.8 14.8 %fusion.8 = (bf16[2048,576]{0,1:T(8,128)(2,1)S(1)}, bf16[2048,576]{0,1:T(8,128)(2,1)S(1)}) fusion(f32[2048,576]{0,1:T(8,128)} %copy-done.58, f32[2048,576]{0,1:T(8,128)} %get-tuple-element.84, bf16[2048,2304]{1,0:T(8,128)(2,1)} %bitcast.124, bf16[576,6912]{1,0:T(8,128)(2,1)} %constant_dynamic-update-slice_fusion), kind=kOutput, calls=%fused_computation.15 | convolution fusion | flops 5468848128 | bytes 26247168 | tf_op jit(solution)/shard_map/dot_general | solution.py:83
  403.6 7.5 fusion.114
  411.2 13.2 %fusion.23 = f32[2048,2304]{1,0:T(8,128)} fusion(bf16[2048,576]{0,1:T(8,128)(2,1)S(1)} %get-tuple-element.42, bf16[576,6912]{1,0:T(8,128)(2,1)} %constant_dynamic-update-slice_fusion), kind=kOutput, calls=%fused_computation.39 | convolution fusion | flops 5435817984 | bytes 23887872 | tf_op jit(solution)/shard_map/dot_general | solution.py:629
  424.4 14.8 %add_convert_fusion = bf16[2048,2304]{1,0:T(8,128)(2,1)} fusion(f32[2048,2304]{1,0:T(8,128)} %fusion.23, bf16[2048,576]{0,1:T(8,128)(2,1)S(1)} %get-tuple-element.41, bf16[576,6912]{1,0:T(8,128)(2,1)} %constant_dynamic-update-slice_fusion), kind=kOutput, calls=%fused_computation.1 | convolution fusion | flops 5445255168 | bytes 33325056 | tf_op jit(solution)/shard_map/dot_general | solution.py:628
  439.2 64.9 %shard_map.105 = f32[128,2304]{1,0:T(8,128)} custom-call(bf16[16,128,2304]{2,1,0:T(8,128)(2,1)} %bitcast.125), custom_call_target="tpu_custom_call" | custom-call | bytes 150000000 | tf_op jit(solution)/shard_map/pallas_call | solution.py:505
  510.6 8.5 %fusion.115 = f32[576,2304]{1,0:T(8,128)S(1)} fusion(bf16[2048,576]{0,1:T(8,128)(2,1)S(1)} %copy-done.60, bf16[2048,2304]{1,0:T(8,128)(2,1)} %bitcast.116), kind=kOutput, calls=%fused_computation.216 | convolution fusion | flops 5435817984 | bytes 17104896 | tf_op jit(solution)/shard_map/dot_general | solution.py:77
  543.9 5.5 fusion.1
  561.3 109.1 %shard_map.106 = f32[144,3200]{1,0:T(8,128)} custom-call(bf16[16,144,256]{2,1,0:T(8,128)(2,1)} %bitcast.130, bf16[256,2048]{1,0:T(8,128)(2,1)} %pad_maximum_fusion.3.right_a, bf16[16,144,256]{2,1,0:T(8,128)(2,1)} %bitcast.129, bf16[256,1024]{1,0:T(8,128)(2,1)} %copy.103.right_b, bf16[16,144,128]{2,1,0:T(8,128)(2,1)} %bitcast.133), custom_call_target="tpu_custom_call" | custom-call | bytes 200000000 | tf_op jit(solution)/shard_map/pallas_call | solution.py:471
  679.1 6.4 collective-permute-done.6
  693.7 84.6 %collective-permute-done.5 = bf16[128,2304]{1,0:T(8,128)(2,1)S(1)} collective-permute-done((bf16[128,2304]{1,0:T(8,128)(2,1)}, bf16[128,2304]{1,0:T(8,128)(2,1)S(1)}, u32[]{:S(2)}, u32[]{:S(2)}) %collective-permute-start.5) | collective-permute-done | bytes 589856 | tf_op jit(solution)/shard_map/ppermute | solution.py:104
  781.3 5.6 maximum_add_fusion
  (272 shorter events, 101.0 us)
Async XLA Ops:
  3.9 14.6 %collective-permute-start.1 = (bf16[72,3200]{1,0:T(8,128)(2,1)S(1)}, bf16[72,3200]{1,0:T(8,128)(2,1)}, u32[]{:S(2)}, u32[]{:S(2)}) collective-permute-start(bf16[72,3200]{1,0:T(8,128)(2,1)S(1)} %fusion.78), channel_id=1, source_target_pairs={{0,1},{1,0},{2,3},{3,2},{4,5},{5,4},{6,7},{7,6},{8,9},{9,8},{10,11... | collective-permute-start | bytes 1382408 | tf_op jit(solution)/shard_map/ppermute | solution.py:104
  6.9 109.0 %collective-permute-start = (bf16[128,2304]{1,0:T(8,128)(2,1)S(1)}, bf16[128,2304]{1,0:T(8,128)(2,1)S(1)}, u32[]{:S(2)}, u32[]{:S(2)}) collective-permute-start(bf16[128,2304]{1,0:T(8,128)(2,1)S(1)} %copy-done.1), channel_id=1, source_target_pairs={{0,1},{1,0},{2,3},{3,2},{4,5},{5,4},{6,7},{7,6},{8,9},{9,8},{10,11... | collective-permute-start | bytes 1769480 | tf_op jit(solution)/shard_map/ppermute | solution.py:104
  8.4 12.1 %copy-start.25 = (f32[256,128]{1,0:T(8,128)}, f32[256,128]{1,0:T(8,128)S(1)}, u32[]{:S(2)}) copy-start(f32[256,128]{1,0:T(8,128)S(1)} %get-tuple-element.73) | copy-start | bytes 393220
  8.4 12.1 %copy-start.27 = (f32[256,128]{1,0:T(8,128)}, f32[256,128]{1,0:T(8,128)S(1)}, u32[]{:S(2)}) copy-start(f32[256,128]{1,0:T(8,128)S(1)} %get-tuple-element.74) | copy-start | bytes 393220
  10.1 118.3 %copy-start.30 = (pred[256,256]{0,1:T(8,128)(4,1)}, pred[256,256]{0,1:T(8,128)(4,1)S(1)}, u32[]{:S(2)}) copy-start(pred[256,256]{0,1:T(8,128)(4,1)S(1)} %fusion.79) | copy-start | bytes 196612
  18.5 193.1 %collective-permute-start.3 = (bf16[288,6912]{1,0:T(8,128)(2,1)}, bf16[288,6912]{1,0:T(8,128)(2,1)}, u32[]{:S(2)}, u32[]{:S(2)}) collective-permute-start(bf16[288,6912]{1,0:T(8,128)(2,1)} %param.9), channel_id=1, source_target_pairs={{0,1},{1,0},{2,3},{3,2},{4,5},{5,4},{6,7},{7,6},{8,9},{9,8},{10,11... | collective-permute-start | bytes 11943944 | tf_op jit(solution)/shard_map/ppermute | solution.py:104
  133.6 17.0 %copy-start.3 = (f32[256,2304]{1,0:T(8,128)}, f32[256,2304]{1,0:T(8,128)S(1)}, u32[]{:S(2)}) copy-start(f32[256,2304]{1,0:T(8,128)S(1)} %fusion.13) | copy-start | bytes 7077892
  134.5 15.8 %collective-permute-start.2 = (bf16[128,2304]{1,0:T(8,128)(2,1)}, bf16[128,2304]{1,0:T(8,128)(2,1)S(1)}, u32[]{:S(2)}, u32[]{:S(2)}) collective-permute-start(bf16[128,2304]{1,0:T(8,128)(2,1)} %slice.331), channel_id=1, source_target_pairs={{0,1},{1,0},{2,3},{3,2},{4,5},{5,4},{6,7},{7,6},{8,9},{9,8},{10,11... | collective-permute-start | bytes 1769480 | tf_op jit(solution)/shard_map/ppermute | solution.py:104
  140.6 12.3 %copy-start.40 = (f32[2304]{0:T(1024)S(1)}, f32[2304]{0:T(1024)}, u32[]{:S(2)}) copy-start(f32[2304]{0:T(1024)} %get-tuple-element.33) | copy-start | bytes 27652
  211.5 13.7 %slice-start.4 = ((s8[9437184]{0:T(1024)(128)(4,1)}), s8[4194304]{0:T(1024)(128)(4,1)S(1)}, s32[]{:S(2)}) async-start(s8[9437184]{0:T(1024)(128)(4,1)} %bitcast.117), calls=%async_computation.4 | async-start | bytes 8388608
  244.8 68.7 %copy-start.9 = (bf16[128,2304]{1,0:T(8,128)(2,1)S(1)}, bf16[128,2304]{1,0:T(8,128)(2,1)}, u32[]{:S(2)}) copy-start(bf16[128,2304]{1,0:T(8,128)(2,1)} %param.11) | copy-start | bytes 1769476
  244.8 68.7 %copy-start.46 = (f32[2304]{0:T(1024)S(1)}, f32[2304]{0:T(1024)}, u32[]{:S(2)}) copy-start(f32[2304]{0:T(1024)} %get-tuple-element.32) | copy-start | bytes 27652
  377.1 26.6 %slice-start.7 = ((s8[9437184]{0:T(1024)(128)(4,1)}), s8[4194304]{0:T(1024)(128)(4,1)S(1)}, s32[]{:S(2)}) async-start(s8[9437184]{0:T(1024)(128)(4,1)} %bitcast.120), calls=%async_computation.7 | async-start | bytes 8388608
  377.1 26.6 %slice-start.8 = ((s8[9437184]{0:T(1024)(128)(4,1)}), s8[4194304]{0:T(1024)(128)(4,1)S(1)}, s32[]{:S(2)}) async-start(s8[9437184]{0:T(1024)(128)(4,1)} %bitcast.120), calls=%async_computation.8 | async-start | bytes 8388608
  388.8 14.9 %slice-start.9 = ((s8[9437184]{0:T(1024)(128)(4,1)}), s8[1048576]{0:T(1024)(128)(4,1)S(1)}, s32[]{:S(2)}) async-start(s8[9437184]{0:T(1024)(128)(4,1)} %bitcast.120), calls=%async_computation.9 | async-start | bytes 2097152
  439.2 65.0 %copy-start.41 = (f32[2304]{0:T(1024)S(1)}, f32[2304]{0:T(1024)}, u32[]{:S(2)}) copy-start(f32[2304]{0:T(1024)} %get-tuple-element.33) | copy-start | bytes 27652
  508.3 10.8 %slice-start = ((s8[5308416]{0:T(1024)(128)(4,1)}), s8[4194304]{0:T(1024)(128)(4,1)S(1)}, s32[]{:S(2)}) async-start(s8[5308416]{0:T(1024)(128)(4,1)} %bitcast.113), calls=%async_computation | async-start | bytes 8388608
  509.3 19.8 %copy-start.20 = (bf16[128,2304]{1,0:T(8,128)(2,1)}, bf16[128,2304]{1,0:T(8,128)(2,1)S(1)}, u32[]{:S(2)}) copy-start(bf16[128,2304]{1,0:T(8,128)(2,1)S(1)} %fusion.44) | copy-start | bytes 1769476
  509.3 19.8 %collective-permute-start.4 = (bf16[128,2304]{1,0:T(8,128)(2,1)S(1)}, bf16[128,2304]{1,0:T(8,128)(2,1)S(1)}, u32[]{:S(2)}, u32[]{:S(2)}) collective-permute-start(bf16[128,2304]{1,0:T(8,128)(2,1)S(1)} %fusion.44), channel_id=1, source_target_pairs={{0,1},{1,0},{2,3},{3,2},{4,5},{5,4},{6,7},{7,6},{8,9},{9,8},{10,11... | collective-permute-start | bytes 1769480 | tf_op jit(solution)/shard_map/ppermute | solution.py:104
  671.9 13.5 %collective-permute-start.6 = (bf16[72,3200]{1,0:T(8,128)(2,1)S(1)}, bf16[72,3200]{1,0:T(8,128)(2,1)S(1)}, u32[]{:S(2)}, u32[]{:S(2)}) collective-permute-start(bf16[72,3200]{1,0:T(8,128)(2,1)S(1)} %select_convert_fusion), channel_id=1, source_target_pairs={{0,1},{1,0},{2,3},{3,2},{4,5},{5,4},{6,7},{7,6},{8,9},{9,8},{10,11... | collective-permute-start | bytes 1382408 | tf_op jit(solution)/shard_map/ppermute | solution.py:104
  672.5 13.0 %copy-start.5 = (f32[144,3200]{1,0:T(8,128)S(1)}, f32[144,3200]{1,0:T(8,128)}, u32[]{:S(2)}) copy-start(f32[144,3200]{1,0:T(8,128)} %shard_map.106) | copy-start | bytes 5529604
  676.1 104.0 %collective-permute-start.7 = (bf16[288,6912]{1,0:T(8,128)(2,1)}, bf16[288,6912]{1,0:T(8,128)(2,1)}, u32[]{:S(2)}, u32[]{:S(2)}) collective-permute-start(bf16[288,6912]{1,0:T(8,128)(2,1)} %pad_maximum_fusion), channel_id=1, source_target_pairs={{0,1},{1,0},{2,3},{3,2},{4,5},{5,4},{6,7},{7,6},{8,9},{9,8},{10,11... | collective-permute-start | bytes 11943944 | tf_op jit(solution)/shard_map/ppermute | solution.py:104
  678.6 99.7 %collective-permute-start.5 = (bf16[128,2304]{1,0:T(8,128)(2,1)}, bf16[128,2304]{1,0:T(8,128)(2,1)S(1)}, u32[]{:S(2)}, u32[]{:S(2)}) collective-permute-start(bf16[128,2304]{1,0:T(8,128)(2,1)} %slice.330), channel_id=1, source_target_pairs={{0,1},{1,0},{2,3},{3,2},{4,5},{5,4},{6,7},{7,6},{8,9},{9,8},{10,11... | collective-permute-start | bytes 1769480 | tf_op jit(solution)/shard_map/ppermute | solution.py:104
  690.2 88.5 %copy-start.7 = (f32[128,2304]{1,0:T(8,128)S(1)}, f32[128,2304]{1,0:T(8,128)}, u32[]{:S(2)}) copy-start(f32[128,2304]{1,0:T(8,128)} %copy-done.6) | copy-start | bytes 3538948
  (57 other events, 185.3 us)

commit v3 on v2

--- a/solution.py
+++ b/solution.py
@@ -30,11 +30,6 @@
 
 def gated_gelu(gate_pre, up_pre):
     return gelu_tanh(gate_pre) * up_pre
-
-
-def gate_grads(gate_rows, d_hidden):
-    d_gate, d_up = jax.vjp(gated_gelu, gate_rows[:, 0], gate_rows[:, 1])[1](d_hidden)
-    return jnp.stack([d_gate, d_up], axis=1).astype(jnp.bfloat16)
 
 
 def rms_norm(value, gain_vec):
@@ -104,7 +99,7 @@
     return lax.ppermute(x, "seq", [(0, 1), (1, 0)])
 
 
-def place_of(n_dp):
+def place_of():
     dp = lax.axis_index("dp")
     seq = lax.axis_index("seq")
     a, b, c = dp // 4, lax.rem(dp // 2, 2), lax.rem(dp, 2)
@@ -140,7 +135,7 @@
 
 def gather_kernel(n_dp, x_ref, out_ref, own_sem, send_sem, recv_sem):
     line = n_dp // 4
-    a, b, c, seq = place_of(n_dp)
+    a, b, c, seq = place_of()
     me = number(a, b, c)
     own = pltpu.make_async_copy(x_ref, out_ref.at[me], own_sem)
     own.start()
@@ -419,9 +414,7 @@
 
         lax.fori_loop(0, p_ref.shape[1] // tile, step, 0)
 
-    scatter_steps(
-        n_dp, place_of(n_dp), produce, lambda block: p_ref.at[block], out_ref, *scratch
-    )
+    scatter_steps(n_dp, place_of(), produce, lambda block: p_ref.at[block], out_ref, *scratch)
 
 
 def product_kernel(n_dp, left_a, right_a, left_b, right_b, extra, out_ref, core_out, *scratch):
@@ -451,7 +444,7 @@
         dst[:, last] = total.astype(dst.dtype)
 
     scatter_steps(
-        n_dp, place_of(n_dp), produce, lambda block: core_out.at[block // 2], out_ref, *scratch
+        n_dp, place_of(), produce, lambda block: core_out.at[block // 2], out_ref, *scratch
     )
 
 
@@ -542,7 +535,7 @@
     ]
 
 
-def on_device(tokens, doc_lengths, attn_weight, ffn_weight, gains, out_grad):
+def layer(tokens, doc_lengths, attn_weight, ffn_weight, gains, out_grad):
     tok_rows = tokens.shape[0]
     n_dp = lax.axis_size("dp")
     heads, kv_heads = HEADS // 2, KV_HEADS // 2
@@ -638,13 +631,15 @@
     ]
     sent = jnp.concatenate([w[own_units:].astype(bf16) for w in weight_sum], axis=1)
     kept = jnp.concatenate([w[:own_units] for w in weight_sum], axis=1)
-    ffn_weight_grad = kept + swapped(sent).astype(jnp.float32)
+    grad_other = swapped(sent)
+    ffn_weight_grad = kept + grad_other.astype(jnp.float32)
 
     d_middle_add, d_gain_ffn = norm_back(middle, gain_vals[2], d_ffn_input)
     d_middle = cotangent + d_middle_add
     d_attn_f, d_gain_post = norm_back(attn_out, gain_vals[1], d_middle)
     d_attn_own = d_attn_f.astype(bf16)
-    d_attn = jnp.concatenate([d_attn_own, swapped(d_attn_own)])
+    d_attn_other = swapped(d_attn_own)
+    d_attn = jnp.concatenate([d_attn_own, d_attn_other])
     d_mixed = jnp.dot(d_attn, out_weights, preferred_element_type=jnp.float32).astype(bf16)
     d_mixed = d_mixed.reshape(pack, kv_heads, group_size, HEAD_DIM)
     attn_p = jnp.exp(capped - log_total)
@@ -668,9 +663,8 @@
         axis=1,
     ).astype(bf16)
     d_attn_in_part = contract_cols(d_projected, attn_weights)
-    d_attn_in = d_attn_in_part[:tok_rows] + swapped(
-        d_attn_in_part[tok_rows:].astype(bf16)
-    ).astype(jnp.float32)
+    d_attn_in_other = swapped(d_attn_in_part[tok_rows:].astype(bf16))
+    d_attn_in = d_attn_in_part[:tok_rows] + d_attn_in_other.astype(jnp.float32)
     normed = pack_tokens * lax.rsqrt(
         jnp.mean(pack_tokens * pack_tokens, axis=-1, keepdims=True) + eps_norm
     )
@@ -704,7 +698,7 @@
 
 def solution(mesh):
     return jax.shard_map(
-        on_device,
+        layer,
         mesh=mesh,
         in_specs=(
             P(("dp", "seq"), None),

time: 798 us -> 798 us (level)
  no operation moved by 1% of the time
where the time goes in v3:
time: 798 us; the launch traced here: 787 us
  Pallas kernels  450 us (56%)
  matrix products  126 us (16%)
  waiting for transfers between devices  109 us (14%)
  local copies, waits for them, and re-layouts  52.6 us (7%)
  other arithmetic  38.4 us (5%)
  starting transfers between devices  8.9 us (1%)
    pallas_call x3, Pallas kernels, gathered(): pl.pallas_call(functools.partial(gather_kernel, n_dp), out_shape=jax.Shap...  209 us
    pallas_call x2, Pallas kernels, scattered_piece(): pl.pallas_call(functools.partial(scatter_kernel, n_dp), out_shape=jax.Sha...  132 us
    pallas_call x1, Pallas kernels, scattered_products(): pl.pallas_call(functools.partial(product_kernel, n_dp), out_shape=jax.Sha...  109 us
    ppermute x8, waiting for transfers between devices, swapped(): return lax.ppermute(x, 'seq', [(0, 1), (1, 0)])  109 us
    dot_general x5, matrix products, contract_cols(): lax.dot_general(left_side, right_side, (((1,), (1,)), ((), ())), preferre...  41.5 us
    dot_general x3, matrix products, contract_rows(): lax.dot_general(left_side, right_side, (((0,), (0,)), ((), ())), preferre...  27.7 us
    unnamed x157, local copies, waits for them, and re-layouts  20.5 us
  transfers between devices with their start and end apart: 8, of which 4 were waited for; matrix products, arithmetic and copies ran while one was open for 8% of the time, Pallas kernels for 19%

profile of v3, /device:TPU:0, one launch (start us, length us, event | category | flops | bytes accessed | tf_op | source)
XLA Modules:
  0.0 787.2 jit_solution(11926975632253196305)
XLA Ops:
  10.1 8.3 %collective-permute-done.1 = bf16[72,3200]{1,0:T(8,128)(2,1)} collective-permute-done((bf16[72,3200]{1,0:T(8,128)(2,1)S(1)}, bf16[72,3200]{1,0:T(8,128)(2,1)}, u32[]{:S(2)}, u32[]{:S(2)}) %collective-permute-start.1) | collective-permute-done | bytes 460832 | tf_op jit(solution)/shard_map/ppermute | solution.py:99
  22.7 91.1 %shard_map.101 = bf16[16,144,3200]{2,1,0:T(8,128)(2,1)} custom-call(bf16[144,3200]{1,0:T(8,128)(2,1)} %pad_maximum_fusion.4.x_ref), custom_call_target="tpu_custom_call" | custom-call | bytes 150000000 | tf_op jit(solution)/shard_map/pallas_call | solution.py:242
  116.3 6.3 fusion.3
  129.5 4.0 fusion.13
  140.6 9.8 %collective-permute-done.2 = bf16[128,2304]{1,0:T(8,128)(2,1)S(1)} collective-permute-done((bf16[128,2304]{1,0:T(8,128)(2,1)}, bf16[128,2304]{1,0:T(8,128)(2,1)S(1)}, u32[]{:S(2)}, u32[]{:S(2)}) %collective-permute-start.2) | collective-permute-done | bytes 589856 | tf_op jit(solution)/shard_map/ppermute | solution.py:99
  153.9 57.7 %shard_map.102 = bf16[16,128,2304]{2,1,0:T(8,128)(2,1)} custom-call(bf16[128,2304]{1,0:T(8,128)(2,1)} %multiply_convert_fusion.2.x_ref), custom_call_target="tpu_custom_call" | custom-call | bytes 150000000 | tf_op jit(solution)/shard_map/pallas_call | solution.py:242
  211.6 4.5 constant_dynamic-update-slice_fusion
  216.1 9.2 %fusion.28 = f32[2048,576]{0,1:T(8,128)S(1)} fusion(bf16[2048,2304]{1,0:T(8,128)(2,1)} %bitcast.115, bf16[576,6912]{1,0:T(8,128)(2,1)} %constant_dynamic-update-slice_fusion), kind=kOutput, calls=%fused_computation.44 | convolution fusion | flops 5435817984 | bytes 16809984 | tf_op jit(solution)/shard_map/dot_general | solution.py:78
  225.3 8.0 %multiply_convert_fusion.1 = (bf16[2048,576]{0,1:T(8,128)(2,1)}, f32[2048,576]{0,1:T(8,128)}) fusion(f32[2048,576]{0,1:T(8,128)S(1)} %fusion.28, bf16[2048,2304]{1,0:T(8,128)(2,1)S(1)} %bitcast.119, bf16[576,6912]{1,0:T(8,128)(2,1)S(1)} %copy-done.23), kind=kOutput, calls=%fused_computation.19 | convolution fusion | flops 5447614464 | bytes 23887872 | tf_op jit(solution)/shard_map/dot_general | solution.py:78
  233.3 11.5 %convolution_convert_fusion = bf16[2048,2304]{1,0:T(8,128)(2,1)} fusion(bf16[2048,576]{0,1:T(8,128)(2,1)} %get-tuple-element.83, bf16[576,6912]{1,0:T(8,128)(2,1)S(1)} %copy-done.23), kind=kOutput, calls=%fused_computation.2 | convolution fusion | flops 5440536576 | bytes 14450688 | tf_op jit(solution)/shard_map/dot_general | solution.py:610
  244.9 67.1 %shard_map.103 = f32[128,2304]{1,0:T(8,128)} custom-call(bf16[16,128,2304]{2,1,0:T(8,128)(2,1)} %bitcast.126), custom_call_target="tpu_custom_call" | custom-call | bytes 150000000 | tf_op jit(solution)/shard_map/pallas_call | solution.py:498
  317.1 59.9 %shard_map.104 = bf16[16,128,2304]{2,1,0:T(8,128)(2,1)} custom-call(bf16[128,2304]{1,0:T(8,128)(2,1)} %get-tuple-element.47.x_ref), custom_call_target="tpu_custom_call" | custom-call | bytes 150000000 | tf_op jit(solution)/shard_map/pallas_call | solution.py:242
  377.1 11.7 %fusion.116 = f32[576,2304]{1,0:T(8,128)} fusion(bf16[2048,576]{0,1:T(8,128)(2,1)} %get-tuple-element.83, bf16[2048,2304]{1,0:T(8,128)(2,1)} %bitcast.123), kind=kOutput, calls=%fused_computation.217 | convolution fusion | flops 5435817984 | bytes 17104896 | tf_op jit(solution)/shard_map/dot_general | solution.py:72
  388.8 14.8 %fusion.8 = (bf16[2048,576]{0,1:T(8,128)(2,1)S(1)}, bf16[2048,576]{0,1:T(8,128)(2,1)S(1)}) fusion(f32[2048,576]{0,1:T(8,128)} %copy-done.58, f32[2048,576]{0,1:T(8,128)} %get-tuple-element.84, bf16[2048,2304]{1,0:T(8,128)(2,1)} %bitcast.124, bf16[576,6912]{1,0:T(8,128)(2,1)} %constant_dynamic-update-slice_fusion), kind=kOutput, calls=%fused_computation.15 | convolution fusion | flops 5468848128 | bytes 26247168 | tf_op jit(solution)/shard_map/dot_general | solution.py:78
  403.6 7.5 fusion.114
  411.2 13.2 %fusion.23 = f32[2048,2304]{1,0:T(8,128)} fusion(bf16[2048,576]{0,1:T(8,128)(2,1)S(1)} %get-tuple-element.42, bf16[576,6912]{1,0:T(8,128)(2,1)} %constant_dynamic-update-slice_fusion), kind=kOutput, calls=%fused_computation.39 | convolution fusion | flops 5435817984 | bytes 23887872 | tf_op jit(solution)/shard_map/dot_general | solution.py:622
  424.4 14.8 %add_convert_fusion = bf16[2048,2304]{1,0:T(8,128)(2,1)} fusion(f32[2048,2304]{1,0:T(8,128)} %fusion.23, bf16[2048,576]{0,1:T(8,128)(2,1)S(1)} %get-tuple-element.41, bf16[576,6912]{1,0:T(8,128)(2,1)} %constant_dynamic-update-slice_fusion), kind=kOutput, calls=%fused_computation.1 | convolution fusion | flops 5445255168 | bytes 33325056 | tf_op jit(solution)/shard_map/dot_general | solution.py:621
  439.2 64.9 %shard_map.105 = f32[128,2304]{1,0:T(8,128)} custom-call(bf16[16,128,2304]{2,1,0:T(8,128)(2,1)} %bitcast.125), custom_call_target="tpu_custom_call" | custom-call | bytes 150000000 | tf_op jit(solution)/shard_map/pallas_call | solution.py:498
  510.6 8.5 %fusion.115 = f32[576,2304]{1,0:T(8,128)S(1)} fusion(bf16[2048,576]{0,1:T(8,128)(2,1)S(1)} %copy-done.60, bf16[2048,2304]{1,0:T(8,128)(2,1)} %bitcast.116), kind=kOutput, calls=%fused_computation.216 | convolution fusion | flops 5435817984 | bytes 17104896 | tf_op jit(solution)/shard_map/dot_general | solution.py:72
  543.9 5.5 fusion.1
  561.3 109.1 %shard_map.106 = f32[144,3200]{1,0:T(8,128)} custom-call(bf16[16,144,256]{2,1,0:T(8,128)(2,1)} %bitcast.130, bf16[256,2048]{1,0:T(8,128)(2,1)} %pad_maximum_fusion.3.right_a, bf16[16,144,256]{2,1,0:T(8,128)(2,1)} %bitcast.129, bf16[256,1024]{1,0:T(8,128)(2,1)} %copy.103.right_b, bf16[16,144,128]{2,1,0:T(8,128)(2,1)} %bitcast.133), custom_call_target="tpu_custom_call" | custom-call | bytes 200000000 | tf_op jit(solution)/shard_map/pallas_call | solution.py:464
  679.3 6.1 collective-permute-done.6
  693.7 84.6 %collective-permute-done.5 = bf16[128,2304]{1,0:T(8,128)(2,1)S(1)} collective-permute-done((bf16[128,2304]{1,0:T(8,128)(2,1)}, bf16[128,2304]{1,0:T(8,128)(2,1)S(1)}, u32[]{:S(2)}, u32[]{:S(2)}) %collective-permute-start.5) | collective-permute-done | bytes 589856 | tf_op jit(solution)/shard_map/ppermute | solution.py:99
  781.3 5.6 maximum_add_fusion
  (272 shorter events, 101.2 us)
Async XLA Ops:
  3.9 14.6 %collective-permute-start.1 = (bf16[72,3200]{1,0:T(8,128)(2,1)S(1)}, bf16[72,3200]{1,0:T(8,128)(2,1)}, u32[]{:S(2)}, u32[]{:S(2)}) collective-permute-start(bf16[72,3200]{1,0:T(8,128)(2,1)S(1)} %fusion.78), channel_id=1, source_target_pairs={{0,1},{1,0},{2,3},{3,2},{4,5},{5,4},{6,7},{7,6},{8,9},{9,8},{10,11... | collective-permute-start | bytes 1382408 | tf_op jit(solution)/shard_map/ppermute | solution.py:99
  6.9 109.0 %collective-permute-start = (bf16[128,2304]{1,0:T(8,128)(2,1)S(1)}, bf16[128,2304]{1,0:T(8,128)(2,1)S(1)}, u32[]{:S(2)}, u32[]{:S(2)}) collective-permute-start(bf16[128,2304]{1,0:T(8,128)(2,1)S(1)} %copy-done.1), channel_id=1, source_target_pairs={{0,1},{1,0},{2,3},{3,2},{4,5},{5,4},{6,7},{7,6},{8,9},{9,8},{10,11... | collective-permute-start | bytes 1769480 | tf_op jit(solution)/shard_map/ppermute | solution.py:99
  8.4 12.1 %copy-start.25 = (f32[256,128]{1,0:T(8,128)}, f32[256,128]{1,0:T(8,128)S(1)}, u32[]{:S(2)}) copy-start(f32[256,128]{1,0:T(8,128)S(1)} %get-tuple-element.73) | copy-start | bytes 393220
  8.4 12.1 %copy-start.27 = (f32[256,128]{1,0:T(8,128)}, f32[256,128]{1,0:T(8,128)S(1)}, u32[]{:S(2)}) copy-start(f32[256,128]{1,0:T(8,128)S(1)} %get-tuple-element.74) | copy-start | bytes 393220
  10.1 118.3 %copy-start.30 = (pred[256,256]{0,1:T(8,128)(4,1)}, pred[256,256]{0,1:T(8,128)(4,1)S(1)}, u32[]{:S(2)}) copy-start(pred[256,256]{0,1:T(8,128)(4,1)S(1)} %fusion.79) | copy-start | bytes 196612
  18.5 193.1 %collective-permute-start.3 = (bf16[288,6912]{1,0:T(8,128)(2,1)}, bf16[288,6912]{1,0:T(8,128)(2,1)}, u32[]{:S(2)}, u32[]{:S(2)}) collective-permute-start(bf16[288,6912]{1,0:T(8,128)(2,1)} %param.9), channel_id=1, source_target_pairs={{0,1},{1,0},{2,3},{3,2},{4,5},{5,4},{6,7},{7,6},{8,9},{9,8},{10,11... | collective-permute-start | bytes 11943944 | tf_op jit(solution)/shard_map/ppermute | solution.py:99
  133.6 17.1 %copy-start.3 = (f32[256,2304]{1,0:T(8,128)}, f32[256,2304]{1,0:T(8,128)S(1)}, u32[]{:S(2)}) copy-start(f32[256,2304]{1,0:T(8,128)S(1)} %fusion.13) | copy-start | bytes 7077892
  134.5 15.8 %collective-permute-start.2 = (bf16[128,2304]{1,0:T(8,128)(2,1)}, bf16[128,2304]{1,0:T(8,128)(2,1)S(1)}, u32[]{:S(2)}, u32[]{:S(2)}) collective-permute-start(bf16[128,2304]{1,0:T(8,128)(2,1)} %slice.331), channel_id=1, source_target_pairs={{0,1},{1,0},{2,3},{3,2},{4,5},{5,4},{6,7},{7,6},{8,9},{9,8},{10,11... | collective-permute-start | bytes 1769480 | tf_op jit(solution)/shard_map/ppermute | solution.py:99
  140.6 12.3 %copy-start.40 = (f32[2304]{0:T(1024)S(1)}, f32[2304]{0:T(1024)}, u32[]{:S(2)}) copy-start(f32[2304]{0:T(1024)} %get-tuple-element.33) | copy-start | bytes 27652
  211.6 13.7 %slice-start.4 = ((s8[9437184]{0:T(1024)(128)(4,1)}), s8[4194304]{0:T(1024)(128)(4,1)S(1)}, s32[]{:S(2)}) async-start(s8[9437184]{0:T(1024)(128)(4,1)} %bitcast.117), calls=%async_computation.4 | async-start | bytes 8388608
  244.8 68.7 %copy-start.9 = (bf16[128,2304]{1,0:T(8,128)(2,1)S(1)}, bf16[128,2304]{1,0:T(8,128)(2,1)}, u32[]{:S(2)}) copy-start(bf16[128,2304]{1,0:T(8,128)(2,1)} %param.11) | copy-start | bytes 1769476
  244.8 68.7 %copy-start.46 = (f32[2304]{0:T(1024)S(1)}, f32[2304]{0:T(1024)}, u32[]{:S(2)}) copy-start(f32[2304]{0:T(1024)} %get-tuple-element.32) | copy-start | bytes 27652
  377.1 26.6 %slice-start.7 = ((s8[9437184]{0:T(1024)(128)(4,1)}), s8[4194304]{0:T(1024)(128)(4,1)S(1)}, s32[]{:S(2)}) async-start(s8[9437184]{0:T(1024)(128)(4,1)} %bitcast.120), calls=%async_computation.7 | async-start | bytes 8388608
  377.1 26.6 %slice-start.8 = ((s8[9437184]{0:T(1024)(128)(4,1)}), s8[4194304]{0:T(1024)(128)(4,1)S(1)}, s32[]{:S(2)}) async-start(s8[9437184]{0:T(1024)(128)(4,1)} %bitcast.120), calls=%async_computation.8 | async-start | bytes 8388608
  388.8 14.9 %slice-start.9 = ((s8[9437184]{0:T(1024)(128)(4,1)}), s8[1048576]{0:T(1024)(128)(4,1)S(1)}, s32[]{:S(2)}) async-start(s8[9437184]{0:T(1024)(128)(4,1)} %bitcast.120), calls=%async_computation.9 | async-start | bytes 2097152
  439.2 65.0 %copy-start.41 = (f32[2304]{0:T(1024)S(1)}, f32[2304]{0:T(1024)}, u32[]{:S(2)}) copy-start(f32[2304]{0:T(1024)} %get-tuple-element.33) | copy-start | bytes 27652
  508.3 10.8 %slice-start = ((s8[5308416]{0:T(1024)(128)(4,1)}), s8[4194304]{0:T(1024)(128)(4,1)S(1)}, s32[]{:S(2)}) async-start(s8[5308416]{0:T(1024)(128)(4,1)} %bitcast.113), calls=%async_computation | async-start | bytes 8388608
  509.3 19.8 %copy-start.20 = (bf16[128,2304]{1,0:T(8,128)(2,1)}, bf16[128,2304]{1,0:T(8,128)(2,1)S(1)}, u32[]{:S(2)}) copy-start(bf16[128,2304]{1,0:T(8,128)(2,1)S(1)} %fusion.44) | copy-start | bytes 1769476
  509.3 19.8 %collective-permute-start.4 = (bf16[128,2304]{1,0:T(8,128)(2,1)S(1)}, bf16[128,2304]{1,0:T(8,128)(2,1)S(1)}, u32[]{:S(2)}, u32[]{:S(2)}) collective-permute-start(bf16[128,2304]{1,0:T(8,128)(2,1)S(1)} %fusion.44), channel_id=1, source_target_pairs={{0,1},{1,0},{2,3},{3,2},{4,5},{5,4},{6,7},{7,6},{8,9},{9,8},{10,11... | collective-permute-start | bytes 1769480 | tf_op jit(solution)/shard_map/ppermute | solution.py:99
  671.9 13.5 %collective-permute-start.6 = (bf16[72,3200]{1,0:T(8,128)(2,1)S(1)}, bf16[72,3200]{1,0:T(8,128)(2,1)S(1)}, u32[]{:S(2)}, u32[]{:S(2)}) collective-permute-start(bf16[72,3200]{1,0:T(8,128)(2,1)S(1)} %select_convert_fusion), channel_id=1, source_target_pairs={{0,1},{1,0},{2,3},{3,2},{4,5},{5,4},{6,7},{7,6},{8,9},{9,8},{10,11... | collective-permute-start | bytes 1382408 | tf_op jit(solution)/shard_map/ppermute | solution.py:99
  672.7 12.7 %copy-start.5 = (f32[144,3200]{1,0:T(8,128)S(1)}, f32[144,3200]{1,0:T(8,128)}, u32[]{:S(2)}) copy-start(f32[144,3200]{1,0:T(8,128)} %shard_map.106) | copy-start | bytes 5529604
  676.4 103.7 %collective-permute-start.7 = (bf16[288,6912]{1,0:T(8,128)(2,1)}, bf16[288,6912]{1,0:T(8,128)(2,1)}, u32[]{:S(2)}, u32[]{:S(2)}) collective-permute-start(bf16[288,6912]{1,0:T(8,128)(2,1)} %pad_maximum_fusion), channel_id=1, source_target_pairs={{0,1},{1,0},{2,3},{3,2},{4,5},{5,4},{6,7},{7,6},{8,9},{9,8},{10,11... | collective-permute-start | bytes 11943944 | tf_op jit(solution)/shard_map/ppermute | solution.py:99
  678.6 99.7 %collective-permute-start.5 = (bf16[128,2304]{1,0:T(8,128)(2,1)}, bf16[128,2304]{1,0:T(8,128)(2,1)S(1)}, u32[]{:S(2)}, u32[]{:S(2)}) collective-permute-start(bf16[128,2304]{1,0:T(8,128)(2,1)} %slice.330), channel_id=1, source_target_pairs={{0,1},{1,0},{2,3},{3,2},{4,5},{5,4},{6,7},{7,6},{8,9},{9,8},{10,11... | collective-permute-start | bytes 1769480 | tf_op jit(solution)/shard_map/ppermute | solution.py:99
  690.2 88.5 %copy-start.7 = (f32[128,2304]{1,0:T(8,128)S(1)}, f32[128,2304]{1,0:T(8,128)}, u32[]{:S(2)}) copy-start(f32[128,2304]{1,0:T(8,128)} %copy-done.6) | copy-start | bytes 3538948
  (57 other events, 185.3 us)

commit v4 on v3

--- a/solution.py
+++ b/solution.py
@@ -258,7 +258,7 @@
     )(x)
 
 
-def scatter_steps(n_dp, place, produce, core_source, out_ref, from_core, from_pair, up_buf,
+def scatter_steps(n_dp, place, prepare, produce, core_source, out_ref, from_core, from_pair, up_buf,
                   down_buf, pair_out, core_send, core_recv, pair_send, pair_recv, up_send,
                   up_recv, down_send, down_recv):
     line = n_dp // 4
@@ -323,8 +323,9 @@
         produce(block, None, core_source(block))
         core_copy(block).start()
 
+    prepare(1 - b, 1 - c)
     each_target(lambda to, way: send_core(number(to, 1 - b, 1 - c)))
-    each_target(lambda to, way: send_core(number(to, b, 1 - c)))
+    prepare(1 - b, c)
 
     def send_pair(to, way):
         block = number(to, 1 - b, c)
@@ -333,6 +334,9 @@
         pair_copy(to).start()
 
     each_target(send_pair)
+    prepare(b, 1 - c)
+    each_target(lambda to, way: send_core(number(to, b, 1 - c)))
+    prepare(b, c)
 
     def line_sum(to, more, dst):
         block = number(to, b, c)
@@ -398,23 +402,46 @@
     lax.fori_loop(0, out_ref.shape[0] // tile, step, 0)
 
 
-def scatter_kernel(n_dp, p_ref, out_ref, *scratch):
+def dots_kernel(n_dp, n_terms, *refs):
+    lefts, rights = refs[:n_terms], refs[n_terms : 2 * n_terms]
+    out_ref, parts, *scratch = refs[2 * n_terms :]
+    _, rows, cols = parts.shape
+    f32 = jnp.float32
+
+    def prepare(b, c):
+        for first in range(0, n_dp // 4, 4):
+            blocks = [number(first + i, b, c) for i in range(4)]
+
+            def step(j, _):
+                at = pl.ds(pl.multiple_of(j * 256, 256), 256)
+                total = jnp.zeros((4 * rows, 256), f32)
+                for left, right in zip(lefts, rights):
+                    stacked = jnp.concatenate([left[k] for k in blocks], axis=0)
+                    total += jnp.dot(stacked, right[:, at], preferred_element_type=f32)
+                for i, k in enumerate(blocks):
+                    parts[k, :, at] = total[i * rows : (i + 1) * rows].astype(parts.dtype)
+                return 0
+
+            lax.fori_loop(0, cols // 256, step, 0)
+
     def produce(block, terms, dst):
         if terms is None:
             return
-        tile = row_tiles(p_ref.shape[1])
+        tile = row_tiles(rows)
 
         def step(i, _):
             at = pl.ds(pl.multiple_of(i * tile, tile), tile)
-            total = p_ref[block, at, :].astype(jnp.float32)
+            total = parts[block, at, :].astype(f32)
             for term in terms:
-                total += term[at, :].astype(jnp.float32)
+                total += term[at, :].astype(f32)
             dst[at, :] = total.astype(dst.dtype)
             return 0
 
-        lax.fori_loop(0, p_ref.shape[1] // tile, step, 0)
-
-    scatter_steps(n_dp, place_of(), produce, lambda block: p_ref.at[block], out_ref, *scratch)
+        lax.fori_loop(0, rows // tile, step, 0)
+
+    scatter_steps(
+        n_dp, place_of(), prepare, produce, lambda block: parts.at[block], out_ref, *scratch
+    )
 
 
 def product_kernel(n_dp, left_a, right_a, left_b, right_b, extra, out_ref, core_out, *scratch):
@@ -444,7 +471,13 @@
         dst[:, last] = total.astype(dst.dtype)
 
     scatter_steps(
-        n_dp, place_of(), produce, lambda block: core_out.at[block // 2], out_ref, *scratch
+        n_dp,
+        place_of(),
+        lambda b, c: None,
+        produce,
+        lambda block: core_out.at[block // 2],
+        out_ref,
+        *scratch,
     )
 
 
@@ -477,37 +510,42 @@
     )(left_a, right_a, left_b, right_b, extra)
 
 
-def scattered(parts, collective_id):
-    n_dp, rows, cols = parts.shape
+def scattered_dots(lefts, rights, collective_id):
+    n_dp, rows, _ = lefts[0].shape
+    cols = rights[0].shape[1]
     held = n_dp * (1 + 1 / 2 + 1) * rows * cols * 2
     pieces = 1
-    while held > pieces * 50 * 2**20 or cols % (128 * pieces):
+    while held > pieces * 36 * 2**20 or cols % (256 * pieces):
         pieces += 1
     width = cols // pieces
     return jnp.concatenate(
         [
-            scattered_piece(parts[:, :, i * width : (i + 1) * width], collective_id)
+            scattered_piece(
+                lefts, [r[:, i * width : (i + 1) * width] for r in rights], collective_id
+            )
             for i in range(pieces)
         ],
         axis=1,
     )
 
 
-def scattered_piece(parts, collective_id):
-    n_dp, rows, cols = parts.shape
+def scattered_piece(lefts, rights, collective_id):
+    n_dp, rows, _ = lefts[0].shape
+    cols = rights[0].shape[1]
     return pl.pallas_call(
-        functools.partial(scatter_kernel, n_dp),
+        functools.partial(dots_kernel, n_dp, len(lefts)),
         out_shape=jax.ShapeDtypeStruct((rows, cols), jnp.float32),
-        in_specs=[pl.BlockSpec(memory_space=pltpu.VMEM)],
+        in_specs=[pl.BlockSpec(memory_space=pltpu.VMEM)] * (2 * len(lefts)),
         out_specs=pl.BlockSpec(memory_space=pltpu.VMEM),
-        scratch_shapes=scatter_scratch(n_dp, rows, cols, parts.dtype),
+        scratch_shapes=[pltpu.VMEM((n_dp, rows, cols), jnp.bfloat16)]
+        + scatter_scratch(n_dp, rows, cols, jnp.bfloat16),
         compiler_params=pltpu.CompilerParams(
             collective_id=collective_id, has_side_effects=True
         ),
         cost_estimate=pl.CostEstimate(
             flops=0, bytes_accessed=150_000_000, transcendentals=0
         ),
-    )(parts)
+    )(*lefts, *rights)
 
 
 def mine_and_other(halves, seq_index):
@@ -592,23 +630,21 @@
     )
     mixed_heads = mixed_heads.reshape(pack, q_cols).astype(bf16)
     attn_part_out = contract_cols(mixed_heads, out_weights)
-    attn_out = attn_part_out[:tok_rows] + swapped(attn_part_out[tok_rows:].astype(bf16)).astype(
-        jnp.float32
-    )
+    attn_part_other = swapped(attn_part_out[tok_rows:].astype(bf16))
+    attn_out = attn_part_out[:tok_rows] + attn_part_other.astype(jnp.float32)
     middle = tokens_f + rms_norm(attn_out, gain_vals[1])
     ffn_input = rms_norm(middle, gain_vals[2]).astype(bf16)
 
-    unit_weights = jnp.concatenate([ffn_own, ffn_other], axis=0)
-    unit_count = unit_weights.shape[0]
-    gate_weights = unit_weights[:, :D]
-    up_weights = unit_weights[:, D : 2 * D]
-    down_weights = unit_weights[:, 2 * D :]
+    gate_weights, up_weights, down_weights = [
+        jnp.concatenate([ffn_own[:, k * D : (k + 1) * D], ffn_other[:, k * D : (k + 1) * D]])
+        for k in range(3)
+    ]
+    unit_count = gate_weights.shape[0]
     ffn_all = gathered(ffn_input, n_dp, 1).reshape(-1, D)
     gate = contract_cols(ffn_all, gate_weights)
     up = contract_cols(ffn_all, up_weights)
     hidden = gated_gelu(gate, up).astype(bf16)
-    ffn_parts = jnp.dot(hidden, down_weights, preferred_element_type=jnp.float32).astype(bf16)
-    ffn_out = scattered(ffn_parts.reshape(n_dp, tok_rows, D), 2)
+    ffn_out = scattered_dots([hidden.reshape(n_dp, tok_rows, -1)], [down_weights], 2)
     out_gain = gain_vals[3]
     block_out = (middle + rms_norm(ffn_out, out_gain)).astype(bf16)
     cotangent = out_grad.astype(jnp.float32)
@@ -617,11 +653,11 @@
     d_hidden = contract_cols(d_ffn_all, down_weights)
     d_gate, d_up = jax.vjp(gated_gelu, gate, up)[1](d_hidden)
     d_gate, d_up = d_gate.astype(bf16), d_up.astype(bf16)
-    d_parts = (
-        jnp.dot(d_gate, gate_weights, preferred_element_type=jnp.float32)
-        + jnp.dot(d_up, up_weights, preferred_element_type=jnp.float32)
-    ).astype(bf16)
-    d_ffn_input = scattered(d_parts.reshape(n_dp, tok_rows, D), 2)
+    d_ffn_input = scattered_dots(
+        [d_gate.reshape(n_dp, tok_rows, -1), d_up.reshape(n_dp, tok_rows, -1)],
+        [gate_weights, up_weights],
+        4,
+    )
 
     own_units = unit_count // 2
     weight_sum = [

time: 798 us -> 847 us (1.061)
  waiting for transfers between devices: 109 us -> 172 us
  matrix products: 126 us -> 91.7 us
  local copies, waits for them, and re-layouts: 52.6 us -> 64.4 us
    ppermute x8, waiting for transfers between devices: 109 us -> 172 us  [swapped(): return lax.ppermute(x, 'seq', [(0, 1), (1, 0)])]
    dot_general x3 -> x0, matrix products: 39.5 us -> none  [the longest x1 14.8 us: layer(): jnp.dot(d_gate, gate_weights, preferred_element_type=jnp.float32)]
    convert_element_type x0 -> x3, local copies, waits for them, and re-layouts: none -> 13.1 us  [the longest x2 8.68 us: layer(): d_gate, d_up = (d_gate.astype(bf16), d_up.astype(bf16))]
    pallas_call x2, Pallas kernels: 132 us -> 142 us  [scattered_piece(): pl.pallas_call(functools.partial(dots_kernel, n_dp, len(lefts)), out_shap...]
    unnamed x157 -> x154, local copies, waits for them, and re-layouts: 20.5 us -> 17.6 us
  transfers between devices with their start and end apart: 8 -> 8, of which waited for: 4 -> 4; matrix products, arithmetic and copies ran while one was open for 8% -> 7% of each run, Pallas kernels for 19% -> 18%
where the time goes in v4:
time: 847 us; the launch traced here: 837 us
  Pallas kernels  451 us (53%)
  waiting for transfers between devices  172 us (20%)
  matrix products  91.7 us (11%)
  local copies, waits for them, and re-layouts  64.4 us (8%)
  other arithmetic  45.3 us (5%)
  starting transfers between devices  10.4 us (1%)
    pallas_call x3, Pallas kernels, gathered(): pl.pallas_call(functools.partial(gather_kernel, n_dp), out_shape=jax.Shap...  208 us
    ppermute x8, waiting for transfers between devices, swapped(): return lax.ppermute(x, 'seq', [(0, 1), (1, 0)])  172 us
    pallas_call x2, Pallas kernels, scattered_piece(): pl.pallas_call(functools.partial(dots_kernel, n_dp, len(lefts)), out_shap...  142 us
    pallas_call x1, Pallas kernels, scattered_products(): pl.pallas_call(functools.partial(product_kernel, n_dp), out_shape=jax.Sha...  101 us
    dot_general x5, matrix products, contract_cols(): lax.dot_general(left_side, right_side, (((1,), (1,)), ((), ())), preferre...  42.4 us
    dot_general x3, matrix products, contract_rows(): lax.dot_general(left_side, right_side, (((0,), (0,)), ((), ())), preferre...  31.3 us
    unnamed x154, local copies, waits for them, and re-layouts  17.6 us
  transfers between devices with their start and end apart: 8, of which 4 were waited for; matrix products, arithmetic and copies ran while one was open for 7% of the time, Pallas kernels for 18%

profile of v4, /device:TPU:0, one launch (start us, length us, event | category | flops | bytes accessed | tf_op | source)
XLA Modules:
  0.0 837.1 jit_solution(14426513673141582350)
XLA Ops:
  10.1 8.2 collective-permute-done.1
  19.5 91.6 %shard_map.101 = bf16[16,144,3200]{2,1,0:T(8,128)(2,1)} custom-call(bf16[144,3200]{1,0:T(8,128)(2,1)} %pad_maximum_fusion.7.x_ref), custom_call_target="tpu_custom_call" | custom-call | bytes 150000000 | tf_op jit(solution)/shard_map/pallas_call | solution.py:242
  115.8 6.3 fusion.3
  128.7 4.0 fusion.13
  139.6 74.3 %collective-permute-done.2 = bf16[128,2304]{1,0:T(8,128)(2,1)S(1)} collective-permute-done((bf16[128,2304]{1,0:T(8,128)(2,1)}, bf16[128,2304]{1,0:T(8,128)(2,1)S(1)}, u32[]{:S(2)}, u32[]{:S(2)}) %collective-permute-start.2) | collective-permute-done | bytes 589856 | tf_op jit(solution)/shard_map/ppermute | solution.py:99
  217.4 57.7 %shard_map.102 = bf16[16,128,2304]{2,1,0:T(8,128)(2,1)} custom-call(bf16[128,2304]{1,0:T(8,128)(2,1)} %multiply_convert_fusion.2.x_ref), custom_call_target="tpu_custom_call" | custom-call | bytes 150000000 | tf_op jit(solution)/shard_map/pallas_call | solution.py:242
  278.7 8.4 %fusion.102 = f32[2048,576]{0,1:T(8,128)S(1)} fusion(bf16[2048,2304]{1,0:T(8,128)(2,1)} %bitcast.118, bf16[288,2304]{1,0:T(8,128)(2,1)S(1)} %get-tuple-element.48, bf16[288,2304]{1,0:T(8,128)(2,1)S(1)} %copy-done.12), kind=kOutput, calls=%fused_computation.202 | convolution fusion | flops 5441126400 | bytes 16809984 | tf_op jit(solution)/shard_map/dot_general | solution.py:78
  291.0 8.3 multiply_convert_fusion.1
  299.2 4.4 copy.78
  307.1 69.6 %shard_map.103 = f32[128,2304]{1,0:T(8,128)} custom-call(bf16[16,128,576]{2,1,0:T(8,128)(2,1)} %bitcast.115, bf16[576,2304]{1,0:T(8,128)(2,1)} %pad_maximum_fusion.3.refs_1_), custom_call_target="tpu_custom_call" | custom-call | bytes 150000000 | tf_op jit(solution)/shard_map/pallas_call | solution.py:535
  381.8 59.0 %shard_map.104 = bf16[16,128,2304]{2,1,0:T(8,128)(2,1)} custom-call(bf16[128,2304]{1,0:T(8,128)(2,1)} %get-tuple-element.53.x_ref), custom_call_target="tpu_custom_call" | custom-call | bytes 150000000 | tf_op jit(solution)/shard_map/pallas_call | solution.py:242
  440.9 11.5 %fusion.111 = f32[576,2304]{1,0:T(8,128)} fusion(bf16[2048,576]{0,1:T(8,128)(2,1)} %get-tuple-element.89, bf16[2048,2304]{1,0:T(8,128)(2,1)} %bitcast.124), kind=kOutput, calls=%fused_computation.211 | convolution fusion | flops 5435817984 | bytes 17104896 | tf_op jit(solution)/shard_map/dot_general | solution.py:72
  452.4 16.3 %multiply_convert_fusion = (bf16[2048,576]{0,1:T(8,128)(2,1)}, bf16[2048,576]{0,1:T(8,128)(2,1)}) fusion(f32[2048,576]{0,1:T(8,128)} %copy-done.62, f32[2048,576]{0,1:T(8,128)} %get-tuple-element.90, bf16[2048,2304]{1,0:T(8,128)(2,1)S(1)} %bitcast.125, bf16[288,2304]{1,0:T(8,128)(2,1)S(1)} %copy-done.10, bf16[288,2304]{1,0:T(8,128)(2,1)S(1)} %copy-done.9), kind=kOutput, calls=%fused_computation.16 | convolution fusion | flops 5474156544 | bytes 26247168 | tf_op jit(solution)/shard_map/dot_general | solution.py:78
  468.6 4.3 copy.80
  473.0 11.5 %fusion.110 = f32[576,2304]{1,0:T(8,128)} fusion(bf16[2048,576]{0,1:T(8,128)(2,1)} %get-tuple-element.41, bf16[2048,2304]{1,0:T(8,128)(2,1)} %bitcast.119), kind=kOutput, calls=%fused_computation.210 | convolution fusion | flops 5435817984 | bytes 17104896 | tf_op jit(solution)/shard_map/dot_general | solution.py:72
  484.5 4.3 copy.79
  488.8 72.3 %shard_map.105 = f32[128,2304]{1,0:T(8,128)} custom-call(bf16[16,128,576]{2,1,0:T(8,128)(2,1)} %bitcast.117, bf16[16,128,576]{2,1,0:T(8,128)(2,1)} %bitcast.116, bf16[576,2304]{1,0:T(8,128)(2,1)} %get-tuple-element.93.refs_2_, bf16[576,2304]{1,0:T(8,128)(2,1)} %get-tuple-element.94.refs_3_), custom_call_target="tpu_custom_call" | custom-call | bytes 150000000 | tf_op jit(solution)/shard_map/pallas_call | solution.py:535
  567.8 8.3 fusion.109
  585.8 3.7 fusion.26
  600.8 5.5 fusion.1
  619.5 100.8 %shard_map.106 = f32[144,3200]{1,0:T(8,128)} custom-call(bf16[16,144,256]{2,1,0:T(8,128)(2,1)} %bitcast.128, bf16[256,2048]{1,0:T(8,128)(2,1)} %pad_maximum_fusion.6.right_a, bf16[16,144,256]{2,1,0:T(8,128)(2,1)} %bitcast.129, bf16[256,1024]{1,0:T(8,128)(2,1)} %copy.112.right_b, bf16[16,144,128]{2,1,0:T(8,128)(2,1)} %bitcast.130), custom_call_target="tpu_custom_call" | custom-call | bytes 200000000 | tf_op jit(solution)/shard_map/pallas_call | solution.py:497
  730.1 5.2 collective-permute-done.6
  743.6 84.6 %collective-permute-done.5 = bf16[128,2304]{1,0:T(8,128)(2,1)S(1)} collective-permute-done((bf16[128,2304]{1,0:T(8,128)(2,1)}, bf16[128,2304]{1,0:T(8,128)(2,1)S(1)}, u32[]{:S(2)}, u32[]{:S(2)}) %collective-permute-start.5) | collective-permute-done | bytes 589856 | tf_op jit(solution)/shard_map/ppermute | solution.py:99
  831.3 5.6 maximum_add_fusion
  (272 shorter events, 109.3 us)
Async XLA Ops:
  3.9 14.4 %collective-permute-start.1 = (bf16[72,3200]{1,0:T(8,128)(2,1)S(1)}, bf16[72,3200]{1,0:T(8,128)(2,1)S(1)}, u32[]{:S(2)}, u32[]{:S(2)}) collective-permute-start(bf16[72,3200]{1,0:T(8,128)(2,1)S(1)} %fusion.68), channel_id=1, source_target_pairs={{0,1},{1,0},{2,3},{3,2},{4,5},{5,4},{6,7},{7,6},{8,9},{9,8},{10,11... | collective-permute-start | bytes 1382408 | tf_op jit(solution)/shard_map/ppermute | solution.py:99
  6.9 107.9 %collective-permute-start = (bf16[128,2304]{1,0:T(8,128)(2,1)S(1)}, bf16[128,2304]{1,0:T(8,128)(2,1)S(1)}, u32[]{:S(2)}, u32[]{:S(2)}) collective-permute-start(bf16[128,2304]{1,0:T(8,128)(2,1)S(1)} %copy-done.1), channel_id=1, source_target_pairs={{0,1},{1,0},{2,3},{3,2},{4,5},{5,4},{6,7},{7,6},{8,9},{9,8},{10,11... | collective-permute-start | bytes 1769480 | tf_op jit(solution)/shard_map/ppermute | solution.py:99
  8.4 102.7 %copy-start.29 = (f32[256,128]{1,0:T(8,128)}, f32[256,128]{1,0:T(8,128)S(1)}, u32[]{:S(2)}) copy-start(f32[256,128]{1,0:T(8,128)S(1)} %get-tuple-element.79) | copy-start | bytes 393220
  8.4 102.7 %copy-start.31 = (f32[256,128]{1,0:T(8,128)}, f32[256,128]{1,0:T(8,128)S(1)}, u32[]{:S(2)}) copy-start(f32[256,128]{1,0:T(8,128)S(1)} %get-tuple-element.80) | copy-start | bytes 393220
  10.1 117.4 %copy-start.36 = (pred[256,256]{0,1:T(8,128)(4,1)}, pred[256,256]{0,1:T(8,128)(4,1)S(1)}, u32[]{:S(2)}) copy-start(pred[256,256]{0,1:T(8,128)(4,1)S(1)} %fusion.69) | copy-start | bytes 196612
  112.7 162.5 %collective-permute-start.3 = (bf16[288,6912]{1,0:T(8,128)(2,1)}, bf16[288,6912]{1,0:T(8,128)(2,1)}, u32[]{:S(2)}, u32[]{:S(2)}) collective-permute-start(bf16[288,6912]{1,0:T(8,128)(2,1)} %param.9), channel_id=1, source_target_pairs={{0,1},{1,0},{2,3},{3,2},{4,5},{5,4},{6,7},{7,6},{8,9},{9,8},{10,11... | collective-permute-start | bytes 11943944 | tf_op jit(solution)/shard_map/ppermute | solution.py:99
  132.7 81.4 %copy-start.2 = (f32[256,2304]{1,0:T(8,128)}, f32[256,2304]{1,0:T(8,128)S(1)}, u32[]{:S(2)}) copy-start(f32[256,2304]{1,0:T(8,128)S(1)} %fusion.13) | copy-start | bytes 7077892
  133.7 80.2 %collective-permute-start.2 = (bf16[128,2304]{1,0:T(8,128)(2,1)}, bf16[128,2304]{1,0:T(8,128)(2,1)S(1)}, u32[]{:S(2)}, u32[]{:S(2)}) collective-permute-start(bf16[128,2304]{1,0:T(8,128)(2,1)} %slice.331), channel_id=1, source_target_pairs={{0,1},{1,0},{2,3},{3,2},{4,5},{5,4},{6,7},{7,6},{8,9},{9,8},{10,11... | collective-permute-start | bytes 1769480 | tf_op jit(solution)/shard_map/ppermute | solution.py:99
  139.6 76.8 %copy-start.43 = (f32[2304]{0:T(1024)S(1)}, f32[2304]{0:T(1024)}, u32[]{:S(2)}) copy-start(f32[2304]{0:T(1024)} %get-tuple-element.33) | copy-start | bytes 27652
  275.1 15.8 %slice-start.6 = ((s8[9437184]{0:T(1024)(128)(4,1)}), s8[4194304]{0:T(1024)(128)(4,1)S(1)}, s32[]{:S(2)}) async-start(s8[9437184]{0:T(1024)(128)(4,1)} %bitcast.121), calls=%async_computation.6 | async-start | bytes 8388608
  278.7 12.2 %slice-start.7 = ((s8[9437184]{0:T(1024)(128)(4,1)}), s8[4194304]{0:T(1024)(128)(4,1)S(1)}, s32[]{:S(2)}) async-start(s8[9437184]{0:T(1024)(128)(4,1)} %bitcast.121), calls=%async_computation.7 | async-start | bytes 8388608
  278.7 12.2 %slice-start.8 = ((s8[9437184]{0:T(1024)(128)(4,1)}), s8[1048576]{0:T(1024)(128)(4,1)S(1)}, s32[]{:S(2)}) async-start(s8[9437184]{0:T(1024)(128)(4,1)} %bitcast.121), calls=%async_computation.8 | async-start | bytes 2097152
  307.1 71.1 %copy-start.8 = (bf16[128,2304]{1,0:T(8,128)(2,1)S(1)}, bf16[128,2304]{1,0:T(8,128)(2,1)}, u32[]{:S(2)}) copy-start(bf16[128,2304]{1,0:T(8,128)(2,1)} %param.11) | copy-start | bytes 1769476
  307.1 71.2 %copy-start.49 = (f32[2304]{0:T(1024)S(1)}, f32[2304]{0:T(1024)}, u32[]{:S(2)}) copy-start(f32[2304]{0:T(1024)} %get-tuple-element.32) | copy-start | bytes 27652
  440.8 11.5 %copy-start.7 = (bf16[16,128,2304]{2,1,0:T(8,128)(2,1)S(1)}, bf16[16,128,2304]{2,1,0:T(8,128)(2,1)}, u32[]{:S(2)}) copy-start(bf16[16,128,2304]{2,1,0:T(8,128)(2,1)} %shard_map.104) | copy-start | bytes 28311556
  440.8 11.5 %copy-start.9 = (bf16[288,2304]{1,0:T(8,128)(2,1)S(1)}, bf16[288,2304]{1,0:T(8,128)(2,1)}, u32[]{:S(2)}) copy-start(bf16[288,2304]{1,0:T(8,128)(2,1)} %get-tuple-element.43) | copy-start | bytes 3981316
  488.8 72.4 %copy-start.44 = (f32[2304]{0:T(1024)S(1)}, f32[2304]{0:T(1024)}, u32[]{:S(2)}) copy-start(f32[2304]{0:T(1024)} %get-tuple-element.33) | copy-start | bytes 27652
  566.3 18.7 %copy-start.24 = (bf16[128,2304]{1,0:T(8,128)(2,1)}, bf16[128,2304]{1,0:T(8,128)(2,1)S(1)}, u32[]{:S(2)}) copy-start(bf16[128,2304]{1,0:T(8,128)(2,1)S(1)} %fusion.34) | copy-start | bytes 1769476
  566.3 18.7 %collective-permute-start.4 = (bf16[128,2304]{1,0:T(8,128)(2,1)S(1)}, bf16[128,2304]{1,0:T(8,128)(2,1)S(1)}, u32[]{:S(2)}, u32[]{:S(2)}) collective-permute-start(bf16[128,2304]{1,0:T(8,128)(2,1)S(1)} %fusion.34), channel_id=1, source_target_pairs={{0,1},{1,0},{2,3},{3,2},{4,5},{5,4},{6,7},{7,6},{8,9},{9,8},{10,11... | collective-permute-start | bytes 1769480 | tf_op jit(solution)/shard_map/ppermute | solution.py:99
  721.9 13.5 %collective-permute-start.6 = (bf16[72,3200]{1,0:T(8,128)(2,1)S(1)}, bf16[72,3200]{1,0:T(8,128)(2,1)S(1)}, u32[]{:S(2)}, u32[]{:S(2)}) collective-permute-start(bf16[72,3200]{1,0:T(8,128)(2,1)S(1)} %select_convert_fusion), channel_id=1, source_target_pairs={{0,1},{1,0},{2,3},{3,2},{4,5},{5,4},{6,7},{7,6},{8,9},{9,8},{10,11... | collective-permute-start | bytes 1382408 | tf_op jit(solution)/shard_map/ppermute | solution.py:99
  723.5 11.8 %copy-start.4 = (f32[144,3200]{1,0:T(8,128)S(1)}, f32[144,3200]{1,0:T(8,128)}, u32[]{:S(2)}) copy-start(f32[144,3200]{1,0:T(8,128)} %shard_map.106) | copy-start | bytes 5529604
  727.2 102.9 %collective-permute-start.7 = (bf16[288,6912]{1,0:T(8,128)(2,1)}, bf16[288,6912]{1,0:T(8,128)(2,1)}, u32[]{:S(2)}, u32[]{:S(2)}) collective-permute-start(bf16[288,6912]{1,0:T(8,128)(2,1)} %pad_maximum_fusion), channel_id=1, source_target_pairs={{0,1},{1,0},{2,3},{3,2},{4,5},{5,4},{6,7},{7,6},{8,9},{9,8},{10,11... | collective-permute-start | bytes 11943944 | tf_op jit(solution)/shard_map/ppermute | solution.py:99
  728.5 99.7 %collective-permute-start.5 = (bf16[128,2304]{1,0:T(8,128)(2,1)}, bf16[128,2304]{1,0:T(8,128)(2,1)S(1)}, u32[]{:S(2)}, u32[]{:S(2)}) collective-permute-start(bf16[128,2304]{1,0:T(8,128)(2,1)} %slice.330), channel_id=1, source_target_pairs={{0,1},{1,0},{2,3},{3,2},{4,5},{5,4},{6,7},{7,6},{8,9},{9,8},{10,11... | collective-permute-start | bytes 1769480 | tf_op jit(solution)/shard_map/ppermute | solution.py:99
  740.1 88.5 %copy-start.6 = (f32[128,2304]{1,0:T(8,128)S(1)}, f32[128,2304]{1,0:T(8,128)}, u32[]{:S(2)}) copy-start(f32[128,2304]{1,0:T(8,128)} %copy-done.5) | copy-start | bytes 3538948
  (57 other events, 164.7 us)

commit v5 on v4

--- a/solution.py
+++ b/solution.py
@@ -4,6 +4,7 @@
 import jax
 import jax.numpy as jnp
 from jax import lax
+from jax.experimental.layout import Layout, with_layout_constraint
 from jax.experimental import pallas as pl
 from jax.experimental.pallas import tpu as pltpu
 from jax.sharding import PartitionSpec as P
@@ -546,6 +547,10 @@
             flops=0, bytes_accessed=150_000_000, transcendentals=0
         ),
     )(*lefts, *rights)
+
+
+def row_major(x):
+    return with_layout_constraint(x, Layout(major_to_minor=(0, 1)))
 
 
 def mine_and_other(halves, seq_index):
@@ -643,7 +648,7 @@
     ffn_all = gathered(ffn_input, n_dp, 1).reshape(-1, D)
     gate = contract_cols(ffn_all, gate_weights)
     up = contract_cols(ffn_all, up_weights)
-    hidden = gated_gelu(gate, up).astype(bf16)
+    hidden = row_major(gated_gelu(gate, up).astype(bf16))
     ffn_out = scattered_dots([hidden.reshape(n_dp, tok_rows, -1)], [down_weights], 2)
     out_gain = gain_vals[3]
     block_out = (middle + rms_norm(ffn_out, out_gain)).astype(bf16)
@@ -652,7 +657,7 @@
     d_ffn_all = gathered(d_ffn_f.astype(bf16), n_dp, 1).reshape(-1, D)
     d_hidden = contract_cols(d_ffn_all, down_weights)
     d_gate, d_up = jax.vjp(gated_gelu, gate, up)[1](d_hidden)
-    d_gate, d_up = d_gate.astype(bf16), d_up.astype(bf16)
+    d_gate, d_up = row_major(d_gate.astype(bf16)), row_major(d_up.astype(bf16))
     d_ffn_input = scattered_dots(
         [d_gate.reshape(n_dp, tok_rows, -1), d_up.reshape(n_dp, tok_rows, -1)],
         [gate_weights, up_weights],

time: 847 us -> 837 us (0.988)
  local copies, waits for them, and re-layouts: 64.4 us -> 49.2 us
    convert_element_type x3 -> x0, local copies, waits for them, and re-layouts: 13.1 us -> none  [the longest x2 8.68 us: layer(): d_gate, d_up = (d_gate.astype(bf16), d_up.astype(bf16))]
    dot_general x5, matrix products: 42.4 us -> 50.9 us  [contract_cols(): lax.dot_general(left_side, right_side, (((1,), (1,)), ((), ())), preferre...]
    unnamed x154 -> x160, local copies, waits for them, and re-layouts: 17.6 us -> 16.6 us
where the time goes in v5:
time: 837 us; the launch traced here: 828 us
  Pallas kernels  451 us (54%)
  waiting for transfers between devices  172 us (21%)
  matrix products  98.9 us (12%)
  local copies, waits for them, and re-layouts  49.2 us (6%)
  other arithmetic  43.4 us (5%)
  starting transfers between devices  10.2 us (1%)
    pallas_call x3, Pallas kernels, gathered(): pl.pallas_call(functools.partial(gather_kernel, n_dp), out_shape=jax.Shap...  208 us
    ppermute x8, waiting for transfers between devices, swapped(): return lax.ppermute(x, 'seq', [(0, 1), (1, 0)])  172 us
    pallas_call x2, Pallas kernels, scattered_piece(): pl.pallas_call(functools.partial(dots_kernel, n_dp, len(lefts)), out_shap...  142 us
    pallas_call x1, Pallas kernels, scattered_products(): pl.pallas_call(functools.partial(product_kernel, n_dp), out_shape=jax.Sha...  101 us
    dot_general x5, matrix products, contract_cols(): lax.dot_general(left_side, right_side, (((1,), (1,)), ((), ())), preferre...  50.9 us
    dot_general x3, matrix products, contract_rows(): lax.dot_general(left_side, right_side, (((0,), (0,)), ((), ())), preferre...  30 us
  transfers between devices with their start and end apart: 8, of which 4 were waited for; matrix products, arithmetic and copies ran while one was open for 7% of the time, Pallas kernels for 18%

profile of v5, /device:TPU:0, one launch (start us, length us, event | category | flops | bytes accessed | tf_op | source)
XLA Modules:
  0.0 827.7 jit_solution(15378591994878779097)
XLA Ops:
  3.9 3.0 collective-permute-start.1
  10.2 8.2 collective-permute-done.1
  19.5 91.6 %shard_map.101 = bf16[16,144,3200]{2,1,0:T(8,128)(2,1)} custom-call(bf16[144,3200]{1,0:T(8,128)(2,1)} %pad_maximum_fusion.7.x_ref), custom_call_target="tpu_custom_call" | custom-call | bytes 150000000 | tf_op jit(solution)/shard_map/pallas_call | solution.py:243
  115.8 6.3 fusion.3
  128.6 4.0 fusion.13
  139.6 74.2 %collective-permute-done.2 = bf16[128,2304]{1,0:T(8,128)(2,1)S(1)} collective-permute-done((bf16[128,2304]{1,0:T(8,128)(2,1)}, bf16[128,2304]{1,0:T(8,128)(2,1)S(1)}, u32[]{:S(2)}, u32[]{:S(2)}) %collective-permute-start.2) | collective-permute-done | bytes 589856 | tf_op jit(solution)/shard_map/ppermute | solution.py:100
  217.3 57.7 %shard_map.102 = bf16[16,128,2304]{2,1,0:T(8,128)(2,1)} custom-call(bf16[128,2304]{1,0:T(8,128)(2,1)} %multiply_convert_fusion.2.x_ref), custom_call_target="tpu_custom_call" | custom-call | bytes 150000000 | tf_op jit(solution)/shard_map/pallas_call | solution.py:243
  277.6 12.4 %fusion.102 = f32[2048,576]{1,0:T(8,128)} fusion(bf16[2048,2304]{1,0:T(8,128)(2,1)} %bitcast.115, bf16[288,2304]{1,0:T(8,128)(2,1)S(1)} %get-tuple-element.53, bf16[288,2304]{1,0:T(8,128)(2,1)S(1)} %copy-done.13), kind=kOutput, calls=%fused_computation.202 | convolution fusion | flops 5441126400 | bytes 16809984 | tf_op jit(solution)/shard_map/dot_general | solution.py:79
  292.8 11.9 %multiply_convert_fusion.1 = (bf16[2048,576]{1,0:T(8,128)(2,1)}, f32[2048,576]{1,0:T(8,128)}) fusion(f32[2048,576]{1,0:T(8,128)} %fusion.102, bf16[2048,2304]{1,0:T(8,128)(2,1)S(1)} %bitcast.119, bf16[288,2304]{1,0:T(8,128)(2,1)S(1)} %get-tuple-element.52, bf16[288,2304]{1,0:T(8,128)(2,1)S(1)} %copy-done.12), kind=kOutput, calls=%fused_computation.17 | convolution fusion | flops 5452922880 | bytes 23887872 | tf_op jit(solution)/shard_map/dot_general | solution.py:79
  306.4 69.5 %shard_map.103 = f32[128,2304]{1,0:T(8,128)} custom-call(bf16[16,128,576]{2,1,0:T(8,128)(2,1)} %bitcast.129, bf16[576,2304]{1,0:T(8,128)(2,1)} %pad_maximum_fusion.3.refs_1_), custom_call_target="tpu_custom_call" | custom-call | bytes 150000000 | tf_op jit(solution)/shard_map/pallas_call | solution.py:536
  381.0 59.0 %shard_map.104 = bf16[16,128,2304]{2,1,0:T(8,128)(2,1)} custom-call(bf16[128,2304]{1,0:T(8,128)(2,1)} %get-tuple-element.58.x_ref), custom_call_target="tpu_custom_call" | custom-call | bytes 150000000 | tf_op jit(solution)/shard_map/pallas_call | solution.py:243
  440.0 11.4 %fusion.111 = f32[576,2304]{1,0:T(8,128)} fusion(bf16[2048,576]{1,0:T(8,128)(2,1)} %get-tuple-element.94, bf16[2048,2304]{1,0:T(8,128)(2,1)} %bitcast.123), kind=kOutput, calls=%fused_computation.211 | convolution fusion | flops 5435817984 | bytes 17104896 | tf_op jit(solution)/shard_map/dot_general | solution.py:73
  451.5 17.1 %multiply_convert_fusion = (bf16[2048,576]{1,0:T(8,128)(2,1)}, bf16[2048,576]{1,0:T(8,128)(2,1)}) fusion(f32[2048,576]{1,0:T(8,128)} %fusion.102, f32[2048,576]{1,0:T(8,128)} %get-tuple-element.95, bf16[2048,2304]{1,0:T(8,128)(2,1)} %bitcast.124, bf16[288,2304]{1,0:T(8,128)(2,1)S(1)} %copy-done.11, bf16[288,2304]{1,0:T(8,128)(2,1)S(1)} %copy-done.9), kind=kOutput, calls=%fused_computation.16 | convolution fusion | flops 5474156544 | bytes 26247168 | tf_op jit(solution)/shard_map/dot_general | solution.py:79
  468.6 10.1 %fusion.110 = f32[576,2304]{1,0:T(8,128)} fusion(bf16[2048,576]{1,0:T(8,128)(2,1)} %get-tuple-element.46, bf16[2048,2304]{1,0:T(8,128)(2,1)S(1)} %bitcast.122), kind=kOutput, calls=%fused_computation.210 | convolution fusion | flops 5435817984 | bytes 17104896 | tf_op jit(solution)/shard_map/dot_general | solution.py:73
  478.7 72.2 %shard_map.105 = f32[128,2304]{1,0:T(8,128)} custom-call(bf16[16,128,576]{2,1,0:T(8,128)(2,1)} %bitcast.130, bf16[16,128,576]{2,1,0:T(8,128)(2,1)} %bitcast.131, bf16[576,2304]{1,0:T(8,128)(2,1)} %get-tuple-element.98.refs_2_, bf16[576,2304]{1,0:T(8,128)(2,1)} %get-tuple-element.99.refs_3_), custom_call_target="tpu_custom_call" | custom-call | bytes 150000000 | tf_op jit(solution)/shard_map/pallas_call | solution.py:536
  557.6 8.6 %fusion.109 = f32[576,2304]{1,0:T(8,128)S(1)} fusion(bf16[2048,576]{1,0:T(8,128)(2,1)S(1)} %copy-done.20, bf16[2048,2304]{1,0:T(8,128)(2,1)} %bitcast.116), kind=kOutput, calls=%fused_computation.209 | convolution fusion | flops 5435817984 | bytes 17104896 | tf_op jit(solution)/shard_map/dot_general | solution.py:73
  575.8 3.7 fusion.26
  583.8 3.5 convolution_multiply_fusion
  590.9 5.5 fusion.1
  609.4 101.4 %shard_map.106 = f32[144,3200]{1,0:T(8,128)} custom-call(bf16[16,144,256]{2,1,0:T(8,128)(2,1)} %bitcast.127, bf16[256,2048]{1,0:T(8,128)(2,1)} %pad_maximum_fusion.6.right_a, bf16[16,144,256]{2,1,0:T(8,128)(2,1)} %bitcast.128, bf16[256,1024]{1,0:T(8,128)(2,1)} %copy.179.right_b, bf16[16,144,128]{2,1,0:T(8,128)(2,1)} %bitcast.132), custom_call_target="tpu_custom_call" | custom-call | bytes 200000000 | tf_op jit(solution)/shard_map/pallas_call | solution.py:498
  713.7 3.7 pad_maximum_fusion
  720.3 5.5 collective-permute-done.6
  734.1 84.5 %collective-permute-done.5 = bf16[128,2304]{1,0:T(8,128)(2,1)S(1)} collective-permute-done((bf16[128,2304]{1,0:T(8,128)(2,1)}, bf16[128,2304]{1,0:T(8,128)(2,1)S(1)}, u32[]{:S(2)}, u32[]{:S(2)}) %collective-permute-start.5) | collective-permute-done | bytes 589856 | tf_op jit(solution)/shard_map/ppermute | solution.py:100
  821.7 5.6 maximum_add_fusion
  (276 shorter events, 94.9 us)
Async XLA Ops:
  3.9 14.4 %collective-permute-start.1 = (bf16[72,3200]{1,0:T(8,128)(2,1)S(1)}, bf16[72,3200]{1,0:T(8,128)(2,1)S(1)}, u32[]{:S(2)}, u32[]{:S(2)}) collective-permute-start(bf16[72,3200]{1,0:T(8,128)(2,1)S(1)} %fusion.68), channel_id=1, source_target_pairs={{0,1},{1,0},{2,3},{3,2},{4,5},{5,4},{6,7},{7,6},{8,9},{9,8},{10,11... | collective-permute-start | bytes 1382408 | tf_op jit(solution)/shard_map/ppermute | solution.py:100
  6.9 107.9 %collective-permute-start = (bf16[128,2304]{1,0:T(8,128)(2,1)S(1)}, bf16[128,2304]{1,0:T(8,128)(2,1)S(1)}, u32[]{:S(2)}, u32[]{:S(2)}) collective-permute-start(bf16[128,2304]{1,0:T(8,128)(2,1)S(1)} %copy-done.1), channel_id=1, source_target_pairs={{0,1},{1,0},{2,3},{3,2},{4,5},{5,4},{6,7},{7,6},{8,9},{9,8},{10,11... | collective-permute-start | bytes 1769480 | tf_op jit(solution)/shard_map/ppermute | solution.py:100
  8.4 102.7 %copy-start.30 = (f32[256,128]{1,0:T(8,128)}, f32[256,128]{1,0:T(8,128)S(1)}, u32[]{:S(2)}) copy-start(f32[256,128]{1,0:T(8,128)S(1)} %get-tuple-element.84) | copy-start | bytes 393220
  8.4 102.7 %copy-start.32 = (f32[256,128]{1,0:T(8,128)}, f32[256,128]{1,0:T(8,128)S(1)}, u32[]{:S(2)}) copy-start(f32[256,128]{1,0:T(8,128)S(1)} %get-tuple-element.85) | copy-start | bytes 393220
  10.1 117.4 %copy-start.37 = (pred[256,256]{0,1:T(8,128)(4,1)}, pred[256,256]{0,1:T(8,128)(4,1)S(1)}, u32[]{:S(2)}) copy-start(pred[256,256]{0,1:T(8,128)(4,1)S(1)} %fusion.69) | copy-start | bytes 196612
  112.7 162.4 %collective-permute-start.3 = (bf16[288,6912]{1,0:T(8,128)(2,1)}, bf16[288,6912]{1,0:T(8,128)(2,1)}, u32[]{:S(2)}, u32[]{:S(2)}) collective-permute-start(bf16[288,6912]{1,0:T(8,128)(2,1)} %param.9), channel_id=1, source_target_pairs={{0,1},{1,0},{2,3},{3,2},{4,5},{5,4},{6,7},{7,6},{8,9},{9,8},{10,11... | collective-permute-start | bytes 11943944 | tf_op jit(solution)/shard_map/ppermute | solution.py:100
  132.7 81.4 %copy-start.2 = (f32[256,2304]{1,0:T(8,128)}, f32[256,2304]{1,0:T(8,128)S(1)}, u32[]{:S(2)}) copy-start(f32[256,2304]{1,0:T(8,128)S(1)} %fusion.13) | copy-start | bytes 7077892
  133.6 80.2 %collective-permute-start.2 = (bf16[128,2304]{1,0:T(8,128)(2,1)}, bf16[128,2304]{1,0:T(8,128)(2,1)S(1)}, u32[]{:S(2)}, u32[]{:S(2)}) collective-permute-start(bf16[128,2304]{1,0:T(8,128)(2,1)} %slice.331), channel_id=1, source_target_pairs={{0,1},{1,0},{2,3},{3,2},{4,5},{5,4},{6,7},{7,6},{8,9},{9,8},{10,11... | collective-permute-start | bytes 1769480 | tf_op jit(solution)/shard_map/ppermute | solution.py:100
  139.6 76.7 %copy-start.44 = (f32[2304]{0:T(1024)S(1)}, f32[2304]{0:T(1024)}, u32[]{:S(2)}) copy-start(f32[2304]{0:T(1024)} %get-tuple-element.38) | copy-start | bytes 27652
  275.0 17.7 %slice-start.6 = ((s8[9437184]{0:T(1024)(128)(4,1)}), s8[4194304]{0:T(1024)(128)(4,1)S(1)}, s32[]{:S(2)}) async-start(s8[9437184]{0:T(1024)(128)(4,1)} %bitcast.117), calls=%async_computation.6 | async-start | bytes 8388608
  277.6 27.1 %copy-start.10 = (bf16[288,2304]{1,0:T(8,128)(2,1)}, bf16[288,2304]{1,0:T(8,128)(2,1)S(1)}, u32[]{:S(2)}) copy-start(bf16[288,2304]{1,0:T(8,128)(2,1)S(1)} %get-tuple-element.51) | copy-start | bytes 3981316
  277.6 15.1 %slice-start.7 = ((s8[9437184]{0:T(1024)(128)(4,1)}), s8[4194304]{0:T(1024)(128)(4,1)S(1)}, s32[]{:S(2)}) async-start(s8[9437184]{0:T(1024)(128)(4,1)} %bitcast.117), calls=%async_computation.7 | async-start | bytes 8388608
  306.3 71.1 %copy-start.7 = (bf16[128,2304]{1,0:T(8,128)(2,1)S(1)}, bf16[128,2304]{1,0:T(8,128)(2,1)}, u32[]{:S(2)}) copy-start(bf16[128,2304]{1,0:T(8,128)(2,1)} %param.11) | copy-start | bytes 1769476
  306.4 71.1 %copy-start.50 = (f32[2304]{0:T(1024)S(1)}, f32[2304]{0:T(1024)}, u32[]{:S(2)}) copy-start(f32[2304]{0:T(1024)} %get-tuple-element.37) | copy-start | bytes 27652
  440.0 28.5 %slice-start.9 = ((s8[9437184]{0:T(1024)(128)(4,1)}), s8[4194304]{0:T(1024)(128)(4,1)S(1)}, s32[]{:S(2)}) async-start(s8[9437184]{0:T(1024)(128)(4,1)} %bitcast.120), calls=%async_computation.9 | async-start | bytes 8388608
  451.4 17.1 %slice-start.10 = ((s8[9437184]{0:T(1024)(128)(4,1)}), s8[4194304]{0:T(1024)(128)(4,1)S(1)}, s32[]{:S(2)}) async-start(s8[9437184]{0:T(1024)(128)(4,1)} %bitcast.120), calls=%async_computation.10 | async-start | bytes 8388608
  451.4 17.1 %slice-start.11 = ((s8[9437184]{0:T(1024)(128)(4,1)}), s8[1048576]{0:T(1024)(128)(4,1)S(1)}, s32[]{:S(2)}) async-start(s8[9437184]{0:T(1024)(128)(4,1)} %bitcast.120), calls=%async_computation.11 | async-start | bytes 2097152
  478.7 72.2 %copy-start.45 = (f32[2304]{0:T(1024)S(1)}, f32[2304]{0:T(1024)}, u32[]{:S(2)}) copy-start(f32[2304]{0:T(1024)} %get-tuple-element.38) | copy-start | bytes 27652
  556.0 19.0 %copy-start.25 = (bf16[128,2304]{1,0:T(8,128)(2,1)}, bf16[128,2304]{1,0:T(8,128)(2,1)S(1)}, u32[]{:S(2)}) copy-start(bf16[128,2304]{1,0:T(8,128)(2,1)S(1)} %fusion.34) | copy-start | bytes 1769476
  556.0 19.0 %collective-permute-start.4 = (bf16[128,2304]{1,0:T(8,128)(2,1)S(1)}, bf16[128,2304]{1,0:T(8,128)(2,1)S(1)}, u32[]{:S(2)}, u32[]{:S(2)}) collective-permute-start(bf16[128,2304]{1,0:T(8,128)(2,1)S(1)} %fusion.34), channel_id=1, source_target_pairs={{0,1},{1,0},{2,3},{3,2},{4,5},{5,4},{6,7},{7,6},{8,9},{9,8},{10,11... | collective-permute-start | bytes 1769480 | tf_op jit(solution)/shard_map/ppermute | solution.py:100
  712.4 13.5 %collective-permute-start.6 = (bf16[72,3200]{1,0:T(8,128)(2,1)S(1)}, bf16[72,3200]{1,0:T(8,128)(2,1)S(1)}, u32[]{:S(2)}, u32[]{:S(2)}) collective-permute-start(bf16[72,3200]{1,0:T(8,128)(2,1)S(1)} %select_convert_fusion), channel_id=1, source_target_pairs={{0,1},{1,0},{2,3},{3,2},{4,5},{5,4},{6,7},{7,6},{8,9},{9,8},{10,11... | collective-permute-start | bytes 1382408 | tf_op jit(solution)/shard_map/ppermute | solution.py:100
  717.4 103.0 %collective-permute-start.7 = (bf16[288,6912]{1,0:T(8,128)(2,1)}, bf16[288,6912]{1,0:T(8,128)(2,1)}, u32[]{:S(2)}, u32[]{:S(2)}) collective-permute-start(bf16[288,6912]{1,0:T(8,128)(2,1)} %pad_maximum_fusion), channel_id=1, source_target_pairs={{0,1},{1,0},{2,3},{3,2},{4,5},{5,4},{6,7},{7,6},{8,9},{9,8},{10,11... | collective-permute-start | bytes 11943944 | tf_op jit(solution)/shard_map/ppermute | solution.py:100
  719.0 99.6 %collective-permute-start.5 = (bf16[128,2304]{1,0:T(8,128)(2,1)}, bf16[128,2304]{1,0:T(8,128)(2,1)S(1)}, u32[]{:S(2)}, u32[]{:S(2)}) collective-permute-start(bf16[128,2304]{1,0:T(8,128)(2,1)} %slice.330), channel_id=1, source_target_pairs={{0,1},{1,0},{2,3},{3,2},{4,5},{5,4},{6,7},{7,6},{8,9},{9,8},{10,11... | collective-permute-start | bytes 1769480 | tf_op jit(solution)/shard_map/ppermute | solution.py:100
  730.6 88.4 %copy-start.6 = (f32[128,2304]{1,0:T(8,128)S(1)}, f32[128,2304]{1,0:T(8,128)}, u32[]{:S(2)}) copy-start(f32[128,2304]{1,0:T(8,128)} %copy-done.5) | copy-start | bytes 3538948
  (60 other events, 215.0 us)

commit v6 on v5

--- a/solution.py
+++ b/solution.py
@@ -134,109 +134,96 @@
     pl.semaphore_wait(barrier, peers)
 
 
+def split_at(cols):
+    return cols // 768 * 128
+
+
 def gather_kernel(n_dp, x_ref, out_ref, own_sem, send_sem, recv_sem):
     line = n_dp // 4
     a, b, c, seq = place_of()
-    me = number(a, b, c)
+    me, pair = number(a, b, c), number(a, 1 - b, c)
+    cols = x_ref.shape[1]
+    late = split_at(cols)
+    spans = (pl.ds(late, cols - late), pl.ds(0, late))
     own = pltpu.make_async_copy(x_ref, out_ref.at[me], own_sem)
     own.start()
     enter(line, a, b, c, seq)
 
-    def copy(way, src, block, a2, b2, c2):
+    def copy(way, block, piece, own=False):
+        a2 = a + (1 if way == 0 else -1 if way == 1 else 0)
+        b2 = 1 - b if way == 2 else b
+        c2 = 1 - c if way == 3 else c
+        there = out_ref.at[block, :, spans[piece]]
         return pltpu.make_async_remote_copy(
-            src_ref=src,
-            dst_ref=out_ref.at[block],
-            send_sem=send_sem.at[way, block],
-            recv_sem=recv_sem.at[block],
+            src_ref=x_ref.at[:, spans[piece]] if own else there,
+            dst_ref=there,
+            send_sem=send_sem.at[way, block, piece],
+            recv_sem=recv_sem.at[block, piece],
             device_id=(number(a2, b2, c2), seq),
             device_id_type=MESH,
         )
 
-    def up(src, block):
-        return copy(0, src, block, a + 1, b, c)
-
-    def down(src, block):
-        return copy(1, src, block, a - 1, b, c)
-
-    def across(src, block):
-        return copy(2, src, block, a, 1 - b, c)
-
-    def over(src, block):
-        return copy(3, src, block, a, b, 1 - c)
-
+    up, down, across, over = range(4)
     has_up, has_down = a < line - 1, a > 0
 
-    @pl.when(has_up)
-    def _():
-        up(x_ref, me).start()
-
-    @pl.when(has_down)
-    def _():
-        down(x_ref, me).start()
-
-    across(x_ref, me).start()
-    over(x_ref, me).start()
-
-    def arrived(block):
-        over(out_ref.at[block], block).wait_recv()
+    def start(way, block, piece, own=False):
+        if way in (up, down):
+
+            @pl.when(has_up if way == up else has_down)
+            def _():
+                copy(way, block, piece, own).start()
+
+        else:
+            copy(way, block, piece, own).start()
+
+    def pass_on(block, piece, ways):
+        copy(over, block, piece).wait_recv()
+        for way in ways:
+            start(way, block, piece)
+
+    for way, piece in (
+        (across, 1), (up, 0), (down, 0), (across, 0), (up, 1), (down, 1), (over, 1), (over, 0)
+    ):
+        start(way, me, piece, own=True)
+    pass_on(pair, 1, (up, down, over))
 
     for k in range(1, line + 1):
         if k < line:
-
-            @pl.when(a - k >= 0)
-            def _(k=k):
-                block = number(a - k, b, c)
-                arrived(block)
-                view = out_ref.at[block]
-
-                @pl.when(has_up)
-                def _():
-                    up(view, block).start()
-
-                across(view, block).start()
-                over(view, block).start()
-
-            @pl.when(a + k < line)
-            def _(k=k):
-                block = number(a + k, b, c)
-                arrived(block)
-                view = out_ref.at[block]
-
-                @pl.when(has_down)
-                def _():
-                    down(view, block).start()
-
-                across(view, block).start()
-                over(view, block).start()
+            for near, piece in ((True, 0), (True, 1), (False, 1)):
+                for sign, way in ((-1, up), (1, down)):
+
+                    @pl.when((a + sign * k >= 0) & (a + sign * k < line))
+                    def _(near=near, piece=piece, sign=sign, way=way, k=k):
+                        block = number(a + sign * k, b if near else 1 - b, c)
+                        pass_on(block, piece, (way, over) if piece else (way, across, over))
 
         j = k - 1
         for sign in (-1, 1) if j else (1,):
 
             @pl.when((a + sign * j >= 0) & (a + sign * j < line))
             def _(j=j, sign=sign):
-                block = number(a + sign * j, 1 - b, c)
-                arrived(block)
-                over(out_ref.at[block], block).start()
+                pass_on(number(a + sign * j, 1 - b, c), 0, (over,))
 
     for other in range(n_dp // 2):
-        block = other * 2 + 1 - c
-        arrived(block)
+        for piece in range(2):
+            copy(over, other * 2 + 1 - c, piece).wait_recv()
 
     own.wait()
+    copy(across, me, 1).wait_send()
     for i in range(line):
-        block = number(i, b, c)
-        across(out_ref.at[block], block).wait_send()
-        over(out_ref.at[block], block).wait_send()
-        second = number(i, 1 - b, c)
-        over(out_ref.at[second], second).wait_send()
-
-        @pl.when(has_up & (i <= a))
-        def _(block=block):
-            up(out_ref.at[block], block).wait_send()
-
-        @pl.when(has_down & (i >= a))
-        def _(block=block):
-            down(out_ref.at[block], block).wait_send()
+        near, far = number(i, b, c), number(i, 1 - b, c)
+        copy(across, near, 0).wait_send()
+        for block, piece in ((near, 0), (near, 1), (far, 0), (far, 1)):
+            copy(over, block, piece).wait_send()
+        for block, piece in ((near, 0), (near, 1), (far, 1)):
+
+            @pl.when(has_up & (i <= a))
+            def _(block=block, piece=piece):
+                copy(up, block, piece).wait_send()
+
+            @pl.when(has_down & (i >= a))
+            def _(block=block, piece=piece):
+                copy(down, block, piece).wait_send()
 
 
 def gathered(x, n_dp, collective_id):
@@ -247,8 +234,8 @@
         out_specs=pl.BlockSpec(memory_space=pl.ANY),
         scratch_shapes=[
             pltpu.SemaphoreType.DMA,
-            pltpu.SemaphoreType.DMA((4, n_dp)),
-            pltpu.SemaphoreType.DMA((n_dp,)),
+            pltpu.SemaphoreType.DMA((4, n_dp, 2)),
+            pltpu.SemaphoreType.DMA((n_dp, 2)),
         ],
         compiler_params=pltpu.CompilerParams(
             collective_id=collective_id, has_side_effects=True
@@ -259,55 +246,52 @@
     )(x)
 
 
-def scatter_steps(n_dp, place, prepare, produce, core_source, out_ref, from_core, from_pair, up_buf,
-                  down_buf, pair_out, core_send, core_recv, pair_send, pair_recv, up_send,
-                  up_recv, down_send, down_recv):
+def scatter_steps(n_dp, place, prepare, produce, core_source, out_ref, from_core, from_pair,
+                  up_buf, down_buf, pair_out, up_few, down_few, pair_few, core_send, core_recv,
+                  pair_send, pair_recv, up_send, up_recv, down_send, down_recv, few_send,
+                  few_recv):
     line = n_dp // 4
     a, b, c, seq = place
+    cols = out_ref.shape[1]
+    late = split_at(cols)
+    most, few = (late, cols), (0, late)
     enter(line, a, b, c, seq)
+
+    def remote(src, dst, send, recv, to_a, to_b, to_c):
+        return pltpu.make_async_remote_copy(
+            src_ref=src,
+            dst_ref=dst,
+            send_sem=send,
+            recv_sem=recv,
+            device_id=(number(to_a, to_b, to_c), seq),
+            device_id_type=MESH,
+        )
 
     def core_copy(block):
         half = block // 2
-        return pltpu.make_async_remote_copy(
-            src_ref=core_source(block),
-            dst_ref=from_core.at[half],
-            send_sem=core_send.at[half],
-            recv_sem=core_recv.at[half],
-            device_id=(number(a, b, 1 - c), seq),
-            device_id_type=MESH,
+        return remote(
+            core_source(block), from_core.at[half], core_send.at[half], core_recv.at[half],
+            a, b, 1 - c,
         )
 
     def pair_copy(to):
-        return pltpu.make_async_remote_copy(
-            src_ref=pair_out.at[to],
-            dst_ref=from_pair.at[to],
-            send_sem=pair_send.at[to],
-            recv_sem=pair_recv.at[to],
-            device_id=(number(a, 1 - b, c), seq),
-            device_id_type=MESH,
+        return remote(
+            pair_out.at[to], from_pair.at[to], pair_send.at[to], pair_recv.at[to], a, 1 - b, c
         )
 
-    def up_copy(to):
-        return pltpu.make_async_remote_copy(
-            src_ref=up_buf.at[to],
-            dst_ref=up_buf.at[to],
-            send_sem=up_send.at[to],
-            recv_sem=up_recv.at[to],
-            device_id=(number(a + 1, b, c), seq),
-            device_id_type=MESH,
+    def few_copy():
+        return remote(
+            pair_few.at[0], pair_few.at[1], few_send.at[0], few_recv.at[0], a, 1 - b, c
         )
 
-    def down_copy(to):
-        return pltpu.make_async_remote_copy(
-            src_ref=down_buf.at[to],
-            dst_ref=down_buf.at[to],
-            send_sem=down_send.at[to],
-            recv_sem=down_recv.at[to],
-            device_id=(number(a - 1, b, c), seq),
-            device_id_type=MESH,
-        )
-
-    def each_target(act):
+    def line_copy(way, to, column):
+        wide, thin = (up_buf, up_few) if way == 1 else (down_buf, down_few)
+        send, recv = (up_send, up_recv) if way == 1 else (down_send, down_recv)
+        buf = wide.at[to] if column is None else thin.at[to * 2 + column]
+        at = to * 3 + (2 if column is None else column)
+        return buf, remote(buf, buf, send.at[at], recv.at[at], a + way, b, c)
+
+    def each_target(act, own=True):
         for k in range(line - 1, 0, -1):
 
             @pl.when(a + k < line)
@@ -318,89 +302,114 @@
             def _(k=k):
                 act(a - k, -1)
 
-        act(a, 0)
+        if own:
+            act(a, 0)
 
     def send_core(block):
-        produce(block, None, core_source(block))
+        produce(block, [], core_source(block), 0, few)
+        produce(block, [], core_source(block), 0, most)
         core_copy(block).start()
+
+    def send_pair(to, way):
+        block = number(to, 1 - b, c)
+        core_copy(block).wait_recv()
+        produce(block, [(from_core.at[block // 2], 0)], pair_out.at[to], late, most)
+        pair_copy(to).start()
+
+    def chain(to, way, column, block, terms, base, span):
+        buf, copy = line_copy(way, to, column)
+        at_end = (a == 0) if way == 1 else (a == line - 1)
+
+        @pl.when(at_end)
+        def _():
+            produce(block, terms, buf, base, span)
+
+        @pl.when(jnp.logical_not(at_end))
+        def _():
+            copy.wait_recv()
+            produce(block, [*terms, (buf, base)], buf, base, span)
+
+        copy.start()
+
+    def collect(column, dst, lo):
+        for way, there in ((1, a > 0), (-1, a < line - 1)):
+
+            @pl.when(there)
+            def _(way=way):
+                buf, copy = line_copy(way, a, column)
+                copy.wait_recv()
+                add_rows(dst, buf, lo)
+
+    def send_few(b2):
+        def act(to, way):
+            block = number(to, b2, c)
+            chain(to, way, b2, block, [(from_core.at[block // 2], 0)], 0, few)
+
+        each_target(act, own=False)
 
     prepare(1 - b, 1 - c)
     each_target(lambda to, way: send_core(number(to, 1 - b, 1 - c)))
     prepare(1 - b, c)
-
-    def send_pair(to, way):
-        block = number(to, 1 - b, c)
-        core_copy(block).wait_recv()
-        produce(block, [from_core.at[block // 2]], pair_out.at[to])
-        pair_copy(to).start()
-
     each_target(send_pair)
     prepare(b, 1 - c)
     each_target(lambda to, way: send_core(number(to, b, 1 - c)))
     prepare(b, c)
-
-    def line_sum(to, more, dst):
+    send_few(1 - b)
+    each_target(lambda to, way: core_copy(number(to, b, c)).wait_recv())
+    send_few(b)
+
+    far = number(a, 1 - b, c)
+    produce(far, [(from_core.at[far // 2], 0)], pair_few.at[0], 0, few)
+    collect(1 - b, pair_few.at[0], 0)
+    few_copy().start()
+
+    def send_line(to, way):
         block = number(to, b, c)
-        produce(block, [from_core.at[block // 2], from_pair.at[to], *more], dst)
-
-    def send_line(to, way):
-        core_copy(number(to, b, c)).wait_recv()
         pair_copy(to).wait_recv()
+        terms = [(from_core.at[block // 2], 0), (from_pair.at[to], late)]
         if way:
-            buf, copy = (up_buf, up_copy) if way == 1 else (down_buf, down_copy)
-            at_end = (a == 0) if way == 1 else (a == line - 1)
-
-            @pl.when(at_end)
-            def _():
-                line_sum(to, [], buf.at[to])
-
-            @pl.when(jnp.logical_not(at_end))
-            def _():
-                copy(to).wait_recv()
-                line_sum(to, [buf.at[to]], buf.at[to])
-
-            copy(to).start()
+            chain(to, way, None, block, terms, late, most)
         else:
-            line_sum(to, [], out_ref)
-            for copy, buf, there in (
-                (up_copy, up_buf, a > 0),
-                (down_copy, down_buf, a < line - 1),
-            ):
-
-                @pl.when(there)
-                def _(copy=copy, buf=buf):
-                    copy(to).wait_recv()
-                    add_rows(out_ref, buf.at[to])
+            produce(block, terms, out_ref, 0, most)
+            collect(None, out_ref, late)
 
     each_target(send_line)
+    me = number(a, b, c)
+    few_copy().wait_recv()
+    produce(me, [(from_core.at[me // 2], 0), (pair_few.at[1], 0)], out_ref, 0, few)
+    collect(b, out_ref, 0)
 
     for i in range(n_dp // 2):
         core_copy(i * 2 + 1 - c).wait_send()
+    few_copy().wait_send()
     for i in range(line):
         pair_copy(i).wait_send()
-
-        @pl.when(i > a)
-        def _(i=i):
-            up_copy(i).wait_send()
-
-        @pl.when(i < a)
-        def _(i=i):
-            down_copy(i).wait_send()
+        for column in (None, 0, 1):
+
+            @pl.when(i > a)
+            def _(i=i, column=column):
+                line_copy(1, i, column)[1].wait_send()
+
+            @pl.when(i < a)
+            def _(i=i, column=column):
+                line_copy(-1, i, column)[1].wait_send()
 
 
 def row_tiles(rows):
     return 16 if rows % 16 == 0 else rows
 
 
-def add_rows(out_ref, term):
-    tile = row_tiles(out_ref.shape[0])
+def add_rows(dst, term, lo):
+    tile = row_tiles(dst.shape[0])
+    width = term.shape[1]
 
     def step(i, _):
         at = pl.ds(pl.multiple_of(i * tile, tile), tile)
-        out_ref[at, :] += term[at, :].astype(jnp.float32)
+        total = dst[at, lo : lo + width].astype(jnp.float32) + term[at, :].astype(jnp.float32)
+        dst[at, lo : lo + width] = total.astype(dst.dtype)
         return 0
 
-    lax.fori_loop(0, out_ref.shape[0] // tile, step, 0)
+    lax.fori_loop(0, dst.shape[0] // tile, step, 0)
 
 
 def dots_kernel(n_dp, n_terms, *refs):
@@ -425,17 +434,18 @@
 
             lax.fori_loop(0, cols // 256, step, 0)
 
-    def produce(block, terms, dst):
-        if terms is None:
+    def produce(block, terms, dst, base, span):
+        if not terms:
             return
+        lo, hi = span
         tile = row_tiles(rows)
 
         def step(i, _):
             at = pl.ds(pl.multiple_of(i * tile, tile), tile)
-            total = parts[block, at, :].astype(f32)
-            for term in terms:
-                total += term[at, :].astype(f32)
-            dst[at, :] = total.astype(dst.dtype)
+            total = parts[block, at, lo:hi].astype(f32)
+            for term, first in terms:
+                total += term[at, lo - first : hi - first].astype(f32)
+            dst[at, lo - base : hi - base] = total.astype(dst.dtype)
             return 0
 
         lax.fori_loop(0, rows // tile, step, 0)
@@ -448,28 +458,33 @@
 def product_kernel(n_dp, left_a, right_a, left_b, right_b, extra, out_ref, core_out, *scratch):
     cols_a, cols_b = right_a.shape[1], right_b.shape[1]
 
-    def produce(block, terms, dst):
-        def part(left, right, first, wide):
+    def produce(block, terms, dst, base, span):
+        lo, hi = span
+
+        def part(left, right, begin, end, offset):
             def step(i, _):
-                inner = pl.ds(pl.multiple_of(i * wide, wide), wide)
-                outer = pl.ds(pl.multiple_of(first + i * wide, 128), wide)
+                inner = pl.ds(pl.multiple_of(begin + i * 256, 128), 256)
+                col = offset + begin + i * 256
                 total = jnp.dot(
                     left[block], right[:, inner], preferred_element_type=jnp.float32
                 )
-                for term in terms or []:
-                    total += term[:, outer].astype(jnp.float32)
-                dst[:, outer] = total.astype(dst.dtype)
+                for term, first in terms:
+                    total += term[:, pl.ds(pl.multiple_of(col - first, 128), 256)].astype(
+                        jnp.float32
+                    )
+                dst[:, pl.ds(pl.multiple_of(col - base, 128), 256)] = total.astype(dst.dtype)
                 return 0
 
-            lax.fori_loop(0, right.shape[1] // wide, step, 0)
-
-        part(left_a, right_a, 0, 256)
-        part(left_b, right_b, cols_a, 256)
-        last = pl.ds(cols_a + cols_b, extra.shape[2])
-        total = extra[block].astype(jnp.float32)
-        for term in terms or []:
-            total += term[:, last].astype(jnp.float32)
-        dst[:, last] = total.astype(dst.dtype)
+            lax.fori_loop(0, (end - begin) // 256, step, 0)
+
+        part(left_a, right_a, lo, min(hi, cols_a), 0)
+        if hi > cols_a:
+            part(left_b, right_b, 0, cols_b, cols_a)
+            at = cols_a + cols_b
+            total = extra[block].astype(jnp.float32)
+            for term, first in terms:
+                total += term[:, at - first : hi - first].astype(jnp.float32)
+            dst[:, at - base : hi - base] = total.astype(dst.dtype)
 
     scatter_steps(
         n_dp,
@@ -484,11 +499,16 @@
 
 def scatter_scratch(n_dp, rows, cols, dtype):
     line = n_dp // 4
+    late = split_at(cols)
     return (
         [pltpu.VMEM((n_dp // 2, rows, cols), dtype)]
-        + [pltpu.VMEM((line, rows, cols), dtype)] * 4
+        + [pltpu.VMEM((line, rows, cols - late), dtype)] * 4
+        + [pltpu.VMEM((2 * line, rows, late), dtype)] * 2
+        + [pltpu.VMEM((2, rows, late), dtype)]
         + [pltpu.SemaphoreType.DMA((n_dp // 2,))] * 2
-        + [pltpu.SemaphoreType.DMA((line,))] * 6
+        + [pltpu.SemaphoreType.DMA((line,))] * 2
+        + [pltpu.SemaphoreType.DMA((3 * line,))] * 4
+        + [pltpu.SemaphoreType.DMA((1,))] * 2
     )
 
 

time: 837 us -> 844 us (level)
  no operation moved by 1% of the time
where the time goes in v6:
time: 844 us; the launch traced here: 834 us
  Pallas kernels  457 us (54%)
  waiting for transfers between devices  173 us (20%)
  matrix products  98.9 us (12%)
  local copies, waits for them, and re-layouts  49.2 us (6%)
  other arithmetic  43.4 us (5%)
  starting transfers between devices  10.5 us (1%)
    pallas_call x3, Pallas kernels, gathered(): pl.pallas_call(functools.partial(gather_kernel, n_dp), out_shape=jax.Shap...  202 us
    ppermute x8, waiting for transfers between devices, swapped(): return lax.ppermute(x, 'seq', [(0, 1), (1, 0)])  173 us
    pallas_call x2, Pallas kernels, scattered_piece(): pl.pallas_call(functools.partial(dots_kernel, n_dp, len(lefts)), out_shap...  148 us
    pallas_call x1, Pallas kernels, scattered_products(): pl.pallas_call(functools.partial(product_kernel, n_dp), out_shape=jax.Sha...  106 us
    dot_general x5, matrix products, contract_cols(): lax.dot_general(left_side, right_side, (((1,), (1,)), ((), ())), preferre...  50.9 us
    dot_general x3, matrix products, contract_rows(): lax.dot_general(left_side, right_side, (((0,), (0,)), ((), ())), preferre...  30.1 us
  transfers between devices with their start and end apart: 8, of which 4 were waited for; matrix products, arithmetic and copies ran while one was open for 7% of the time, Pallas kernels for 18%

profile of v6, /device:TPU:0, one launch (start us, length us, event | category | flops | bytes accessed | tf_op | source)
XLA Modules:
  0.0 834.4 jit_solution(2500563366821517578)
XLA Ops:
  3.9 3.0 collective-permute-start.1
  10.2 8.2 collective-permute-done.1
  19.5 88.5 %shard_map.101 = bf16[16,144,3200]{2,1,0:T(8,128)(2,1)} custom-call(bf16[144,3200]{1,0:T(8,128)(2,1)} %pad_maximum_fusion.7.x_ref), custom_call_target="tpu_custom_call" | custom-call | bytes 150000000 | tf_op jit(solution)/shard_map/pallas_call | solution.py:230
  112.6 6.3 fusion.3
  125.5 4.0 fusion.13
  136.5 74.3 %collective-permute-done.2 = bf16[128,2304]{1,0:T(8,128)(2,1)S(1)} collective-permute-done((bf16[128,2304]{1,0:T(8,128)(2,1)}, bf16[128,2304]{1,0:T(8,128)(2,1)S(1)}, u32[]{:S(2)}, u32[]{:S(2)}) %collective-permute-start.2) | collective-permute-done | bytes 589856 | tf_op jit(solution)/shard_map/ppermute | solution.py:100
  214.2 57.6 %shard_map.102 = bf16[16,128,2304]{2,1,0:T(8,128)(2,1)} custom-call(bf16[128,2304]{1,0:T(8,128)(2,1)} %multiply_convert_fusion.2.x_ref), custom_call_target="tpu_custom_call" | custom-call | bytes 150000000 | tf_op jit(solution)/shard_map/pallas_call | solution.py:230
  274.4 12.4 %fusion.102 = f32[2048,576]{1,0:T(8,128)} fusion(bf16[2048,2304]{1,0:T(8,128)(2,1)} %bitcast.115, bf16[288,2304]{1,0:T(8,128)(2,1)S(1)} %get-tuple-element.53, bf16[288,2304]{1,0:T(8,128)(2,1)S(1)} %copy-done.13), kind=kOutput, calls=%fused_computation.202 | convolution fusion | flops 5441126400 | bytes 16809984 | tf_op jit(solution)/shard_map/dot_general | solution.py:79
  289.5 11.9 %multiply_convert_fusion.1 = (bf16[2048,576]{1,0:T(8,128)(2,1)}, f32[2048,576]{1,0:T(8,128)}) fusion(f32[2048,576]{1,0:T(8,128)} %fusion.102, bf16[2048,2304]{1,0:T(8,128)(2,1)S(1)} %bitcast.119, bf16[288,2304]{1,0:T(8,128)(2,1)S(1)} %get-tuple-element.52, bf16[288,2304]{1,0:T(8,128)(2,1)S(1)} %copy-done.12), kind=kOutput, calls=%fused_computation.17 | convolution fusion | flops 5452922880 | bytes 23887872 | tf_op jit(solution)/shard_map/dot_general | solution.py:79
  303.1 70.9 %shard_map.103 = f32[128,2304]{1,0:T(8,128)} custom-call(bf16[16,128,576]{2,1,0:T(8,128)(2,1)} %bitcast.129, bf16[576,2304]{1,0:T(8,128)(2,1)} %pad_maximum_fusion.3.refs_1_), custom_call_target="tpu_custom_call" | custom-call | bytes 150000000 | tf_op jit(solution)/shard_map/pallas_call | solution.py:556
  379.1 56.0 %shard_map.104 = bf16[16,128,2304]{2,1,0:T(8,128)(2,1)} custom-call(bf16[128,2304]{1,0:T(8,128)(2,1)} %get-tuple-element.58.x_ref), custom_call_target="tpu_custom_call" | custom-call | bytes 150000000 | tf_op jit(solution)/shard_map/pallas_call | solution.py:230
  435.1 11.4 %fusion.111 = f32[576,2304]{1,0:T(8,128)} fusion(bf16[2048,576]{1,0:T(8,128)(2,1)} %get-tuple-element.94, bf16[2048,2304]{1,0:T(8,128)(2,1)} %bitcast.123), kind=kOutput, calls=%fused_computation.211 | convolution fusion | flops 5435817984 | bytes 17104896 | tf_op jit(solution)/shard_map/dot_general | solution.py:73
  446.5 17.1 %multiply_convert_fusion = (bf16[2048,576]{1,0:T(8,128)(2,1)}, bf16[2048,576]{1,0:T(8,128)(2,1)}) fusion(f32[2048,576]{1,0:T(8,128)} %fusion.102, f32[2048,576]{1,0:T(8,128)} %get-tuple-element.95, bf16[2048,2304]{1,0:T(8,128)(2,1)} %bitcast.124, bf16[288,2304]{1,0:T(8,128)(2,1)S(1)} %copy-done.11, bf16[288,2304]{1,0:T(8,128)(2,1)S(1)} %copy-done.9), kind=kOutput, calls=%fused_computation.16 | convolution fusion | flops 5474156544 | bytes 26247168 | tf_op jit(solution)/shard_map/dot_general | solution.py:79
  463.7 10.1 %fusion.110 = f32[576,2304]{1,0:T(8,128)} fusion(bf16[2048,576]{1,0:T(8,128)(2,1)} %get-tuple-element.46, bf16[2048,2304]{1,0:T(8,128)(2,1)S(1)} %bitcast.122), kind=kOutput, calls=%fused_computation.210 | convolution fusion | flops 5435817984 | bytes 17104896 | tf_op jit(solution)/shard_map/dot_general | solution.py:73
  473.7 77.6 %shard_map.105 = f32[128,2304]{1,0:T(8,128)} custom-call(bf16[16,128,576]{2,1,0:T(8,128)(2,1)} %bitcast.130, bf16[16,128,576]{2,1,0:T(8,128)(2,1)} %bitcast.131, bf16[576,2304]{1,0:T(8,128)(2,1)} %get-tuple-element.98.refs_2_, bf16[576,2304]{1,0:T(8,128)(2,1)} %get-tuple-element.99.refs_3_), custom_call_target="tpu_custom_call" | custom-call | bytes 150000000 | tf_op jit(solution)/shard_map/pallas_call | solution.py:556
  558.0 8.6 %fusion.109 = f32[576,2304]{1,0:T(8,128)S(1)} fusion(bf16[2048,576]{1,0:T(8,128)(2,1)S(1)} %copy-done.20, bf16[2048,2304]{1,0:T(8,128)(2,1)} %bitcast.116), kind=kOutput, calls=%fused_computation.209 | convolution fusion | flops 5435817984 | bytes 17104896 | tf_op jit(solution)/shard_map/dot_general | solution.py:73
  576.3 3.7 fusion.26
  584.3 3.5 convolution_multiply_fusion
  591.4 5.5 fusion.1
  609.9 106.4 %shard_map.106 = f32[144,3200]{1,0:T(8,128)} custom-call(bf16[16,144,256]{2,1,0:T(8,128)(2,1)} %bitcast.127, bf16[256,2048]{1,0:T(8,128)(2,1)} %pad_maximum_fusion.6.right_a, bf16[16,144,256]{2,1,0:T(8,128)(2,1)} %bitcast.128, bf16[256,1024]{1,0:T(8,128)(2,1)} %copy.179.right_b, bf16[16,144,128]{2,1,0:T(8,128)(2,1)} %bitcast.132), custom_call_target="tpu_custom_call" | custom-call | bytes 200000000 | tf_op jit(solution)/shard_map/pallas_call | solution.py:518
  719.6 3.7 pad_maximum_fusion
  726.2 5.1 collective-permute-done.6
  739.6 85.7 %collective-permute-done.5 = bf16[128,2304]{1,0:T(8,128)(2,1)S(1)} collective-permute-done((bf16[128,2304]{1,0:T(8,128)(2,1)}, bf16[128,2304]{1,0:T(8,128)(2,1)S(1)}, u32[]{:S(2)}, u32[]{:S(2)}) %collective-permute-start.5) | collective-permute-done | bytes 589856 | tf_op jit(solution)/shard_map/ppermute | solution.py:100
  828.3 5.6 maximum_add_fusion
  (276 shorter events, 95.3 us)
Async XLA Ops:
  3.9 14.4 %collective-permute-start.1 = (bf16[72,3200]{1,0:T(8,128)(2,1)S(1)}, bf16[72,3200]{1,0:T(8,128)(2,1)S(1)}, u32[]{:S(2)}, u32[]{:S(2)}) collective-permute-start(bf16[72,3200]{1,0:T(8,128)(2,1)S(1)} %fusion.68), channel_id=1, source_target_pairs={{0,1},{1,0},{2,3},{3,2},{4,5},{5,4},{6,7},{7,6},{8,9},{9,8},{10,11... | collective-permute-start | bytes 1382408 | tf_op jit(solution)/shard_map/ppermute | solution.py:100
  6.9 104.8 %collective-permute-start = (bf16[128,2304]{1,0:T(8,128)(2,1)S(1)}, bf16[128,2304]{1,0:T(8,128)(2,1)S(1)}, u32[]{:S(2)}, u32[]{:S(2)}) collective-permute-start(bf16[128,2304]{1,0:T(8,128)(2,1)S(1)} %copy-done.1), channel_id=1, source_target_pairs={{0,1},{1,0},{2,3},{3,2},{4,5},{5,4},{6,7},{7,6},{8,9},{9,8},{10,11... | collective-permute-start | bytes 1769480 | tf_op jit(solution)/shard_map/ppermute | solution.py:100
  8.4 99.6 %copy-start.30 = (f32[256,128]{1,0:T(8,128)}, f32[256,128]{1,0:T(8,128)S(1)}, u32[]{:S(2)}) copy-start(f32[256,128]{1,0:T(8,128)S(1)} %get-tuple-element.84) | copy-start | bytes 393220
  8.4 99.6 %copy-start.32 = (f32[256,128]{1,0:T(8,128)}, f32[256,128]{1,0:T(8,128)S(1)}, u32[]{:S(2)}) copy-start(f32[256,128]{1,0:T(8,128)S(1)} %get-tuple-element.85) | copy-start | bytes 393220
  10.1 114.2 %copy-start.37 = (pred[256,256]{0,1:T(8,128)(4,1)}, pred[256,256]{0,1:T(8,128)(4,1)S(1)}, u32[]{:S(2)}) copy-start(pred[256,256]{0,1:T(8,128)(4,1)S(1)} %fusion.69) | copy-start | bytes 196612
  109.5 162.3 %collective-permute-start.3 = (bf16[288,6912]{1,0:T(8,128)(2,1)}, bf16[288,6912]{1,0:T(8,128)(2,1)}, u32[]{:S(2)}, u32[]{:S(2)}) collective-permute-start(bf16[288,6912]{1,0:T(8,128)(2,1)} %param.9), channel_id=1, source_target_pairs={{0,1},{1,0},{2,3},{3,2},{4,5},{5,4},{6,7},{7,6},{8,9},{9,8},{10,11... | collective-permute-start | bytes 11943944 | tf_op jit(solution)/shard_map/ppermute | solution.py:100
  129.5 81.5 %copy-start.2 = (f32[256,2304]{1,0:T(8,128)}, f32[256,2304]{1,0:T(8,128)S(1)}, u32[]{:S(2)}) copy-start(f32[256,2304]{1,0:T(8,128)S(1)} %fusion.13) | copy-start | bytes 7077892
  130.5 80.3 %collective-permute-start.2 = (bf16[128,2304]{1,0:T(8,128)(2,1)}, bf16[128,2304]{1,0:T(8,128)(2,1)S(1)}, u32[]{:S(2)}, u32[]{:S(2)}) collective-permute-start(bf16[128,2304]{1,0:T(8,128)(2,1)} %slice.331), channel_id=1, source_target_pairs={{0,1},{1,0},{2,3},{3,2},{4,5},{5,4},{6,7},{7,6},{8,9},{9,8},{10,11... | collective-permute-start | bytes 1769480 | tf_op jit(solution)/shard_map/ppermute | solution.py:100
  136.4 76.7 %copy-start.44 = (f32[2304]{0:T(1024)S(1)}, f32[2304]{0:T(1024)}, u32[]{:S(2)}) copy-start(f32[2304]{0:T(1024)} %get-tuple-element.38) | copy-start | bytes 27652
  271.8 17.7 %slice-start.6 = ((s8[9437184]{0:T(1024)(128)(4,1)}), s8[4194304]{0:T(1024)(128)(4,1)S(1)}, s32[]{:S(2)}) async-start(s8[9437184]{0:T(1024)(128)(4,1)} %bitcast.117), calls=%async_computation.6 | async-start | bytes 8388608
  274.3 27.1 %copy-start.10 = (bf16[288,2304]{1,0:T(8,128)(2,1)}, bf16[288,2304]{1,0:T(8,128)(2,1)S(1)}, u32[]{:S(2)}) copy-start(bf16[288,2304]{1,0:T(8,128)(2,1)S(1)} %get-tuple-element.51) | copy-start | bytes 3981316
  274.3 15.1 %slice-start.7 = ((s8[9437184]{0:T(1024)(128)(4,1)}), s8[4194304]{0:T(1024)(128)(4,1)S(1)}, s32[]{:S(2)}) async-start(s8[9437184]{0:T(1024)(128)(4,1)} %bitcast.117), calls=%async_computation.7 | async-start | bytes 8388608
  303.1 72.4 %copy-start.7 = (bf16[128,2304]{1,0:T(8,128)(2,1)S(1)}, bf16[128,2304]{1,0:T(8,128)(2,1)}, u32[]{:S(2)}) copy-start(bf16[128,2304]{1,0:T(8,128)(2,1)} %param.11) | copy-start | bytes 1769476
  303.1 72.4 %copy-start.50 = (f32[2304]{0:T(1024)S(1)}, f32[2304]{0:T(1024)}, u32[]{:S(2)}) copy-start(f32[2304]{0:T(1024)} %get-tuple-element.37) | copy-start | bytes 27652
  435.1 28.5 %slice-start.9 = ((s8[9437184]{0:T(1024)(128)(4,1)}), s8[4194304]{0:T(1024)(128)(4,1)S(1)}, s32[]{:S(2)}) async-start(s8[9437184]{0:T(1024)(128)(4,1)} %bitcast.120), calls=%async_computation.9 | async-start | bytes 8388608
  446.5 17.1 %slice-start.10 = ((s8[9437184]{0:T(1024)(128)(4,1)}), s8[4194304]{0:T(1024)(128)(4,1)S(1)}, s32[]{:S(2)}) async-start(s8[9437184]{0:T(1024)(128)(4,1)} %bitcast.120), calls=%async_computation.10 | async-start | bytes 8388608
  446.5 17.1 %slice-start.11 = ((s8[9437184]{0:T(1024)(128)(4,1)}), s8[1048576]{0:T(1024)(128)(4,1)S(1)}, s32[]{:S(2)}) async-start(s8[9437184]{0:T(1024)(128)(4,1)} %bitcast.120), calls=%async_computation.11 | async-start | bytes 2097152
  473.7 77.6 %copy-start.45 = (f32[2304]{0:T(1024)S(1)}, f32[2304]{0:T(1024)}, u32[]{:S(2)}) copy-start(f32[2304]{0:T(1024)} %get-tuple-element.38) | copy-start | bytes 27652
  556.4 19.0 %copy-start.25 = (bf16[128,2304]{1,0:T(8,128)(2,1)}, bf16[128,2304]{1,0:T(8,128)(2,1)S(1)}, u32[]{:S(2)}) copy-start(bf16[128,2304]{1,0:T(8,128)(2,1)S(1)} %fusion.34) | copy-start | bytes 1769476
  556.4 19.0 %collective-permute-start.4 = (bf16[128,2304]{1,0:T(8,128)(2,1)S(1)}, bf16[128,2304]{1,0:T(8,128)(2,1)S(1)}, u32[]{:S(2)}, u32[]{:S(2)}) collective-permute-start(bf16[128,2304]{1,0:T(8,128)(2,1)S(1)} %fusion.34), channel_id=1, source_target_pairs={{0,1},{1,0},{2,3},{3,2},{4,5},{5,4},{6,7},{7,6},{8,9},{9,8},{10,11... | collective-permute-start | bytes 1769480 | tf_op jit(solution)/shard_map/ppermute | solution.py:100
  717.8 13.5 %collective-permute-start.6 = (bf16[72,3200]{1,0:T(8,128)(2,1)S(1)}, bf16[72,3200]{1,0:T(8,128)(2,1)S(1)}, u32[]{:S(2)}, u32[]{:S(2)}) collective-permute-start(bf16[72,3200]{1,0:T(8,128)(2,1)S(1)} %select_convert_fusion), channel_id=1, source_target_pairs={{0,1},{1,0},{2,3},{3,2},{4,5},{5,4},{6,7},{7,6},{8,9},{9,8},{10,11... | collective-permute-start | bytes 1382408 | tf_op jit(solution)/shard_map/ppermute | solution.py:100
  723.3 103.8 %collective-permute-start.7 = (bf16[288,6912]{1,0:T(8,128)(2,1)}, bf16[288,6912]{1,0:T(8,128)(2,1)}, u32[]{:S(2)}, u32[]{:S(2)}) collective-permute-start(bf16[288,6912]{1,0:T(8,128)(2,1)} %pad_maximum_fusion), channel_id=1, source_target_pairs={{0,1},{1,0},{2,3},{3,2},{4,5},{5,4},{6,7},{7,6},{8,9},{9,8},{10,11... | collective-permute-start | bytes 11943944 | tf_op jit(solution)/shard_map/ppermute | solution.py:100
  724.5 100.8 %collective-permute-start.5 = (bf16[128,2304]{1,0:T(8,128)(2,1)}, bf16[128,2304]{1,0:T(8,128)(2,1)S(1)}, u32[]{:S(2)}, u32[]{:S(2)}) collective-permute-start(bf16[128,2304]{1,0:T(8,128)(2,1)} %slice.330), channel_id=1, source_target_pairs={{0,1},{1,0},{2,3},{3,2},{4,5},{5,4},{6,7},{7,6},{8,9},{9,8},{10,11... | collective-permute-start | bytes 1769480 | tf_op jit(solution)/shard_map/ppermute | solution.py:100
  736.1 89.6 %copy-start.6 = (f32[128,2304]{1,0:T(8,128)S(1)}, f32[128,2304]{1,0:T(8,128)}, u32[]{:S(2)}) copy-start(f32[128,2304]{1,0:T(8,128)} %copy-done.5) | copy-start | bytes 3538948
  (60 other events, 214.5 us)

commit v7 on v5

--- a/solution.py
+++ b/solution.py
@@ -134,109 +134,109 @@
     pl.semaphore_wait(barrier, peers)
 
 
+def split_at(cols):
+    return cols // 768 * 128
+
+
 def gather_kernel(n_dp, x_ref, out_ref, own_sem, send_sem, recv_sem):
     line = n_dp // 4
     a, b, c, seq = place_of()
-    me = number(a, b, c)
+    me, pair = number(a, b, c), number(a, 1 - b, c)
+    cols = x_ref.shape[1]
+    late = split_at(cols)
+    spans = (pl.ds(late, cols - late), pl.ds(0, late))
     own = pltpu.make_async_copy(x_ref, out_ref.at[me], own_sem)
     own.start()
     enter(line, a, b, c, seq)
 
-    def copy(way, src, block, a2, b2, c2):
+    def copy(way, block, piece, own=False):
+        a2 = a + (1 if way == 0 else -1 if way == 1 else 0)
+        b2 = 1 - b if way == 2 else b
+        c2 = 1 - c if way == 3 else c
+        there = out_ref.at[block, :, spans[piece]]
         return pltpu.make_async_remote_copy(
-            src_ref=src,
-            dst_ref=out_ref.at[block],
-            send_sem=send_sem.at[way, block],
-            recv_sem=recv_sem.at[block],
+            src_ref=x_ref.at[:, spans[piece]] if own else there,
+            dst_ref=there,
+            send_sem=send_sem.at[way, block, piece],
+            recv_sem=recv_sem.at[block, piece],
             device_id=(number(a2, b2, c2), seq),
             device_id_type=MESH,
         )
 
-    def up(src, block):
-        return copy(0, src, block, a + 1, b, c)
-
-    def down(src, block):
-        return copy(1, src, block, a - 1, b, c)
-
-    def across(src, block):
-        return copy(2, src, block, a, 1 - b, c)
-
-    def over(src, block):
-        return copy(3, src, block, a, b, 1 - c)
-
+    up, down, across, over = range(4)
     has_up, has_down = a < line - 1, a > 0
 
-    @pl.when(has_up)
-    def _():
-        up(x_ref, me).start()
-
-    @pl.when(has_down)
-    def _():
-        down(x_ref, me).start()
-
-    across(x_ref, me).start()
-    over(x_ref, me).start()
-
-    def arrived(block):
-        over(out_ref.at[block], block).wait_recv()
-
-    for k in range(1, line + 1):
-        if k < line:
-
-            @pl.when(a - k >= 0)
-            def _(k=k):
-                block = number(a - k, b, c)
-                arrived(block)
-                view = out_ref.at[block]
-
-                @pl.when(has_up)
-                def _():
-                    up(view, block).start()
-
-                across(view, block).start()
-                over(view, block).start()
-
-            @pl.when(a + k < line)
-            def _(k=k):
-                block = number(a + k, b, c)
-                arrived(block)
-                view = out_ref.at[block]
-
-                @pl.when(has_down)
-                def _():
-                    down(view, block).start()
-
-                across(view, block).start()
-                over(view, block).start()
-
-        j = k - 1
-        for sign in (-1, 1) if j else (1,):
-
-            @pl.when((a + sign * j >= 0) & (a + sign * j < line))
-            def _(j=j, sign=sign):
-                block = number(a + sign * j, 1 - b, c)
-                arrived(block)
-                over(out_ref.at[block], block).start()
+    def start(way, block, piece, own=False):
+        if way in (up, down):
+
+            @pl.when(has_up if way == up else has_down)
+            def _():
+                copy(way, block, piece, own).start()
+
+        else:
+            copy(way, block, piece, own).start()
+
+    def pass_on(block, piece, ways):
+        copy(over, block, piece).wait_recv()
+        for way in ways:
+            start(way, block, piece)
+
+    for way, piece in ((up, 0), (down, 0), (across, 1), (across, 0), (over, 0), (over, 1)):
+        start(way, me, piece, own=True)
+
+    def each_at(k, act):
+        for sign, way in ((-1, up), (1, down)) if k else ((1, over),):
+
+            @pl.when((a + sign * k >= 0) & (a + sign * k < line))
+            def _(sign=sign, way=way):
+                act(a + sign * k, way)
+
+    pass_on(pair, 1, (over,))
+
+    def after(k):
+        for way, last in ((up, a == k), (down, line - 1 - a == k)):
+
+            @pl.when(last)
+            def _(way=way):
+                start(way, me, 1, own=True)
+                start(way, pair, 1)
+
+    def from_pair(k):
+        each_at(k, lambda i, way: pass_on(number(i, 1 - b, c), 0, (over,)))
+
+    after(0)
+    for k in range(1, line):
+        each_at(k, lambda i, way: pass_on(number(i, b, c), 0, (way, across, over)))
+        after(k)
+    half = line // 2
+    for k in range(half):
+        from_pair(k)
+    for k in range(1, line):
+        for b2 in (b, 1 - b):
+            each_at(k, lambda i, way, b2=b2: pass_on(number(i, b2, c), 1, (way, over)))
+    for k in range(half, line):
+        from_pair(k)
 
     for other in range(n_dp // 2):
-        block = other * 2 + 1 - c
-        arrived(block)
+        for piece in range(2):
+            copy(over, other * 2 + 1 - c, piece).wait_recv()
 
     own.wait()
+    copy(across, me, 1).wait_send()
     for i in range(line):
-        block = number(i, b, c)
-        across(out_ref.at[block], block).wait_send()
-        over(out_ref.at[block], block).wait_send()
-        second = number(i, 1 - b, c)
-        over(out_ref.at[second], second).wait_send()
-
-        @pl.when(has_up & (i <= a))
-        def _(block=block):
-            up(out_ref.at[block], block).wait_send()
-
-        @pl.when(has_down & (i >= a))
-        def _(block=block):
-            down(out_ref.at[block], block).wait_send()
+        near, far = number(i, b, c), number(i, 1 - b, c)
+        copy(across, near, 0).wait_send()
+        for block, piece in ((near, 0), (near, 1), (far, 0), (far, 1)):
+            copy(over, block, piece).wait_send()
+        for block, piece in ((near, 0), (near, 1), (far, 1)):
+
+            @pl.when(has_up & (i <= a))
+            def _(block=block, piece=piece):
+                copy(up, block, piece).wait_send()
+
+            @pl.when(has_down & (i >= a))
+            def _(block=block, piece=piece):
+                copy(down, block, piece).wait_send()
 
 
 def gathered(x, n_dp, collective_id):
@@ -247,8 +247,8 @@
         out_specs=pl.BlockSpec(memory_space=pl.ANY),
         scratch_shapes=[
             pltpu.SemaphoreType.DMA,
-            pltpu.SemaphoreType.DMA((4, n_dp)),
-            pltpu.SemaphoreType.DMA((n_dp,)),
+            pltpu.SemaphoreType.DMA((4, n_dp, 2)),
+            pltpu.SemaphoreType.DMA((n_dp, 2)),
         ],
         compiler_params=pltpu.CompilerParams(
             collective_id=collective_id, has_side_effects=True

time: 837 us -> 814 us (0.973)
  Pallas kernels: 451 us -> 433 us
    pallas_call x3, Pallas kernels: 208 us -> 187 us  [gathered(): pl.pallas_call(functools.partial(gather_kernel, n_dp), out_shape=jax.Shap...]
  transfers between devices with their start and end apart: 8 -> 8, of which waited for: 4 -> 4; matrix products, arithmetic and copies ran while one was open for 7% -> 7% of each run, Pallas kernels for 18% -> 17%
where the time goes in v7:
time: 814 us; the launch traced here: 810 us
  Pallas kernels  433 us (53%)
  waiting for transfers between devices  173 us (21%)
  matrix products  98.9 us (12%)
  local copies, waits for them, and re-layouts  49.2 us (6%)
  other arithmetic  43.4 us (5%)
  starting transfers between devices  10.4 us (1%)
    pallas_call x3, Pallas kernels, gathered(): pl.pallas_call(functools.partial(gather_kernel, n_dp), out_shape=jax.Shap...  187 us
    ppermute x8, waiting for transfers between devices, swapped(): return lax.ppermute(x, 'seq', [(0, 1), (1, 0)])  173 us
    pallas_call x2, Pallas kernels, scattered_piece(): pl.pallas_call(functools.partial(dots_kernel, n_dp, len(lefts)), out_shap...  142 us
    pallas_call x1, Pallas kernels, scattered_products(): pl.pallas_call(functools.partial(product_kernel, n_dp), out_shape=jax.Sha...  104 us
    dot_general x5, matrix products, contract_cols(): lax.dot_general(left_side, right_side, (((1,), (1,)), ((), ())), preferre...  50.9 us
    dot_general x3, matrix products, contract_rows(): lax.dot_general(left_side, right_side, (((0,), (0,)), ((), ())), preferre...  30.1 us
    unnamed x160, local copies, waits for them, and re-layouts  16.6 us
  transfers between devices with their start and end apart: 8, of which 4 were waited for; matrix products, arithmetic and copies ran while one was open for 7% of the time, Pallas kernels for 17%

profile of v7, /device:TPU:0, one launch (start us, length us, event | category | flops | bytes accessed | tf_op | source)
XLA Modules:
  0.0 809.8 jit_solution(12166533579781036598)
XLA Ops:
  3.9 3.0 collective-permute-start.1
  10.2 8.2 %collective-permute-done.1 = bf16[72,3200]{1,0:T(8,128)(2,1)S(1)} collective-permute-done((bf16[72,3200]{1,0:T(8,128)(2,1)S(1)}, bf16[72,3200]{1,0:T(8,128)(2,1)S(1)}, u32[]{:S(2)}, u32[]{:S(2)}) %collective-permute-start.1) | collective-permute-done | bytes 460832 | tf_op jit(solution)/shard_map/ppermute | solution.py:100
  19.5 79.6 %shard_map.101 = bf16[16,144,3200]{2,1,0:T(8,128)(2,1)} custom-call(bf16[144,3200]{1,0:T(8,128)(2,1)} %pad_maximum_fusion.7.x_ref), custom_call_target="tpu_custom_call" | custom-call | bytes 150000000 | tf_op jit(solution)/shard_map/pallas_call | solution.py:243
  103.7 6.3 fusion.3
  116.6 4.0 fusion.13
  127.6 74.3 %collective-permute-done.2 = bf16[128,2304]{1,0:T(8,128)(2,1)S(1)} collective-permute-done((bf16[128,2304]{1,0:T(8,128)(2,1)}, bf16[128,2304]{1,0:T(8,128)(2,1)S(1)}, u32[]{:S(2)}, u32[]{:S(2)}) %collective-permute-start.2) | collective-permute-done | bytes 589856 | tf_op jit(solution)/shard_map/ppermute | solution.py:100
  205.3 55.1 %shard_map.102 = bf16[16,128,2304]{2,1,0:T(8,128)(2,1)} custom-call(bf16[128,2304]{1,0:T(8,128)(2,1)} %multiply_convert_fusion.2.x_ref), custom_call_target="tpu_custom_call" | custom-call | bytes 150000000 | tf_op jit(solution)/shard_map/pallas_call | solution.py:243
  263.1 12.4 %fusion.102 = f32[2048,576]{1,0:T(8,128)} fusion(bf16[2048,2304]{1,0:T(8,128)(2,1)} %bitcast.115, bf16[288,2304]{1,0:T(8,128)(2,1)S(1)} %get-tuple-element.53, bf16[288,2304]{1,0:T(8,128)(2,1)S(1)} %copy-done.13), kind=kOutput, calls=%fused_computation.202 | convolution fusion | flops 5441126400 | bytes 16809984 | tf_op jit(solution)/shard_map/dot_general | solution.py:79
  278.2 11.9 %multiply_convert_fusion.1 = (bf16[2048,576]{1,0:T(8,128)(2,1)}, f32[2048,576]{1,0:T(8,128)}) fusion(f32[2048,576]{1,0:T(8,128)} %fusion.102, bf16[2048,2304]{1,0:T(8,128)(2,1)S(1)} %bitcast.119, bf16[288,2304]{1,0:T(8,128)(2,1)S(1)} %get-tuple-element.52, bf16[288,2304]{1,0:T(8,128)(2,1)S(1)} %copy-done.12), kind=kOutput, calls=%fused_computation.17 | convolution fusion | flops 5452922880 | bytes 23887872 | tf_op jit(solution)/shard_map/dot_general | solution.py:79
  291.8 69.1 %shard_map.103 = f32[128,2304]{1,0:T(8,128)} custom-call(bf16[16,128,576]{2,1,0:T(8,128)(2,1)} %bitcast.129, bf16[576,2304]{1,0:T(8,128)(2,1)} %pad_maximum_fusion.3.refs_1_), custom_call_target="tpu_custom_call" | custom-call | bytes 150000000 | tf_op jit(solution)/shard_map/pallas_call | solution.py:536
  366.0 52.7 %shard_map.104 = bf16[16,128,2304]{2,1,0:T(8,128)(2,1)} custom-call(bf16[128,2304]{1,0:T(8,128)(2,1)} %get-tuple-element.58.x_ref), custom_call_target="tpu_custom_call" | custom-call | bytes 150000000 | tf_op jit(solution)/shard_map/pallas_call | solution.py:243
  418.7 11.4 %fusion.111 = f32[576,2304]{1,0:T(8,128)} fusion(bf16[2048,576]{1,0:T(8,128)(2,1)} %get-tuple-element.94, bf16[2048,2304]{1,0:T(8,128)(2,1)} %bitcast.123), kind=kOutput, calls=%fused_computation.211 | convolution fusion | flops 5435817984 | bytes 17104896 | tf_op jit(solution)/shard_map/dot_general | solution.py:73
  430.1 17.1 %multiply_convert_fusion = (bf16[2048,576]{1,0:T(8,128)(2,1)}, bf16[2048,576]{1,0:T(8,128)(2,1)}) fusion(f32[2048,576]{1,0:T(8,128)} %fusion.102, f32[2048,576]{1,0:T(8,128)} %get-tuple-element.95, bf16[2048,2304]{1,0:T(8,128)(2,1)} %bitcast.124, bf16[288,2304]{1,0:T(8,128)(2,1)S(1)} %copy-done.11, bf16[288,2304]{1,0:T(8,128)(2,1)S(1)} %copy-done.9), kind=kOutput, calls=%fused_computation.16 | convolution fusion | flops 5474156544 | bytes 26247168 | tf_op jit(solution)/shard_map/dot_general | solution.py:79
  447.2 10.1 %fusion.110 = f32[576,2304]{1,0:T(8,128)} fusion(bf16[2048,576]{1,0:T(8,128)(2,1)} %get-tuple-element.46, bf16[2048,2304]{1,0:T(8,128)(2,1)S(1)} %bitcast.122), kind=kOutput, calls=%fused_computation.210 | convolution fusion | flops 5435817984 | bytes 17104896 | tf_op jit(solution)/shard_map/dot_general | solution.py:73
  457.3 72.9 %shard_map.105 = f32[128,2304]{1,0:T(8,128)} custom-call(bf16[16,128,576]{2,1,0:T(8,128)(2,1)} %bitcast.130, bf16[16,128,576]{2,1,0:T(8,128)(2,1)} %bitcast.131, bf16[576,2304]{1,0:T(8,128)(2,1)} %get-tuple-element.98.refs_2_, bf16[576,2304]{1,0:T(8,128)(2,1)} %get-tuple-element.99.refs_3_), custom_call_target="tpu_custom_call" | custom-call | bytes 150000000 | tf_op jit(solution)/shard_map/pallas_call | solution.py:536
  536.9 8.6 %fusion.109 = f32[576,2304]{1,0:T(8,128)S(1)} fusion(bf16[2048,576]{1,0:T(8,128)(2,1)S(1)} %copy-done.20, bf16[2048,2304]{1,0:T(8,128)(2,1)} %bitcast.116), kind=kOutput, calls=%fused_computation.209 | convolution fusion | flops 5435817984 | bytes 17104896 | tf_op jit(solution)/shard_map/dot_general | solution.py:73
  555.2 3.7 fusion.26
  563.2 3.5 convolution_multiply_fusion
  570.2 5.5 fusion.1
  588.8 103.7 %shard_map.106 = f32[144,3200]{1,0:T(8,128)} custom-call(bf16[16,144,256]{2,1,0:T(8,128)(2,1)} %bitcast.127, bf16[256,2048]{1,0:T(8,128)(2,1)} %pad_maximum_fusion.6.right_a, bf16[16,144,256]{2,1,0:T(8,128)(2,1)} %bitcast.128, bf16[256,1024]{1,0:T(8,128)(2,1)} %copy.179.right_b, bf16[16,144,128]{2,1,0:T(8,128)(2,1)} %bitcast.132), custom_call_target="tpu_custom_call" | custom-call | bytes 200000000 | tf_op jit(solution)/shard_map/pallas_call | solution.py:498
  695.7 3.7 pad_maximum_fusion
  702.2 5.3 collective-permute-done.6
  715.8 85.1 %collective-permute-done.5 = bf16[128,2304]{1,0:T(8,128)(2,1)S(1)} collective-permute-done((bf16[128,2304]{1,0:T(8,128)(2,1)}, bf16[128,2304]{1,0:T(8,128)(2,1)S(1)}, u32[]{:S(2)}, u32[]{:S(2)}) %collective-permute-start.5) | collective-permute-done | bytes 589856 | tf_op jit(solution)/shard_map/ppermute | solution.py:100
  803.9 5.6 maximum_add_fusion
  (276 shorter events, 95.1 us)
Async XLA Ops:
  3.9 14.4 %collective-permute-start.1 = (bf16[72,3200]{1,0:T(8,128)(2,1)S(1)}, bf16[72,3200]{1,0:T(8,128)(2,1)S(1)}, u32[]{:S(2)}, u32[]{:S(2)}) collective-permute-start(bf16[72,3200]{1,0:T(8,128)(2,1)S(1)} %fusion.68), channel_id=1, source_target_pairs={{0,1},{1,0},{2,3},{3,2},{4,5},{5,4},{6,7},{7,6},{8,9},{9,8},{10,11... | collective-permute-start | bytes 1382408 | tf_op jit(solution)/shard_map/ppermute | solution.py:100
  6.9 95.9 %collective-permute-start = (bf16[128,2304]{1,0:T(8,128)(2,1)S(1)}, bf16[128,2304]{1,0:T(8,128)(2,1)S(1)}, u32[]{:S(2)}, u32[]{:S(2)}) collective-permute-start(bf16[128,2304]{1,0:T(8,128)(2,1)S(1)} %copy-done.1), channel_id=1, source_target_pairs={{0,1},{1,0},{2,3},{3,2},{4,5},{5,4},{6,7},{7,6},{8,9},{9,8},{10,11... | collective-permute-start | bytes 1769480 | tf_op jit(solution)/shard_map/ppermute | solution.py:100
  8.4 90.7 %copy-start.30 = (f32[256,128]{1,0:T(8,128)}, f32[256,128]{1,0:T(8,128)S(1)}, u32[]{:S(2)}) copy-start(f32[256,128]{1,0:T(8,128)S(1)} %get-tuple-element.84) | copy-start | bytes 393220
  8.4 90.7 %copy-start.32 = (f32[256,128]{1,0:T(8,128)}, f32[256,128]{1,0:T(8,128)S(1)}, u32[]{:S(2)}) copy-start(f32[256,128]{1,0:T(8,128)S(1)} %get-tuple-element.85) | copy-start | bytes 393220
  10.1 105.3 %copy-start.37 = (pred[256,256]{0,1:T(8,128)(4,1)}, pred[256,256]{0,1:T(8,128)(4,1)S(1)}, u32[]{:S(2)}) copy-start(pred[256,256]{0,1:T(8,128)(4,1)S(1)} %fusion.69) | copy-start | bytes 196612
  100.6 159.9 %collective-permute-start.3 = (bf16[288,6912]{1,0:T(8,128)(2,1)}, bf16[288,6912]{1,0:T(8,128)(2,1)}, u32[]{:S(2)}, u32[]{:S(2)}) collective-permute-start(bf16[288,6912]{1,0:T(8,128)(2,1)} %param.9), channel_id=1, source_target_pairs={{0,1},{1,0},{2,3},{3,2},{4,5},{5,4},{6,7},{7,6},{8,9},{9,8},{10,11... | collective-permute-start | bytes 11943944 | tf_op jit(solution)/shard_map/ppermute | solution.py:100
  120.6 81.5 %copy-start.2 = (f32[256,2304]{1,0:T(8,128)}, f32[256,2304]{1,0:T(8,128)S(1)}, u32[]{:S(2)}) copy-start(f32[256,2304]{1,0:T(8,128)S(1)} %fusion.13) | copy-start | bytes 7077892
  121.6 80.3 %collective-permute-start.2 = (bf16[128,2304]{1,0:T(8,128)(2,1)}, bf16[128,2304]{1,0:T(8,128)(2,1)S(1)}, u32[]{:S(2)}, u32[]{:S(2)}) collective-permute-start(bf16[128,2304]{1,0:T(8,128)(2,1)} %slice.331), channel_id=1, source_target_pairs={{0,1},{1,0},{2,3},{3,2},{4,5},{5,4},{6,7},{7,6},{8,9},{9,8},{10,11... | collective-permute-start | bytes 1769480 | tf_op jit(solution)/shard_map/ppermute | solution.py:100
  127.5 76.7 %copy-start.44 = (f32[2304]{0:T(1024)S(1)}, f32[2304]{0:T(1024)}, u32[]{:S(2)}) copy-start(f32[2304]{0:T(1024)} %get-tuple-element.38) | copy-start | bytes 27652
  260.5 17.7 %slice-start.6 = ((s8[9437184]{0:T(1024)(128)(4,1)}), s8[4194304]{0:T(1024)(128)(4,1)S(1)}, s32[]{:S(2)}) async-start(s8[9437184]{0:T(1024)(128)(4,1)} %bitcast.117), calls=%async_computation.6 | async-start | bytes 8388608
  263.0 27.1 %copy-start.10 = (bf16[288,2304]{1,0:T(8,128)(2,1)}, bf16[288,2304]{1,0:T(8,128)(2,1)S(1)}, u32[]{:S(2)}) copy-start(bf16[288,2304]{1,0:T(8,128)(2,1)S(1)} %get-tuple-element.51) | copy-start | bytes 3981316
  263.0 15.1 %slice-start.7 = ((s8[9437184]{0:T(1024)(128)(4,1)}), s8[4194304]{0:T(1024)(128)(4,1)S(1)}, s32[]{:S(2)}) async-start(s8[9437184]{0:T(1024)(128)(4,1)} %bitcast.117), calls=%async_computation.7 | async-start | bytes 8388608
  291.8 70.6 %copy-start.7 = (bf16[128,2304]{1,0:T(8,128)(2,1)S(1)}, bf16[128,2304]{1,0:T(8,128)(2,1)}, u32[]{:S(2)}) copy-start(bf16[128,2304]{1,0:T(8,128)(2,1)} %param.11) | copy-start | bytes 1769476
  291.8 70.6 %copy-start.50 = (f32[2304]{0:T(1024)S(1)}, f32[2304]{0:T(1024)}, u32[]{:S(2)}) copy-start(f32[2304]{0:T(1024)} %get-tuple-element.37) | copy-start | bytes 27652
  418.7 28.5 %slice-start.9 = ((s8[9437184]{0:T(1024)(128)(4,1)}), s8[4194304]{0:T(1024)(128)(4,1)S(1)}, s32[]{:S(2)}) async-start(s8[9437184]{0:T(1024)(128)(4,1)} %bitcast.120), calls=%async_computation.9 | async-start | bytes 8388608
  430.1 17.1 %slice-start.10 = ((s8[9437184]{0:T(1024)(128)(4,1)}), s8[4194304]{0:T(1024)(128)(4,1)S(1)}, s32[]{:S(2)}) async-start(s8[9437184]{0:T(1024)(128)(4,1)} %bitcast.120), calls=%async_computation.10 | async-start | bytes 8388608
  430.1 17.1 %slice-start.11 = ((s8[9437184]{0:T(1024)(128)(4,1)}), s8[1048576]{0:T(1024)(128)(4,1)S(1)}, s32[]{:S(2)}) async-start(s8[9437184]{0:T(1024)(128)(4,1)} %bitcast.120), calls=%async_computation.11 | async-start | bytes 2097152
  457.3 72.9 %copy-start.45 = (f32[2304]{0:T(1024)S(1)}, f32[2304]{0:T(1024)}, u32[]{:S(2)}) copy-start(f32[2304]{0:T(1024)} %get-tuple-element.38) | copy-start | bytes 27652
  535.3 19.0 %copy-start.25 = (bf16[128,2304]{1,0:T(8,128)(2,1)}, bf16[128,2304]{1,0:T(8,128)(2,1)S(1)}, u32[]{:S(2)}) copy-start(bf16[128,2304]{1,0:T(8,128)(2,1)S(1)} %fusion.34) | copy-start | bytes 1769476
  535.3 19.0 %collective-permute-start.4 = (bf16[128,2304]{1,0:T(8,128)(2,1)S(1)}, bf16[128,2304]{1,0:T(8,128)(2,1)S(1)}, u32[]{:S(2)}, u32[]{:S(2)}) collective-permute-start(bf16[128,2304]{1,0:T(8,128)(2,1)S(1)} %fusion.34), channel_id=1, source_target_pairs={{0,1},{1,0},{2,3},{3,2},{4,5},{5,4},{6,7},{7,6},{8,9},{9,8},{10,11... | collective-permute-start | bytes 1769480 | tf_op jit(solution)/shard_map/ppermute | solution.py:100
  694.0 13.5 %collective-permute-start.6 = (bf16[72,3200]{1,0:T(8,128)(2,1)S(1)}, bf16[72,3200]{1,0:T(8,128)(2,1)S(1)}, u32[]{:S(2)}, u32[]{:S(2)}) collective-permute-start(bf16[72,3200]{1,0:T(8,128)(2,1)S(1)} %select_convert_fusion), channel_id=1, source_target_pairs={{0,1},{1,0},{2,3},{3,2},{4,5},{5,4},{6,7},{7,6},{8,9},{9,8},{10,11... | collective-permute-start | bytes 1382408 | tf_op jit(solution)/shard_map/ppermute | solution.py:100
  699.3 103.4 %collective-permute-start.7 = (bf16[288,6912]{1,0:T(8,128)(2,1)}, bf16[288,6912]{1,0:T(8,128)(2,1)}, u32[]{:S(2)}, u32[]{:S(2)}) collective-permute-start(bf16[288,6912]{1,0:T(8,128)(2,1)} %pad_maximum_fusion), channel_id=1, source_target_pairs={{0,1},{1,0},{2,3},{3,2},{4,5},{5,4},{6,7},{7,6},{8,9},{9,8},{10,11... | collective-permute-start | bytes 11943944 | tf_op jit(solution)/shard_map/ppermute | solution.py:100
  700.7 100.2 %collective-permute-start.5 = (bf16[128,2304]{1,0:T(8,128)(2,1)}, bf16[128,2304]{1,0:T(8,128)(2,1)S(1)}, u32[]{:S(2)}, u32[]{:S(2)}) collective-permute-start(bf16[128,2304]{1,0:T(8,128)(2,1)} %slice.330), channel_id=1, source_target_pairs={{0,1},{1,0},{2,3},{3,2},{4,5},{5,4},{6,7},{7,6},{8,9},{9,8},{10,11... | collective-permute-start | bytes 1769480 | tf_op jit(solution)/shard_map/ppermute | solution.py:100
  712.3 89.0 %copy-start.6 = (f32[128,2304]{1,0:T(8,128)S(1)}, f32[128,2304]{1,0:T(8,128)}, u32[]{:S(2)}) copy-start(f32[128,2304]{1,0:T(8,128)} %copy-done.5) | copy-start | bytes 3538948
  (60 other events, 214.7 us)

commit v8 on v7

--- a/solution.py
+++ b/solution.py
@@ -142,9 +142,10 @@
     line = n_dp // 4
     a, b, c, seq = place_of()
     me, pair = number(a, b, c), number(a, 1 - b, c)
-    cols = x_ref.shape[1]
+    halves, _, cols = x_ref.shape
     late = split_at(cols)
     spans = (pl.ds(late, cols - late), pl.ds(0, late))
+    large, small = range(halves), range(halves, 2 * halves)
     own = pltpu.make_async_copy(x_ref, out_ref.at[me], own_sem)
     own.start()
     enter(line, a, b, c, seq)
@@ -153,9 +154,10 @@
         a2 = a + (1 if way == 0 else -1 if way == 1 else 0)
         b2 = 1 - b if way == 2 else b
         c2 = 1 - c if way == 3 else c
-        there = out_ref.at[block, :, spans[piece]]
+        half, span = piece % halves, spans[piece // halves]
+        there = out_ref.at[block, half, :, span]
         return pltpu.make_async_remote_copy(
-            src_ref=x_ref.at[:, spans[piece]] if own else there,
+            src_ref=x_ref.at[half, :, span] if own else there,
             dst_ref=there,
             send_sem=send_sem.at[way, block, piece],
             recv_sem=recv_sem.at[block, piece],
@@ -181,8 +183,10 @@
         for way in ways:
             start(way, block, piece)
 
-    for way, piece in ((up, 0), (down, 0), (across, 1), (across, 0), (over, 0), (over, 1)):
-        start(way, me, piece, own=True)
+    for way, pieces in ((across, small), (up, large), (down, large), (across, large),
+                        (over, large), (over, small)):
+        for piece in pieces:
+            start(way, me, piece, own=True)
 
     def each_at(k, act):
         for sign, way in ((-1, up), (1, down)) if k else ((1, over),):
@@ -191,55 +195,66 @@
             def _(sign=sign, way=way):
                 act(a + sign * k, way)
 
-    pass_on(pair, 1, (over,))
+    for piece in small:
+        pass_on(pair, piece, (over,))
 
     def after(k):
         for way, last in ((up, a == k), (down, line - 1 - a == k)):
 
             @pl.when(last)
             def _(way=way):
-                start(way, me, 1, own=True)
-                start(way, pair, 1)
+                for piece in small:
+                    start(way, me, piece, own=True)
+                    start(way, pair, piece)
 
     def from_pair(k):
-        each_at(k, lambda i, way: pass_on(number(i, 1 - b, c), 0, (over,)))
+        for p in large:
+            each_at(k, lambda i, way, p=p: pass_on(number(i, 1 - b, c), p, (over,)))
 
     after(0)
     for k in range(1, line):
-        each_at(k, lambda i, way: pass_on(number(i, b, c), 0, (way, across, over)))
+        for p in large:
+            each_at(k, lambda i, way, p=p: pass_on(number(i, b, c), p, (way, across, over)))
         after(k)
-    half = line // 2
-    for k in range(half):
+    half_line = line // 2
+    for k in range(half_line):
         from_pair(k)
     for k in range(1, line):
         for b2 in (b, 1 - b):
-            each_at(k, lambda i, way, b2=b2: pass_on(number(i, b2, c), 1, (way, over)))
-    for k in range(half, line):
+            for p in small:
+                each_at(k, lambda i, way, b2=b2, p=p: pass_on(number(i, b2, c), p, (way, over)))
+    for k in range(half_line, line):
         from_pair(k)
 
     for other in range(n_dp // 2):
-        for piece in range(2):
+        for piece in range(2 * halves):
             copy(over, other * 2 + 1 - c, piece).wait_recv()
 
     own.wait()
-    copy(across, me, 1).wait_send()
+    for p in small:
+        copy(across, me, p).wait_send()
     for i in range(line):
         near, far = number(i, b, c), number(i, 1 - b, c)
-        copy(across, near, 0).wait_send()
-        for block, piece in ((near, 0), (near, 1), (far, 0), (far, 1)):
-            copy(over, block, piece).wait_send()
-        for block, piece in ((near, 0), (near, 1), (far, 1)):
-
-            @pl.when(has_up & (i <= a))
-            def _(block=block, piece=piece):
-                copy(up, block, piece).wait_send()
-
-            @pl.when(has_down & (i >= a))
-            def _(block=block, piece=piece):
-                copy(down, block, piece).wait_send()
+        for p in large:
+            copy(across, near, p).wait_send()
+        for block in (near, far):
+            for piece in range(2 * halves):
+                copy(over, block, piece).wait_send()
+        for block, pieces in ((near, large), (near, small), (far, small)):
+            for piece in pieces:
+
+                @pl.when(has_up & (i <= a))
+                def _(block=block, piece=piece):
+                    copy(up, block, piece).wait_send()
+
+                @pl.when(has_down & (i >= a))
+                def _(block=block, piece=piece):
+                    copy(down, block, piece).wait_send()
 
 
 def gathered(x, n_dp, collective_id):
+    rows, cols = x.shape
+    x = x.reshape(2, rows // 2, cols)
     return pl.pallas_call(
         functools.partial(gather_kernel, n_dp),
         out_shape=jax.ShapeDtypeStruct((n_dp, *x.shape), x.dtype),
@@ -247,8 +262,8 @@
         out_specs=pl.BlockSpec(memory_space=pl.ANY),
         scratch_shapes=[
             pltpu.SemaphoreType.DMA,
-            pltpu.SemaphoreType.DMA((4, n_dp, 2)),
-            pltpu.SemaphoreType.DMA((n_dp, 2)),
+            pltpu.SemaphoreType.DMA((4, n_dp, 4)),
+            pltpu.SemaphoreType.DMA((n_dp, 4)),
         ],
         compiler_params=pltpu.CompilerParams(
             collective_id=collective_id, has_side_effects=True
@@ -307,26 +322,26 @@
             device_id_type=MESH,
         )
 
+    def target_at(k, act):
+        if k == 0:
+            act(a, 0)
+            return
+
+        @pl.when(a + k < line)
+        def _():
+            act(a + k, 1)
+
+        @pl.when(a - k >= 0)
+        def _():
+            act(a - k, -1)
+
     def each_target(act):
-        for k in range(line - 1, 0, -1):
-
-            @pl.when(a + k < line)
-            def _(k=k):
-                act(a + k, 1)
-
-            @pl.when(a - k >= 0)
-            def _(k=k):
-                act(a - k, -1)
-
-        act(a, 0)
+        for k in range(line - 1, -1, -1):
+            target_at(k, act)
 
     def send_core(block):
         produce(block, None, core_source(block))
         core_copy(block).start()
-
-    prepare(1 - b, 1 - c)
-    each_target(lambda to, way: send_core(number(to, 1 - b, 1 - c)))
-    prepare(1 - b, c)
 
     def send_pair(to, way):
         block = number(to, 1 - b, c)
@@ -334,7 +349,16 @@
         produce(block, [from_core.at[block // 2]], pair_out.at[to])
         pair_copy(to).start()
 
-    each_target(send_pair)
+    def first_core(to, way):
+        send_core(number(to, 1 - b, 1 - c))
+
+    prepare(1 - b, 1 - c)
+    target_at(line - 1, first_core)
+    prepare(1 - b, c)
+    for k in range(line - 1, -1, -1):
+        if k:
+            target_at(k - 1, first_core)
+        target_at(k, send_pair)
     prepare(b, 1 - c)
     each_target(lambda to, way: send_core(number(to, b, 1 - c)))
     prepare(b, c)

time: 814 us -> 814 us (level)
  no operation moved by 1% of the time
where the time goes in v8:
time: 814 us; the launch traced here: 810 us
  Pallas kernels  431 us (53%)
  waiting for transfers between devices  175 us (21%)
  matrix products  99 us (12%)
  local copies, waits for them, and re-layouts  49.2 us (6%)
  other arithmetic  43.4 us (5%)
  starting transfers between devices  10.2 us (1%)
    pallas_call x3, Pallas kernels, gathered(): pl.pallas_call(functools.partial(gather_kernel, n_dp), out_shape=jax.Shap...  188 us
    ppermute x8, waiting for transfers between devices, swapped(): return lax.ppermute(x, 'seq', [(0, 1), (1, 0)])  175 us
    pallas_call x2, Pallas kernels, scattered_piece(): pl.pallas_call(functools.partial(dots_kernel, n_dp, len(lefts)), out_shap...  141 us
    pallas_call x1, Pallas kernels, scattered_products(): pl.pallas_call(functools.partial(product_kernel, n_dp), out_shape=jax.Sha...  102 us
    dot_general x5, matrix products, contract_cols(): lax.dot_general(left_side, right_side, (((1,), (1,)), ((), ())), preferre...  50.9 us
    dot_general x3, matrix products, contract_rows(): lax.dot_general(left_side, right_side, (((0,), (0,)), ((), ())), preferre...  30.1 us
    unnamed x160, local copies, waits for them, and re-layouts  16.6 us
  transfers between devices with their start and end apart: 8, of which 4 were waited for; matrix products, arithmetic and copies ran while one was open for 7% of the time, Pallas kernels for 17%

profile of v8, /device:TPU:0, one launch (start us, length us, event | category | flops | bytes accessed | tf_op | source)
XLA Modules:
  0.0 809.7 jit_solution(16325376786363107449)
XLA Ops:
  3.9 3.0 collective-permute-start.1
  10.2 8.2 %collective-permute-done.1 = bf16[72,3200]{1,0:T(8,128)(2,1)S(1)} collective-permute-done((bf16[72,3200]{1,0:T(8,128)(2,1)S(1)}, bf16[72,3200]{1,0:T(8,128)(2,1)S(1)}, u32[]{:S(2)}, u32[]{:S(2)}) %collective-permute-start.1) | collective-permute-done | bytes 460832 | tf_op jit(solution)/shard_map/ppermute | solution.py:100
  19.5 79.9 %shard_map.101 = bf16[16,2,72,3200]{3,2,1,0:T(8,128)(2,1)} custom-call(bf16[2,72,3200]{2,1,0:T(8,128)(2,1)} %bitcast.132), custom_call_target="tpu_custom_call" | custom-call | bytes 150000000 | tf_op jit(solution)/shard_map/pallas_call | solution.py:258
  104.0 6.3 fusion.3
  116.9 4.0 fusion.13
  127.9 74.3 %collective-permute-done.2 = bf16[128,2304]{1,0:T(8,128)(2,1)S(1)} collective-permute-done((bf16[128,2304]{1,0:T(8,128)(2,1)}, bf16[128,2304]{1,0:T(8,128)(2,1)S(1)}, u32[]{:S(2)}, u32[]{:S(2)}) %collective-permute-start.2) | collective-permute-done | bytes 589856 | tf_op jit(solution)/shard_map/ppermute | solution.py:100
  205.6 53.8 %shard_map.102 = bf16[16,2,64,2304]{3,2,1,0:T(8,128)(2,1)} custom-call(bf16[2,64,2304]{2,1,0:T(8,128)(2,1)} %bitcast.138), custom_call_target="tpu_custom_call" | custom-call | bytes 150000000 | tf_op jit(solution)/shard_map/pallas_call | solution.py:258
  262.0 12.4 %fusion.102 = f32[2048,576]{1,0:T(8,128)} fusion(bf16[2048,2304]{1,0:T(8,128)(2,1)} %bitcast.118, bf16[288,2304]{1,0:T(8,128)(2,1)S(1)} %get-tuple-element.53, bf16[288,2304]{1,0:T(8,128)(2,1)S(1)} %copy-done.13), kind=kOutput, calls=%fused_computation.202 | convolution fusion | flops 5441126400 | bytes 16809984 | tf_op jit(solution)/shard_map/dot_general | solution.py:79
  277.2 11.9 %multiply_convert_fusion.1 = (bf16[2048,576]{1,0:T(8,128)(2,1)}, f32[2048,576]{1,0:T(8,128)}) fusion(f32[2048,576]{1,0:T(8,128)} %fusion.102, bf16[2048,2304]{1,0:T(8,128)(2,1)S(1)} %bitcast.122, bf16[288,2304]{1,0:T(8,128)(2,1)S(1)} %get-tuple-element.52, bf16[288,2304]{1,0:T(8,128)(2,1)S(1)} %copy-done.12), kind=kOutput, calls=%fused_computation.17 | convolution fusion | flops 5452922880 | bytes 23887872 | tf_op jit(solution)/shard_map/dot_general | solution.py:79
  290.8 68.5 %shard_map.103 = f32[128,2304]{1,0:T(8,128)} custom-call(bf16[16,128,576]{2,1,0:T(8,128)(2,1)} %bitcast.133, bf16[576,2304]{1,0:T(8,128)(2,1)} %pad_maximum_fusion.3.refs_1_), custom_call_target="tpu_custom_call" | custom-call | bytes 150000000 | tf_op jit(solution)/shard_map/pallas_call | solution.py:560
  364.4 54.2 %shard_map.104 = bf16[16,2,64,2304]{3,2,1,0:T(8,128)(2,1)} custom-call(bf16[2,64,2304]{2,1,0:T(8,128)(2,1)} %bitcast.137), custom_call_target="tpu_custom_call" | custom-call | bytes 150000000 | tf_op jit(solution)/shard_map/pallas_call | solution.py:258
  418.7 11.4 %fusion.111 = f32[576,2304]{1,0:T(8,128)} fusion(bf16[2048,576]{1,0:T(8,128)(2,1)} %get-tuple-element.94, bf16[2048,2304]{1,0:T(8,128)(2,1)} %bitcast.126), kind=kOutput, calls=%fused_computation.211 | convolution fusion | flops 5435817984 | bytes 17104896 | tf_op jit(solution)/shard_map/dot_general | solution.py:73
  430.1 17.1 %multiply_convert_fusion = (bf16[2048,576]{1,0:T(8,128)(2,1)}, bf16[2048,576]{1,0:T(8,128)(2,1)}) fusion(f32[2048,576]{1,0:T(8,128)} %fusion.102, f32[2048,576]{1,0:T(8,128)} %get-tuple-element.95, bf16[2048,2304]{1,0:T(8,128)(2,1)} %bitcast.127, bf16[288,2304]{1,0:T(8,128)(2,1)S(1)} %copy-done.11, bf16[288,2304]{1,0:T(8,128)(2,1)S(1)} %copy-done.9), kind=kOutput, calls=%fused_computation.16 | convolution fusion | flops 5474156544 | bytes 26247168 | tf_op jit(solution)/shard_map/dot_general | solution.py:79
  447.2 10.1 %fusion.110 = f32[576,2304]{1,0:T(8,128)} fusion(bf16[2048,576]{1,0:T(8,128)(2,1)} %get-tuple-element.46, bf16[2048,2304]{1,0:T(8,128)(2,1)S(1)} %bitcast.125), kind=kOutput, calls=%fused_computation.210 | convolution fusion | flops 5435817984 | bytes 17104896 | tf_op jit(solution)/shard_map/dot_general | solution.py:73
  457.3 72.8 %shard_map.105 = f32[128,2304]{1,0:T(8,128)} custom-call(bf16[16,128,576]{2,1,0:T(8,128)(2,1)} %bitcast.134, bf16[16,128,576]{2,1,0:T(8,128)(2,1)} %bitcast.135, bf16[576,2304]{1,0:T(8,128)(2,1)} %get-tuple-element.98.refs_2_, bf16[576,2304]{1,0:T(8,128)(2,1)} %get-tuple-element.99.refs_3_), custom_call_target="tpu_custom_call" | custom-call | bytes 150000000 | tf_op jit(solution)/shard_map/pallas_call | solution.py:560
  536.7 8.7 %fusion.109 = f32[576,2304]{1,0:T(8,128)S(1)} fusion(bf16[2048,576]{1,0:T(8,128)(2,1)S(1)} %copy-done.20, bf16[2048,2304]{1,0:T(8,128)(2,1)} %bitcast.119), kind=kOutput, calls=%fused_computation.209 | convolution fusion | flops 5435817984 | bytes 17104896 | tf_op jit(solution)/shard_map/dot_general | solution.py:73
  555.1 3.7 fusion.26
  563.1 3.5 convolution_multiply_fusion
  570.1 5.5 fusion.1
  588.7 101.9 %shard_map.106 = f32[144,3200]{1,0:T(8,128)} custom-call(bf16[16,144,256]{2,1,0:T(8,128)(2,1)} %bitcast.130, bf16[256,2048]{1,0:T(8,128)(2,1)} %pad_maximum_fusion.6.right_a, bf16[16,144,256]{2,1,0:T(8,128)(2,1)} %bitcast.131, bf16[256,1024]{1,0:T(8,128)(2,1)} %copy.179.right_b, bf16[16,144,128]{2,1,0:T(8,128)(2,1)} %bitcast.136), custom_call_target="tpu_custom_call" | custom-call | bytes 200000000 | tf_op jit(solution)/shard_map/pallas_call | solution.py:522
  693.7 3.7 pad_maximum_fusion
  700.2 5.4 collective-permute-done.6
  713.9 86.9 %collective-permute-done.5 = bf16[128,2304]{1,0:T(8,128)(2,1)S(1)} collective-permute-done((bf16[128,2304]{1,0:T(8,128)(2,1)}, bf16[128,2304]{1,0:T(8,128)(2,1)S(1)}, u32[]{:S(2)}, u32[]{:S(2)}) %collective-permute-start.5) | collective-permute-done | bytes 589856 | tf_op jit(solution)/shard_map/ppermute | solution.py:100
  803.8 5.6 maximum_add_fusion
  (276 shorter events, 94.9 us)
Async XLA Ops:
  3.9 14.4 %collective-permute-start.1 = (bf16[72,3200]{1,0:T(8,128)(2,1)S(1)}, bf16[72,3200]{1,0:T(8,128)(2,1)S(1)}, u32[]{:S(2)}, u32[]{:S(2)}) collective-permute-start(bf16[72,3200]{1,0:T(8,128)(2,1)S(1)} %fusion.68), channel_id=1, source_target_pairs={{0,1},{1,0},{2,3},{3,2},{4,5},{5,4},{6,7},{7,6},{8,9},{9,8},{10,11... | collective-permute-start | bytes 1382408 | tf_op jit(solution)/shard_map/ppermute | solution.py:100
  6.9 96.2 %collective-permute-start = (bf16[128,2304]{1,0:T(8,128)(2,1)S(1)}, bf16[128,2304]{1,0:T(8,128)(2,1)S(1)}, u32[]{:S(2)}, u32[]{:S(2)}) collective-permute-start(bf16[128,2304]{1,0:T(8,128)(2,1)S(1)} %copy-done.1), channel_id=1, source_target_pairs={{0,1},{1,0},{2,3},{3,2},{4,5},{5,4},{6,7},{7,6},{8,9},{9,8},{10,11... | collective-permute-start | bytes 1769480 | tf_op jit(solution)/shard_map/ppermute | solution.py:100
  8.4 91.0 %copy-start.30 = (f32[256,128]{1,0:T(8,128)}, f32[256,128]{1,0:T(8,128)S(1)}, u32[]{:S(2)}) copy-start(f32[256,128]{1,0:T(8,128)S(1)} %get-tuple-element.84) | copy-start | bytes 393220
  8.4 91.0 %copy-start.32 = (f32[256,128]{1,0:T(8,128)}, f32[256,128]{1,0:T(8,128)S(1)}, u32[]{:S(2)}) copy-start(f32[256,128]{1,0:T(8,128)S(1)} %get-tuple-element.85) | copy-start | bytes 393220
  10.1 105.6 %copy-start.37 = (pred[256,256]{0,1:T(8,128)(4,1)}, pred[256,256]{0,1:T(8,128)(4,1)S(1)}, u32[]{:S(2)}) copy-start(pred[256,256]{0,1:T(8,128)(4,1)S(1)} %fusion.69) | copy-start | bytes 196612
  100.9 158.5 %collective-permute-start.3 = (bf16[288,6912]{1,0:T(8,128)(2,1)}, bf16[288,6912]{1,0:T(8,128)(2,1)}, u32[]{:S(2)}, u32[]{:S(2)}) collective-permute-start(bf16[288,6912]{1,0:T(8,128)(2,1)} %param.9), channel_id=1, source_target_pairs={{0,1},{1,0},{2,3},{3,2},{4,5},{5,4},{6,7},{7,6},{8,9},{9,8},{10,11... | collective-permute-start | bytes 11943944 | tf_op jit(solution)/shard_map/ppermute | solution.py:100
  120.9 81.5 %copy-start.2 = (f32[256,2304]{1,0:T(8,128)}, f32[256,2304]{1,0:T(8,128)S(1)}, u32[]{:S(2)}) copy-start(f32[256,2304]{1,0:T(8,128)S(1)} %fusion.13) | copy-start | bytes 7077892
  121.9 80.3 %collective-permute-start.2 = (bf16[128,2304]{1,0:T(8,128)(2,1)}, bf16[128,2304]{1,0:T(8,128)(2,1)S(1)}, u32[]{:S(2)}, u32[]{:S(2)}) collective-permute-start(bf16[128,2304]{1,0:T(8,128)(2,1)} %slice.331), channel_id=1, source_target_pairs={{0,1},{1,0},{2,3},{3,2},{4,5},{5,4},{6,7},{7,6},{8,9},{9,8},{10,11... | collective-permute-start | bytes 1769480 | tf_op jit(solution)/shard_map/ppermute | solution.py:100
  127.9 76.8 %copy-start.44 = (f32[2304]{0:T(1024)S(1)}, f32[2304]{0:T(1024)}, u32[]{:S(2)}) copy-start(f32[2304]{0:T(1024)} %get-tuple-element.38) | copy-start | bytes 27652
  259.4 17.7 %slice-start.6 = ((s8[9437184]{0:T(1024)(128)(4,1)}), s8[4194304]{0:T(1024)(128)(4,1)S(1)}, s32[]{:S(2)}) async-start(s8[9437184]{0:T(1024)(128)(4,1)} %bitcast.120), calls=%async_computation.6 | async-start | bytes 8388608
  262.0 27.1 %copy-start.10 = (bf16[288,2304]{1,0:T(8,128)(2,1)}, bf16[288,2304]{1,0:T(8,128)(2,1)S(1)}, u32[]{:S(2)}) copy-start(bf16[288,2304]{1,0:T(8,128)(2,1)S(1)} %get-tuple-element.51) | copy-start | bytes 3981316
  262.0 15.1 %slice-start.7 = ((s8[9437184]{0:T(1024)(128)(4,1)}), s8[4194304]{0:T(1024)(128)(4,1)S(1)}, s32[]{:S(2)}) async-start(s8[9437184]{0:T(1024)(128)(4,1)} %bitcast.120), calls=%async_computation.7 | async-start | bytes 8388608
  290.7 70.0 %copy-start.7 = (bf16[128,2304]{1,0:T(8,128)(2,1)S(1)}, bf16[128,2304]{1,0:T(8,128)(2,1)}, u32[]{:S(2)}) copy-start(bf16[128,2304]{1,0:T(8,128)(2,1)} %param.11) | copy-start | bytes 1769476
  290.8 70.0 %copy-start.50 = (f32[2304]{0:T(1024)S(1)}, f32[2304]{0:T(1024)}, u32[]{:S(2)}) copy-start(f32[2304]{0:T(1024)} %get-tuple-element.37) | copy-start | bytes 27652
  418.7 28.5 %slice-start.9 = ((s8[9437184]{0:T(1024)(128)(4,1)}), s8[4194304]{0:T(1024)(128)(4,1)S(1)}, s32[]{:S(2)}) async-start(s8[9437184]{0:T(1024)(128)(4,1)} %bitcast.123), calls=%async_computation.9 | async-start | bytes 8388608
  430.1 17.1 %slice-start.10 = ((s8[9437184]{0:T(1024)(128)(4,1)}), s8[4194304]{0:T(1024)(128)(4,1)S(1)}, s32[]{:S(2)}) async-start(s8[9437184]{0:T(1024)(128)(4,1)} %bitcast.123), calls=%async_computation.10 | async-start | bytes 8388608
  430.1 17.1 %slice-start.11 = ((s8[9437184]{0:T(1024)(128)(4,1)}), s8[1048576]{0:T(1024)(128)(4,1)S(1)}, s32[]{:S(2)}) async-start(s8[9437184]{0:T(1024)(128)(4,1)} %bitcast.123), calls=%async_computation.11 | async-start | bytes 2097152
  457.3 72.8 %copy-start.45 = (f32[2304]{0:T(1024)S(1)}, f32[2304]{0:T(1024)}, u32[]{:S(2)}) copy-start(f32[2304]{0:T(1024)} %get-tuple-element.38) | copy-start | bytes 27652
  535.2 19.0 %copy-start.25 = (bf16[128,2304]{1,0:T(8,128)(2,1)}, bf16[128,2304]{1,0:T(8,128)(2,1)S(1)}, u32[]{:S(2)}) copy-start(bf16[128,2304]{1,0:T(8,128)(2,1)S(1)} %fusion.34) | copy-start | bytes 1769476
  535.2 19.0 %collective-permute-start.4 = (bf16[128,2304]{1,0:T(8,128)(2,1)S(1)}, bf16[128,2304]{1,0:T(8,128)(2,1)S(1)}, u32[]{:S(2)}, u32[]{:S(2)}) collective-permute-start(bf16[128,2304]{1,0:T(8,128)(2,1)S(1)} %fusion.34), channel_id=1, source_target_pairs={{0,1},{1,0},{2,3},{3,2},{4,5},{5,4},{6,7},{7,6},{8,9},{9,8},{10,11... | collective-permute-start | bytes 1769480 | tf_op jit(solution)/shard_map/ppermute | solution.py:100
  692.1 13.5 %collective-permute-start.6 = (bf16[72,3200]{1,0:T(8,128)(2,1)S(1)}, bf16[72,3200]{1,0:T(8,128)(2,1)S(1)}, u32[]{:S(2)}, u32[]{:S(2)}) collective-permute-start(bf16[72,3200]{1,0:T(8,128)(2,1)S(1)} %select_convert_fusion), channel_id=1, source_target_pairs={{0,1},{1,0},{2,3},{3,2},{4,5},{5,4},{6,7},{7,6},{8,9},{9,8},{10,11... | collective-permute-start | bytes 1382408 | tf_op jit(solution)/shard_map/ppermute | solution.py:100
  697.3 105.3 %collective-permute-start.7 = (bf16[288,6912]{1,0:T(8,128)(2,1)}, bf16[288,6912]{1,0:T(8,128)(2,1)}, u32[]{:S(2)}, u32[]{:S(2)}) collective-permute-start(bf16[288,6912]{1,0:T(8,128)(2,1)} %pad_maximum_fusion), channel_id=1, source_target_pairs={{0,1},{1,0},{2,3},{3,2},{4,5},{5,4},{6,7},{7,6},{8,9},{9,8},{10,11... | collective-permute-start | bytes 11943944 | tf_op jit(solution)/shard_map/ppermute | solution.py:100
  698.8 102.0 %collective-permute-start.5 = (bf16[128,2304]{1,0:T(8,128)(2,1)}, bf16[128,2304]{1,0:T(8,128)(2,1)S(1)}, u32[]{:S(2)}, u32[]{:S(2)}) collective-permute-start(bf16[128,2304]{1,0:T(8,128)(2,1)} %slice.330), channel_id=1, source_target_pairs={{0,1},{1,0},{2,3},{3,2},{4,5},{5,4},{6,7},{7,6},{8,9},{9,8},{10,11... | collective-permute-start | bytes 1769480 | tf_op jit(solution)/shard_map/ppermute | solution.py:100
  710.4 90.8 %copy-start.6 = (f32[128,2304]{1,0:T(8,128)S(1)}, f32[128,2304]{1,0:T(8,128)}, u32[]{:S(2)}) copy-start(f32[128,2304]{1,0:T(8,128)} %copy-done.5) | copy-start | bytes 3538948
  (60 other events, 214.7 us)

commit v9 on v7

--- a/solution.py
+++ b/solution.py
@@ -614,6 +614,8 @@
     pack_tokens = jnp.concatenate([tokens, other_tokens]).astype(jnp.float32)
     tokens_f = tokens.astype(jnp.float32)
     attn_in = rms_norm(pack_tokens, gain_vals[0]).astype(bf16)
+    block_rows = (n_dp, 2 * weight_rows)
+    attn_in_turned = attn_in.T.reshape(*block_rows, 2 * tok_rows)
     projected = jnp.dot(attn_in, attn_weights, preferred_element_type=jnp.float32)
     pack = 2 * tok_rows
     queries = (
@@ -712,9 +714,8 @@
     d_gain_in = jnp.sum(d_attn_in_part * normed, axis=0)
 
     gain_part = jnp.stack([d_gain_in, d_gain_post, d_gain_ffn, d_gain_out], axis=1)
-    block_rows = (n_dp, 2 * weight_rows)
     attn_sum = scattered_products(
-        attn_in.T.reshape(*block_rows, pack),
+        attn_in_turned,
         d_projected,
         d_attn.T.reshape(*block_rows, pack),
         mixed_heads,
@@ -726,7 +727,8 @@
     mine, others = mine_and_other(
         (attn_sum[:weight_rows], attn_sum[weight_rows:]), seq_index
     )
-    partner = swapped(others.astype(bf16)).astype(jnp.float32)
+    partner = swapped(others.astype(bf16))
+    partner = partner.astype(jnp.float32)
     gains_grad = mine[:, half_cols : half_cols + 4] + partner[:, half_cols : half_cols + 4]
     first, second = in_order(mine, partner, seq_index)
     cuts = ((0, q_cols), (q_cols, q_cols + k_cols), (q_cols + k_cols, proj_cols),

time: 814 us -> 814 us (level)
  no operation moved by 1% of the time
where the time goes in v9:
time: 814 us; the launch traced here: 810 us
  Pallas kernels  433 us (53%)
  waiting for transfers between devices  173 us (21%)
  matrix products  98.9 us (12%)
  local copies, waits for them, and re-layouts  49.2 us (6%)
  other arithmetic  43.4 us (5%)
  starting transfers between devices  10.4 us (1%)
    pallas_call x3, Pallas kernels, gathered(): pl.pallas_call(functools.partial(gather_kernel, n_dp), out_shape=jax.Shap...  187 us
    ppermute x8, waiting for transfers between devices, swapped(): return lax.ppermute(x, 'seq', [(0, 1), (1, 0)])  173 us
    pallas_call x2, Pallas kernels, scattered_piece(): pl.pallas_call(functools.partial(dots_kernel, n_dp, len(lefts)), out_shap...  142 us
    pallas_call x1, Pallas kernels, scattered_products(): pl.pallas_call(functools.partial(product_kernel, n_dp), out_shape=jax.Sha...  104 us
    dot_general x5, matrix products, contract_cols(): lax.dot_general(left_side, right_side, (((1,), (1,)), ((), ())), preferre...  50.9 us
    dot_general x3, matrix products, contract_rows(): lax.dot_general(left_side, right_side, (((0,), (0,)), ((), ())), preferre...  30.1 us
    unnamed x160, local copies, waits for them, and re-layouts  16.6 us
  transfers between devices with their start and end apart: 8, of which 4 were waited for; matrix products, arithmetic and copies ran while one was open for 7% of the time, Pallas kernels for 17%

profile of v9, /device:TPU:0, one launch (start us, length us, event | category | flops | bytes accessed | tf_op | source)
XLA Modules:
  0.0 809.8 jit_solution(12166533579781036598)
XLA Ops:
  3.9 3.0 collective-permute-start.1
  10.2 8.2 %collective-permute-done.1 = bf16[72,3200]{1,0:T(8,128)(2,1)S(1)} collective-permute-done((bf16[72,3200]{1,0:T(8,128)(2,1)S(1)}, bf16[72,3200]{1,0:T(8,128)(2,1)S(1)}, u32[]{:S(2)}, u32[]{:S(2)}) %collective-permute-start.1) | collective-permute-done | bytes 460832 | tf_op jit(solution)/shard_map/ppermute | solution.py:100
  19.5 79.6 %shard_map.101 = bf16[16,144,3200]{2,1,0:T(8,128)(2,1)} custom-call(bf16[144,3200]{1,0:T(8,128)(2,1)} %pad_maximum_fusion.7.x_ref), custom_call_target="tpu_custom_call" | custom-call | bytes 150000000 | tf_op jit(solution)/shard_map/pallas_call | solution.py:243
  103.7 6.3 fusion.3
  116.6 4.0 fusion.13
  127.6 74.3 %collective-permute-done.2 = bf16[128,2304]{1,0:T(8,128)(2,1)S(1)} collective-permute-done((bf16[128,2304]{1,0:T(8,128)(2,1)}, bf16[128,2304]{1,0:T(8,128)(2,1)S(1)}, u32[]{:S(2)}, u32[]{:S(2)}) %collective-permute-start.2) | collective-permute-done | bytes 589856 | tf_op jit(solution)/shard_map/ppermute | solution.py:100
  205.3 55.1 %shard_map.102 = bf16[16,128,2304]{2,1,0:T(8,128)(2,1)} custom-call(bf16[128,2304]{1,0:T(8,128)(2,1)} %multiply_convert_fusion.2.x_ref), custom_call_target="tpu_custom_call" | custom-call | bytes 150000000 | tf_op jit(solution)/shard_map/pallas_call | solution.py:243
  263.1 12.4 %fusion.102 = f32[2048,576]{1,0:T(8,128)} fusion(bf16[2048,2304]{1,0:T(8,128)(2,1)} %bitcast.115, bf16[288,2304]{1,0:T(8,128)(2,1)S(1)} %get-tuple-element.53, bf16[288,2304]{1,0:T(8,128)(2,1)S(1)} %copy-done.13), kind=kOutput, calls=%fused_computation.202 | convolution fusion | flops 5441126400 | bytes 16809984 | tf_op jit(solution)/shard_map/dot_general | solution.py:79
  278.2 11.9 %multiply_convert_fusion.1 = (bf16[2048,576]{1,0:T(8,128)(2,1)}, f32[2048,576]{1,0:T(8,128)}) fusion(f32[2048,576]{1,0:T(8,128)} %fusion.102, bf16[2048,2304]{1,0:T(8,128)(2,1)S(1)} %bitcast.119, bf16[288,2304]{1,0:T(8,128)(2,1)S(1)} %get-tuple-element.52, bf16[288,2304]{1,0:T(8,128)(2,1)S(1)} %copy-done.12), kind=kOutput, calls=%fused_computation.17 | convolution fusion | flops 5452922880 | bytes 23887872 | tf_op jit(solution)/shard_map/dot_general | solution.py:79
  291.8 69.1 %shard_map.103 = f32[128,2304]{1,0:T(8,128)} custom-call(bf16[16,128,576]{2,1,0:T(8,128)(2,1)} %bitcast.129, bf16[576,2304]{1,0:T(8,128)(2,1)} %pad_maximum_fusion.3.refs_1_), custom_call_target="tpu_custom_call" | custom-call | bytes 150000000 | tf_op jit(solution)/shard_map/pallas_call | solution.py:536
  366.0 52.7 %shard_map.104 = bf16[16,128,2304]{2,1,0:T(8,128)(2,1)} custom-call(bf16[128,2304]{1,0:T(8,128)(2,1)} %get-tuple-element.58.x_ref), custom_call_target="tpu_custom_call" | custom-call | bytes 150000000 | tf_op jit(solution)/shard_map/pallas_call | solution.py:243
  418.7 11.4 %fusion.111 = f32[576,2304]{1,0:T(8,128)} fusion(bf16[2048,576]{1,0:T(8,128)(2,1)} %get-tuple-element.94, bf16[2048,2304]{1,0:T(8,128)(2,1)} %bitcast.123), kind=kOutput, calls=%fused_computation.211 | convolution fusion | flops 5435817984 | bytes 17104896 | tf_op jit(solution)/shard_map/dot_general | solution.py:73
  430.1 17.1 %multiply_convert_fusion = (bf16[2048,576]{1,0:T(8,128)(2,1)}, bf16[2048,576]{1,0:T(8,128)(2,1)}) fusion(f32[2048,576]{1,0:T(8,128)} %fusion.102, f32[2048,576]{1,0:T(8,128)} %get-tuple-element.95, bf16[2048,2304]{1,0:T(8,128)(2,1)} %bitcast.124, bf16[288,2304]{1,0:T(8,128)(2,1)S(1)} %copy-done.11, bf16[288,2304]{1,0:T(8,128)(2,1)S(1)} %copy-done.9), kind=kOutput, calls=%fused_computation.16 | convolution fusion | flops 5474156544 | bytes 26247168 | tf_op jit(solution)/shard_map/dot_general | solution.py:79
  447.2 10.1 %fusion.110 = f32[576,2304]{1,0:T(8,128)} fusion(bf16[2048,576]{1,0:T(8,128)(2,1)} %get-tuple-element.46, bf16[2048,2304]{1,0:T(8,128)(2,1)S(1)} %bitcast.122), kind=kOutput, calls=%fused_computation.210 | convolution fusion | flops 5435817984 | bytes 17104896 | tf_op jit(solution)/shard_map/dot_general | solution.py:73
  457.3 72.9 %shard_map.105 = f32[128,2304]{1,0:T(8,128)} custom-call(bf16[16,128,576]{2,1,0:T(8,128)(2,1)} %bitcast.130, bf16[16,128,576]{2,1,0:T(8,128)(2,1)} %bitcast.131, bf16[576,2304]{1,0:T(8,128)(2,1)} %get-tuple-element.98.refs_2_, bf16[576,2304]{1,0:T(8,128)(2,1)} %get-tuple-element.99.refs_3_), custom_call_target="tpu_custom_call" | custom-call | bytes 150000000 | tf_op jit(solution)/shard_map/pallas_call | solution.py:536
  536.9 8.6 %fusion.109 = f32[576,2304]{1,0:T(8,128)S(1)} fusion(bf16[2048,576]{1,0:T(8,128)(2,1)S(1)} %copy-done.20, bf16[2048,2304]{1,0:T(8,128)(2,1)} %bitcast.116), kind=kOutput, calls=%fused_computation.209 | convolution fusion | flops 5435817984 | bytes 17104896 | tf_op jit(solution)/shard_map/dot_general | solution.py:73
  555.2 3.7 fusion.26
  563.2 3.5 convolution_multiply_fusion
  570.2 5.5 fusion.1
  588.8 103.7 %shard_map.106 = f32[144,3200]{1,0:T(8,128)} custom-call(bf16[16,144,256]{2,1,0:T(8,128)(2,1)} %bitcast.127, bf16[256,2048]{1,0:T(8,128)(2,1)} %pad_maximum_fusion.6.right_a, bf16[16,144,256]{2,1,0:T(8,128)(2,1)} %bitcast.128, bf16[256,1024]{1,0:T(8,128)(2,1)} %copy.179.right_b, bf16[16,144,128]{2,1,0:T(8,128)(2,1)} %bitcast.132), custom_call_target="tpu_custom_call" | custom-call | bytes 200000000 | tf_op jit(solution)/shard_map/pallas_call | solution.py:498
  695.7 3.7 pad_maximum_fusion
  702.2 5.3 collective-permute-done.6
  715.8 85.1 %collective-permute-done.5 = bf16[128,2304]{1,0:T(8,128)(2,1)S(1)} collective-permute-done((bf16[128,2304]{1,0:T(8,128)(2,1)}, bf16[128,2304]{1,0:T(8,128)(2,1)S(1)}, u32[]{:S(2)}, u32[]{:S(2)}) %collective-permute-start.5) | collective-permute-done | bytes 589856 | tf_op jit(solution)/shard_map/ppermute | solution.py:100
  803.9 5.6 maximum_add_fusion
  (276 shorter events, 95.1 us)
Async XLA Ops:
  3.9 14.4 %collective-permute-start.1 = (bf16[72,3200]{1,0:T(8,128)(2,1)S(1)}, bf16[72,3200]{1,0:T(8,128)(2,1)S(1)}, u32[]{:S(2)}, u32[]{:S(2)}) collective-permute-start(bf16[72,3200]{1,0:T(8,128)(2,1)S(1)} %fusion.68), channel_id=1, source_target_pairs={{0,1},{1,0},{2,3},{3,2},{4,5},{5,4},{6,7},{7,6},{8,9},{9,8},{10,11... | collective-permute-start | bytes 1382408 | tf_op jit(solution)/shard_map/ppermute | solution.py:100
  6.9 95.9 %collective-permute-start = (bf16[128,2304]{1,0:T(8,128)(2,1)S(1)}, bf16[128,2304]{1,0:T(8,128)(2,1)S(1)}, u32[]{:S(2)}, u32[]{:S(2)}) collective-permute-start(bf16[128,2304]{1,0:T(8,128)(2,1)S(1)} %copy-done.1), channel_id=1, source_target_pairs={{0,1},{1,0},{2,3},{3,2},{4,5},{5,4},{6,7},{7,6},{8,9},{9,8},{10,11... | collective-permute-start | bytes 1769480 | tf_op jit(solution)/shard_map/ppermute | solution.py:100
  8.4 90.7 %copy-start.30 = (f32[256,128]{1,0:T(8,128)}, f32[256,128]{1,0:T(8,128)S(1)}, u32[]{:S(2)}) copy-start(f32[256,128]{1,0:T(8,128)S(1)} %get-tuple-element.84) | copy-start | bytes 393220
  8.4 90.7 %copy-start.32 = (f32[256,128]{1,0:T(8,128)}, f32[256,128]{1,0:T(8,128)S(1)}, u32[]{:S(2)}) copy-start(f32[256,128]{1,0:T(8,128)S(1)} %get-tuple-element.85) | copy-start | bytes 393220
  10.1 105.3 %copy-start.37 = (pred[256,256]{0,1:T(8,128)(4,1)}, pred[256,256]{0,1:T(8,128)(4,1)S(1)}, u32[]{:S(2)}) copy-start(pred[256,256]{0,1:T(8,128)(4,1)S(1)} %fusion.69) | copy-start | bytes 196612
  100.6 159.9 %collective-permute-start.3 = (bf16[288,6912]{1,0:T(8,128)(2,1)}, bf16[288,6912]{1,0:T(8,128)(2,1)}, u32[]{:S(2)}, u32[]{:S(2)}) collective-permute-start(bf16[288,6912]{1,0:T(8,128)(2,1)} %param.9), channel_id=1, source_target_pairs={{0,1},{1,0},{2,3},{3,2},{4,5},{5,4},{6,7},{7,6},{8,9},{9,8},{10,11... | collective-permute-start | bytes 11943944 | tf_op jit(solution)/shard_map/ppermute | solution.py:100
  120.6 81.5 %copy-start.2 = (f32[256,2304]{1,0:T(8,128)}, f32[256,2304]{1,0:T(8,128)S(1)}, u32[]{:S(2)}) copy-start(f32[256,2304]{1,0:T(8,128)S(1)} %fusion.13) | copy-start | bytes 7077892
  121.6 80.3 %collective-permute-start.2 = (bf16[128,2304]{1,0:T(8,128)(2,1)}, bf16[128,2304]{1,0:T(8,128)(2,1)S(1)}, u32[]{:S(2)}, u32[]{:S(2)}) collective-permute-start(bf16[128,2304]{1,0:T(8,128)(2,1)} %slice.331), channel_id=1, source_target_pairs={{0,1},{1,0},{2,3},{3,2},{4,5},{5,4},{6,7},{7,6},{8,9},{9,8},{10,11... | collective-permute-start | bytes 1769480 | tf_op jit(solution)/shard_map/ppermute | solution.py:100
  127.5 76.7 %copy-start.44 = (f32[2304]{0:T(1024)S(1)}, f32[2304]{0:T(1024)}, u32[]{:S(2)}) copy-start(f32[2304]{0:T(1024)} %get-tuple-element.38) | copy-start | bytes 27652
  260.5 17.7 %slice-start.6 = ((s8[9437184]{0:T(1024)(128)(4,1)}), s8[4194304]{0:T(1024)(128)(4,1)S(1)}, s32[]{:S(2)}) async-start(s8[9437184]{0:T(1024)(128)(4,1)} %bitcast.117), calls=%async_computation.6 | async-start | bytes 8388608
  263.0 27.1 %copy-start.10 = (bf16[288,2304]{1,0:T(8,128)(2,1)}, bf16[288,2304]{1,0:T(8,128)(2,1)S(1)}, u32[]{:S(2)}) copy-start(bf16[288,2304]{1,0:T(8,128)(2,1)S(1)} %get-tuple-element.51) | copy-start | bytes 3981316
  263.0 15.1 %slice-start.7 = ((s8[9437184]{0:T(1024)(128)(4,1)}), s8[4194304]{0:T(1024)(128)(4,1)S(1)}, s32[]{:S(2)}) async-start(s8[9437184]{0:T(1024)(128)(4,1)} %bitcast.117), calls=%async_computation.7 | async-start | bytes 8388608
  291.8 70.6 %copy-start.7 = (bf16[128,2304]{1,0:T(8,128)(2,1)S(1)}, bf16[128,2304]{1,0:T(8,128)(2,1)}, u32[]{:S(2)}) copy-start(bf16[128,2304]{1,0:T(8,128)(2,1)} %param.11) | copy-start | bytes 1769476
  291.8 70.6 %copy-start.50 = (f32[2304]{0:T(1024)S(1)}, f32[2304]{0:T(1024)}, u32[]{:S(2)}) copy-start(f32[2304]{0:T(1024)} %get-tuple-element.37) | copy-start | bytes 27652
  418.7 28.5 %slice-start.9 = ((s8[9437184]{0:T(1024)(128)(4,1)}), s8[4194304]{0:T(1024)(128)(4,1)S(1)}, s32[]{:S(2)}) async-start(s8[9437184]{0:T(1024)(128)(4,1)} %bitcast.120), calls=%async_computation.9 | async-start | bytes 8388608
  430.1 17.1 %slice-start.10 = ((s8[9437184]{0:T(1024)(128)(4,1)}), s8[4194304]{0:T(1024)(128)(4,1)S(1)}, s32[]{:S(2)}) async-start(s8[9437184]{0:T(1024)(128)(4,1)} %bitcast.120), calls=%async_computation.10 | async-start | bytes 8388608
  430.1 17.1 %slice-start.11 = ((s8[9437184]{0:T(1024)(128)(4,1)}), s8[1048576]{0:T(1024)(128)(4,1)S(1)}, s32[]{:S(2)}) async-start(s8[9437184]{0:T(1024)(128)(4,1)} %bitcast.120), calls=%async_computation.11 | async-start | bytes 2097152
  457.3 72.9 %copy-start.45 = (f32[2304]{0:T(1024)S(1)}, f32[2304]{0:T(1024)}, u32[]{:S(2)}) copy-start(f32[2304]{0:T(1024)} %get-tuple-element.38) | copy-start | bytes 27652
  535.3 19.0 %copy-start.25 = (bf16[128,2304]{1,0:T(8,128)(2,1)}, bf16[128,2304]{1,0:T(8,128)(2,1)S(1)}, u32[]{:S(2)}) copy-start(bf16[128,2304]{1,0:T(8,128)(2,1)S(1)} %fusion.34) | copy-start | bytes 1769476
  535.3 19.0 %collective-permute-start.4 = (bf16[128,2304]{1,0:T(8,128)(2,1)S(1)}, bf16[128,2304]{1,0:T(8,128)(2,1)S(1)}, u32[]{:S(2)}, u32[]{:S(2)}) collective-permute-start(bf16[128,2304]{1,0:T(8,128)(2,1)S(1)} %fusion.34), channel_id=1, source_target_pairs={{0,1},{1,0},{2,3},{3,2},{4,5},{5,4},{6,7},{7,6},{8,9},{9,8},{10,11... | collective-permute-start | bytes 1769480 | tf_op jit(solution)/shard_map/ppermute | solution.py:100
  694.0 13.5 %collective-permute-start.6 = (bf16[72,3200]{1,0:T(8,128)(2,1)S(1)}, bf16[72,3200]{1,0:T(8,128)(2,1)S(1)}, u32[]{:S(2)}, u32[]{:S(2)}) collective-permute-start(bf16[72,3200]{1,0:T(8,128)(2,1)S(1)} %select_convert_fusion), channel_id=1, source_target_pairs={{0,1},{1,0},{2,3},{3,2},{4,5},{5,4},{6,7},{7,6},{8,9},{9,8},{10,11... | collective-permute-start | bytes 1382408 | tf_op jit(solution)/shard_map/ppermute | solution.py:100
  699.3 103.4 %collective-permute-start.7 = (bf16[288,6912]{1,0:T(8,128)(2,1)}, bf16[288,6912]{1,0:T(8,128)(2,1)}, u32[]{:S(2)}, u32[]{:S(2)}) collective-permute-start(bf16[288,6912]{1,0:T(8,128)(2,1)} %pad_maximum_fusion), channel_id=1, source_target_pairs={{0,1},{1,0},{2,3},{3,2},{4,5},{5,4},{6,7},{7,6},{8,9},{9,8},{10,11... | collective-permute-start | bytes 11943944 | tf_op jit(solution)/shard_map/ppermute | solution.py:100
  700.7 100.2 %collective-permute-start.5 = (bf16[128,2304]{1,0:T(8,128)(2,1)}, bf16[128,2304]{1,0:T(8,128)(2,1)S(1)}, u32[]{:S(2)}, u32[]{:S(2)}) collective-permute-start(bf16[128,2304]{1,0:T(8,128)(2,1)} %slice.330), channel_id=1, source_target_pairs={{0,1},{1,0},{2,3},{3,2},{4,5},{5,4},{6,7},{7,6},{8,9},{9,8},{10,11... | collective-permute-start | bytes 1769480 | tf_op jit(solution)/shard_map/ppermute | solution.py:100
  712.3 89.0 %copy-start.6 = (f32[128,2304]{1,0:T(8,128)S(1)}, f32[128,2304]{1,0:T(8,128)}, u32[]{:S(2)}) copy-start(f32[128,2304]{1,0:T(8,128)} %copy-done.5) | copy-start | bytes 3538948
  (60 other events, 214.7 us)
